TPU v7x, 32 devices: a whole 2x2x4 slice. The times are simulated.
32 devices in a mesh: dp: 2 (over x), section: 4 (over z), tensor: 4 (over y, core).
Axes of the slice: x: 2, y: 2, z: 4, core: 2. Of those that a mesh axis runs over, the one named last changes fastest.
Arguments:
- cotangent: bfloat16 [2, 64, 6144], P(None, 'tensor', 'dp'), may hold values from -6 to 6
- inputs: bfloat16 [4, 2, 64, 6144], P('section', None, 'tensor', 'dp'), may hold values from -6 to 6
- queries: bfloat16 [4, 2, 64, 6144], P('section', None, None, 'tensor'), may hold values from -256 to 256
- keys: bfloat16 [4, 2, 64, 6144], P('section', None, None, 'tensor'), may hold values from -8 to 8
- context: bfloat16 [4, 2, 64, 6144], P('section', None, None, 'tensor'), may hold values from -6 to 6
- value_weight: bfloat16 [4, 6144, 6144], P('section', 'dp', 'tensor'), may hold values from -0.078125 to 0.078125
- out_weight: bfloat16 [4, 6144, 6144], P('section', 'tensor', 'dp'), may hold values from -0.078125 to 0.078125
Outputs:
- section_grads: bfloat16 [4, 2, 64, 6144], P('section', None, 'tensor', 'dp')
- value_weight_grad: bfloat16 [4, 6144, 6144], P('section', 'dp', 'tensor')
- out_weight_grad: bfloat16 [4, 6144, 6144], P('section', 'tensor', 'dp')
All inputs are finite; a program needn't handle non-finite values.
Results may differ from a plain program's by a relative error of at most 0.018.
Values may be sent and summed in bfloat16 or wider, within the bound.
No kernel may reach another device: no remote copies, remote signals or barrier semaphores. Data moves between devices by JAX's collectives and lax.ppermute only.
A program may use at most 128 MiB of HBM per device.

v0:
```python
import jax
import jax.numpy as jnp
from jax import lax
from jax.sharding import PartitionSpec as P

HEAD_DIM = 128


def shifted(array, axis, by):
    peers = lax.axis_size(axis)
    pairs = [(i, i + by) for i in range(peers) if 0 <= i + by < peers]
    return lax.ppermute(array, axis, pairs)


def attention_probs(query_layer, key_layer):
    micro_count, seq_len, width = query_layer.shape
    head_count = width // HEAD_DIM
    query_heads = query_layer.reshape(micro_count, seq_len, head_count, HEAD_DIM)
    key_heads = key_layer.reshape(micro_count, seq_len, head_count, HEAD_DIM)
    scores = jnp.einsum(
        "mihd,mjhd->mhij", query_heads, key_heads, preferred_element_type=jnp.float32
    )
    scores = scores / jnp.sqrt(jnp.float32(HEAD_DIM))
    rows = jnp.arange(seq_len)
    causal = rows[:, None] >= rows[None, :]
    scores = jnp.where(causal[None, None], scores, jnp.float32(-1e30))
    highest = jnp.max(scores, axis=-1, keepdims=True)
    expo = jnp.exp(scores - highest)
    return (expo / jnp.sum(expo, axis=-1, keepdims=True)).astype(jnp.bfloat16)


def per_device(cotangent, inputs, queries, keys, context, value_weight, out_weight):
    section_count = lax.axis_size("section")
    section_place = lax.axis_index("section")
    micro_count = cotangent.shape[0]
    part_rows = cotangent.shape[1]
    width_cols = cotangent.shape[2]
    seq_len = queries.shape[2]
    head_cols = queries.shape[3]
    heads_here = head_cols // HEAD_DIM
    value_proj = value_weight[0]
    out_proj = out_weight[0]
    saved_context = context[0]
    whole_inputs = lax.all_gather(inputs[0], "tensor", axis=1, tiled=True)
    attention = attention_probs(queries[0], keys[0])

    def tick(tick_number, carry):
        received, acc_out, acc_value, grads = carry
        raw_index = tick_number - (section_count - 1 - section_place)
        valid = (raw_index >= 0) & (raw_index < micro_count)
        micro_index = jnp.clip(raw_index, 0, micro_count - 1)
        cot_here = lax.dynamic_index_in_dim(cotangent, micro_index, 0, keepdims=False)
        incoming = jnp.where(section_place == section_count - 1, cot_here, received)
        grad_cols = lax.all_gather(incoming, "tensor", axis=0, tiled=True)
        ctx_part = lax.dot_general(
            grad_cols, out_proj, (((1,), (1,)), ((), ())), preferred_element_type=jnp.float32
        )
        attn_here = lax.dynamic_index_in_dim(attention, micro_index, 0, keepdims=False)
        ctx_grad = lax.psum(ctx_part, "dp").astype(jnp.bfloat16)
        ctx_heads = ctx_grad.reshape(seq_len, heads_here, HEAD_DIM)
        value_heads = jnp.einsum(
            "hij,ihd->jhd", attn_here, ctx_heads, preferred_element_type=jnp.float32
        )
        value_grad = value_heads.reshape(seq_len, head_cols).astype(jnp.bfloat16)
        input_here = lax.dynamic_index_in_dim(whole_inputs, micro_index, 0, keepdims=False)
        context_here = lax.dynamic_index_in_dim(saved_context, micro_index, 0, keepdims=False)
        value_term = lax.dot_general(
            input_here, value_grad, (((0,), (0,)), ((), ())), preferred_element_type=jnp.float32
        )
        out_term = lax.dot_general(
            context_here, grad_cols, (((0,), (0,)), ((), ())), preferred_element_type=jnp.float32
        )
        acc_value = acc_value + jnp.where(valid, value_term, jnp.float32(0.0))
        acc_out = acc_out + jnp.where(valid, out_term, jnp.float32(0.0))
        branch = lax.dot_general(
            value_grad, value_proj, (((1,), (1,)), ((), ())), preferred_element_type=jnp.float32
        )
        summed = lax.psum_scatter(branch, "tensor", scatter_dimension=0, tiled=True)
        fresh = (summed + incoming.astype(jnp.float32)).astype(jnp.bfloat16)
        passed = shifted(fresh, "section", -1)
        current = lax.dynamic_index_in_dim(grads, micro_index, 0, keepdims=False)
        grads = lax.dynamic_update_index_in_dim(
            grads, jnp.where(valid, fresh, current), micro_index, 0
        )
        return (passed, acc_out, acc_value, grads)

    start_recv = jnp.zeros((part_rows, width_cols), jnp.bfloat16)
    start_out = jnp.zeros((head_cols, width_cols), jnp.float32)
    start_value = jnp.zeros((width_cols, head_cols), jnp.float32)
    start_grads = jnp.zeros((micro_count, part_rows, width_cols), jnp.bfloat16)
    final = lax.fori_loop(
        0, micro_count + section_count - 1, tick, (start_recv, start_out, start_value, start_grads)
    )
    acc_out = final[1]
    acc_value = final[2]
    grads = final[3]
    return (grads[None], acc_value.astype(jnp.bfloat16)[None], acc_out.astype(jnp.bfloat16)[None])


def solution(mesh):
    placed = (
        P(None, "tensor", "dp"),
        P("section", None, "tensor", "dp"),
        P("section", None, None, "tensor"),
        P("section", None, None, "tensor"),
        P("section", None, None, "tensor"),
        P("section", "dp", "tensor"),
        P("section", "tensor", "dp"),
    )
    return jax.shard_map(
        per_device,
        mesh=mesh,
        in_specs=placed,
        out_specs=(
            P("section", None, "tensor", "dp"),
            P("section", "dp", "tensor"),
            P("section", "tensor", "dp"),
        ),
        check_vma=False,
    )
```

profile of v0, /device:TPU:0, one launch (start us, length us, event | category | flops | bytes accessed | tf_op | source)
XLA Modules:
  0.0 416.7 jit_solution(681128822975914403)
XLA Ops:
  10.2 10.3 %all-gather = bf16[1,2,64,3072]{3,2,1,0:T(8,128)(2,1)S(1)} all-gather(bf16[1,2,16,3072]{3,2,1,0:T(8,128)(2,1)} %param.10), channel_id=2, replica_groups=mesh['dp'=2,'section'=4,'tensor'=4] {'tensor'}, dimensions={2}, use_global_device_ids=true | all-gather | bytes 983040 | tf_op jit(solution)/shard_map/all_gather | solution.py:44
  20.6 369.8 %while.22 = (s32[]{:T(128)}, bf16[16,3072]{1,0:T(8,128)(2,1)S(1)}, f32[1536,3072]{1,0:T(8,128)}, f32[3072,1536]{1,0:T(8,128)}, bf16[2,16,3072]{2,1,0:T(8,128)(2,...) while((s32[]{:T(128)}, bf16[16,3072]{1,0:T(8,128)(2,1)S(1)}, ...), condition=%wide.region_5.6_spmd.clone, body=%wide.region_2.5_spmd.clone.sunk | while | flops 2457255936 | bytes 104989032 | solution.py:91
  34.8 15.2 %all-reduce.1 = bf16[64,1536]{1,0:T(8,128)(2,1)S(1)} all-reduce(f32[64,1536]{1,0:T(8,128)S(1)} %fusion.66), channel_id=1, replica_groups=mesh['dp'=2,'section'=4,'tensor'=4] {'dp'}, use_global_device_ids=true, to_apply=%region_3.3 | all-reduce | flops 98304 | bytes 589824 | tf_op jit(solution)/shard_map/while/body/eval_jaxpr/psum | solution.py:59
  50.2 7.5 %fusion.68 = f32[64,3072]{1,0:T(8,128)} fusion(bf16[3072,1536]{1,0:T(8,128)(2,1)} %get-tuple-element.483, bf16[12,8,8,128]{3,2,1,0:T(8,128)(2,1)S(1)} %fusion.67), kind=kOutput, calls=%fused_computation.7.clone.1 | convolution fusion | flops 603979776 | bytes 10420224 | tf_op jit(solution)/shard_map/while/body/eval_jaxpr/dot_general | solution.py:75
  57.8 8.2 %select_add_fusion.4 = f32[1536,3072]{1,0:T(8,128)} fusion(f32[1536,3072]{1,0:T(8,128)} %get-tuple-element.459, bf16[64,3072]{1,0:T(8,128)(2,1)S(1)} %all_gather.15, pred[]{:T(512)S(6)} %compare.3, pred[]{:T(512)S(6)} %and.12, bf16[2,64,1536]{2,1,0:T(8,128)(2,1)S(1)} %copy-done.1, s32[]{:T(128)S(6)} %min.12), kind=kOutput, calls=%fused_computation.1.clone.1 | convolution fusion | flops 618135552 | bytes 38338568 | tf_op jit(solution)/shard_map/while/body/eval_jaxpr/dot_general | solution.py:70
  66.0 15.0 %reduce-scatter.2.cloned.1.call-done = f32[16,3072]{1,0:T(8,128)} async-done(((f32[64,3072]{1,0:T(8,128)}), f32[16,3072]{1,0:T(8,128)}) %reduce-scatter.2.cloned.1.call-update) | async-done | bytes 196624 | tf_op jit(solution)/shard_map/while/body/eval_jaxpr/reduce_scatter | solution.py:78
  83.3 7.9 %select_add_fusion.5 = f32[3072,1536]{1,0:T(8,128)} fusion(f32[3072,1536]{1,0:T(8,128)} %get-tuple-element.460, pred[]{:T(512)S(6)} %compare.3, pred[]{:T(512)S(6)} %and.12, bf16[2,64,3072]{2,1,0:T(8,128)(2,1)S(1)} %get-tuple-element.485, s32[]{:T(128)S(6)} %min.12, bf16[12,8,8,128]{3,2,1,0:T(8,128)(2,1)S(1)} %fusion.67), kind=kOutput, calls=%fused_computation.clone.1 | convolution fusion | flops 618135552 | bytes 38338568 | tf_op jit(solution)/shard_map/while/body/eval_jaxpr/dot_general | solution.py:67
  105.0 15.2 %all-reduce.1 = bf16[64,1536]{1,0:T(8,128)(2,1)S(1)} all-reduce(f32[64,1536]{1,0:T(8,128)S(1)} %fusion.66), channel_id=1, replica_groups=mesh['dp'=2,'section'=4,'tensor'=4] {'dp'}, use_global_device_ids=true, to_apply=%region_3.3 | all-reduce | flops 98304 | bytes 589824 | tf_op jit(solution)/shard_map/while/body/eval_jaxpr/psum | solution.py:59
  127.9 12.2 %select_add_fusion.4 = f32[1536,3072]{1,0:T(8,128)} fusion(f32[1536,3072]{1,0:T(8,128)} %get-tuple-element.459, bf16[64,3072]{1,0:T(8,128)(2,1)S(1)} %all_gather.15, pred[]{:T(512)S(6)} %compare.3, pred[]{:T(512)S(6)} %and.12, bf16[2,64,1536]{2,1,0:T(8,128)(2,1)S(1)} %copy-done.1, s32[]{:T(128)S(6)} %min.12), kind=kOutput, calls=%fused_computation.1.clone.1 | convolution fusion | flops 618135552 | bytes 38338568 | tf_op jit(solution)/shard_map/while/body/eval_jaxpr/dot_general | solution.py:70
  140.1 11.6 %reduce-scatter.2.cloned.1.call-done = f32[16,3072]{1,0:T(8,128)} async-done(((f32[64,3072]{1,0:T(8,128)}), f32[16,3072]{1,0:T(8,128)}) %reduce-scatter.2.cloned.1.call-update) | async-done | bytes 196624 | tf_op jit(solution)/shard_map/while/body/eval_jaxpr/reduce_scatter | solution.py:78
  154.1 11.9 %select_add_fusion.5 = f32[3072,1536]{1,0:T(8,128)} fusion(f32[3072,1536]{1,0:T(8,128)} %get-tuple-element.460, pred[]{:T(512)S(6)} %compare.3, pred[]{:T(512)S(6)} %and.12, bf16[2,64,3072]{2,1,0:T(8,128)(2,1)S(1)} %get-tuple-element.485, s32[]{:T(128)S(6)} %min.12, bf16[12,8,8,128]{3,2,1,0:T(8,128)(2,1)S(1)} %fusion.67), kind=kOutput, calls=%fused_computation.clone.1 | convolution fusion | flops 618135552 | bytes 38338568 | tf_op jit(solution)/shard_map/while/body/eval_jaxpr/dot_general | solution.py:67
  179.8 15.2 %all-reduce.1 = bf16[64,1536]{1,0:T(8,128)(2,1)S(1)} all-reduce(f32[64,1536]{1,0:T(8,128)S(1)} %fusion.66), channel_id=1, replica_groups=mesh['dp'=2,'section'=4,'tensor'=4] {'dp'}, use_global_device_ids=true, to_apply=%region_3.3 | all-reduce | flops 98304 | bytes 589824 | tf_op jit(solution)/shard_map/while/body/eval_jaxpr/psum | solution.py:59
  202.7 12.2 %select_add_fusion.4 = f32[1536,3072]{1,0:T(8,128)} fusion(f32[1536,3072]{1,0:T(8,128)} %get-tuple-element.459, bf16[64,3072]{1,0:T(8,128)(2,1)S(1)} %all_gather.15, pred[]{:T(512)S(6)} %compare.3, pred[]{:T(512)S(6)} %and.12, bf16[2,64,1536]{2,1,0:T(8,128)(2,1)S(1)} %copy-done.1, s32[]{:T(128)S(6)} %min.12), kind=kOutput, calls=%fused_computation.1.clone.1 | convolution fusion | flops 618135552 | bytes 38338568 | tf_op jit(solution)/shard_map/while/body/eval_jaxpr/dot_general | solution.py:70
  214.9 11.7 %reduce-scatter.2.cloned.1.call-done = f32[16,3072]{1,0:T(8,128)} async-done(((f32[64,3072]{1,0:T(8,128)}), f32[16,3072]{1,0:T(8,128)}) %reduce-scatter.2.cloned.1.call-update) | async-done | bytes 196624 | tf_op jit(solution)/shard_map/while/body/eval_jaxpr/reduce_scatter | solution.py:78
  228.8 11.9 %select_add_fusion.5 = f32[3072,1536]{1,0:T(8,128)} fusion(f32[3072,1536]{1,0:T(8,128)} %get-tuple-element.460, pred[]{:T(512)S(6)} %compare.3, pred[]{:T(512)S(6)} %and.12, bf16[2,64,3072]{2,1,0:T(8,128)(2,1)S(1)} %get-tuple-element.485, s32[]{:T(128)S(6)} %min.12, bf16[12,8,8,128]{3,2,1,0:T(8,128)(2,1)S(1)} %fusion.67), kind=kOutput, calls=%fused_computation.clone.1 | convolution fusion | flops 618135552 | bytes 38338568 | tf_op jit(solution)/shard_map/while/body/eval_jaxpr/dot_general | solution.py:67
  254.6 15.1 %all-reduce.1 = bf16[64,1536]{1,0:T(8,128)(2,1)S(1)} all-reduce(f32[64,1536]{1,0:T(8,128)S(1)} %fusion.66), channel_id=1, replica_groups=mesh['dp'=2,'section'=4,'tensor'=4] {'dp'}, use_global_device_ids=true, to_apply=%region_3.3 | all-reduce | flops 98304 | bytes 589824 | tf_op jit(solution)/shard_map/while/body/eval_jaxpr/psum | solution.py:59
  277.5 12.2 %select_add_fusion.4 = f32[1536,3072]{1,0:T(8,128)} fusion(f32[1536,3072]{1,0:T(8,128)} %get-tuple-element.459, bf16[64,3072]{1,0:T(8,128)(2,1)S(1)} %all_gather.15, pred[]{:T(512)S(6)} %compare.3, pred[]{:T(512)S(6)} %and.12, bf16[2,64,1536]{2,1,0:T(8,128)(2,1)S(1)} %copy-done.1, s32[]{:T(128)S(6)} %min.12), kind=kOutput, calls=%fused_computation.1.clone.1 | convolution fusion | flops 618135552 | bytes 38338568 | tf_op jit(solution)/shard_map/while/body/eval_jaxpr/dot_general | solution.py:70
  289.6 11.7 %reduce-scatter.2.cloned.1.call-done = f32[16,3072]{1,0:T(8,128)} async-done(((f32[64,3072]{1,0:T(8,128)}), f32[16,3072]{1,0:T(8,128)}) %reduce-scatter.2.cloned.1.call-update) | async-done | bytes 196624 | tf_op jit(solution)/shard_map/while/body/eval_jaxpr/reduce_scatter | solution.py:78
  303.6 11.9 %select_add_fusion.5 = f32[3072,1536]{1,0:T(8,128)} fusion(f32[3072,1536]{1,0:T(8,128)} %get-tuple-element.460, pred[]{:T(512)S(6)} %compare.3, pred[]{:T(512)S(6)} %and.12, bf16[2,64,3072]{2,1,0:T(8,128)(2,1)S(1)} %get-tuple-element.485, s32[]{:T(128)S(6)} %min.12, bf16[12,8,8,128]{3,2,1,0:T(8,128)(2,1)S(1)} %fusion.67), kind=kOutput, calls=%fused_computation.clone.1 | convolution fusion | flops 618135552 | bytes 38338568 | tf_op jit(solution)/shard_map/while/body/eval_jaxpr/dot_general | solution.py:67
  329.4 15.1 %all-reduce.1 = bf16[64,1536]{1,0:T(8,128)(2,1)S(1)} all-reduce(f32[64,1536]{1,0:T(8,128)S(1)} %fusion.66), channel_id=1, replica_groups=mesh['dp'=2,'section'=4,'tensor'=4] {'dp'}, use_global_device_ids=true, to_apply=%region_3.3 | all-reduce | flops 98304 | bytes 589824 | tf_op jit(solution)/shard_map/while/body/eval_jaxpr/psum | solution.py:59
  352.3 12.2 %select_add_fusion.4 = f32[1536,3072]{1,0:T(8,128)} fusion(f32[1536,3072]{1,0:T(8,128)} %get-tuple-element.459, bf16[64,3072]{1,0:T(8,128)(2,1)S(1)} %all_gather.15, pred[]{:T(512)S(6)} %compare.3, pred[]{:T(512)S(6)} %and.12, bf16[2,64,1536]{2,1,0:T(8,128)(2,1)S(1)} %copy-done.1, s32[]{:T(128)S(6)} %min.12), kind=kOutput, calls=%fused_computation.1.clone.1 | convolution fusion | flops 618135552 | bytes 38338568 | tf_op jit(solution)/shard_map/while/body/eval_jaxpr/dot_general | solution.py:70
  364.5 11.7 %reduce-scatter.2.cloned.1.call-done = f32[16,3072]{1,0:T(8,128)} async-done(((f32[64,3072]{1,0:T(8,128)}), f32[16,3072]{1,0:T(8,128)}) %reduce-scatter.2.cloned.1.call-update) | async-done | bytes 196624 | tf_op jit(solution)/shard_map/while/body/eval_jaxpr/reduce_scatter | solution.py:78
  378.4 11.9 %select_add_fusion.5 = f32[3072,1536]{1,0:T(8,128)} fusion(f32[3072,1536]{1,0:T(8,128)} %get-tuple-element.460, pred[]{:T(512)S(6)} %compare.3, pred[]{:T(512)S(6)} %and.12, bf16[2,64,3072]{2,1,0:T(8,128)(2,1)S(1)} %get-tuple-element.485, s32[]{:T(128)S(6)} %min.12, bf16[12,8,8,128]{3,2,1,0:T(8,128)(2,1)S(1)} %fusion.67), kind=kOutput, calls=%fused_computation.clone.1 | convolution fusion | flops 618135552 | bytes 38338568 | tf_op jit(solution)/shard_map/while/body/eval_jaxpr/dot_general | solution.py:67
  390.3 11.5 %convert_bitcast_fusion.2 = bf16[1,3072,1536]{2,1,0:T(8,128)(2,1)} fusion(f32[3072,1536]{1,0:T(8,128)} %get-tuple-element.286), kind=kLoop, calls=%fused_computation.29 | loop fusion | flops 4718592 | bytes 28311552 | tf_op jit(solution)/shard_map/broadcast_in_dim | solution.py:97
  (77 shorter events, 123.0 us)
Async XLA Ops:
  20.6 37.2 %copy-start.1 = (bf16[2,64,1536]{2,1,0:T(8,128)(2,1)S(1)}, bf16[2,64,1536]{2,1,0:T(8,128)(2,1)}, u32[]{:S(2)}) copy-start(bf16[2,64,1536]{2,1,0:T(8,128)(2,1)} %get-tuple-element.484) | copy-start | bytes 1179652 | tf_op jit(solution)/shard_map/while
  20.6 60.4 %reduce-scatter.2.cloned.1.call-start = ((), (), s32[]{:S(2)}) async-start(), calls=%async_computation.1 | async-start | bytes 983040 | tf_op jit(solution)/shard_map/while/body/eval_jaxpr/reduce_scatter | solution.py:78
  82.0 9.2 %collective-permute-start = (bf16[16,3072]{1,0:T(8,128)(2,1)S(1)}, bf16[16,3072]{1,0:T(8,128)(2,1)S(1)}, u32[]{:S(2)}, u32[]{:S(2)}) collective-permute-start(bf16[16,3072]{1,0:T(8,128)(2,1)S(1)} %get-tuple-element.439), channel_id=1, source_target_pairs={{4,0},{8,4},{12,8},{5,1},{9,5},{13,9},{6,2},{10,6},{14,10},{7,3},{... | collective-permute-start | bytes 294920 | tf_op jit(solution)/shard_map/while/body/eval_jaxpr/ppermute | solution.py:12
  91.2 36.8 %copy-start.1 = (bf16[2,64,1536]{2,1,0:T(8,128)(2,1)S(1)}, bf16[2,64,1536]{2,1,0:T(8,128)(2,1)}, u32[]{:S(2)}) copy-start(bf16[2,64,1536]{2,1,0:T(8,128)(2,1)} %get-tuple-element.484) | copy-start | bytes 1179652 | tf_op jit(solution)/shard_map/while
  91.2 60.6 %reduce-scatter.2.cloned.1.call-start = ((), (), s32[]{:S(2)}) async-start(), calls=%async_computation.1 | async-start | bytes 983040 | tf_op jit(solution)/shard_map/while/body/eval_jaxpr/reduce_scatter | solution.py:78
  152.8 13.2 %collective-permute-start = (bf16[16,3072]{1,0:T(8,128)(2,1)S(1)}, bf16[16,3072]{1,0:T(8,128)(2,1)S(1)}, u32[]{:S(2)}, u32[]{:S(2)}) collective-permute-start(bf16[16,3072]{1,0:T(8,128)(2,1)S(1)} %get-tuple-element.439), channel_id=1, source_target_pairs={{4,0},{8,4},{12,8},{5,1},{9,5},{13,9},{6,2},{10,6},{14,10},{7,3},{... | collective-permute-start | bytes 294920 | tf_op jit(solution)/shard_map/while/body/eval_jaxpr/ppermute | solution.py:12
  166.0 36.7 %copy-start.1 = (bf16[2,64,1536]{2,1,0:T(8,128)(2,1)S(1)}, bf16[2,64,1536]{2,1,0:T(8,128)(2,1)}, u32[]{:S(2)}) copy-start(bf16[2,64,1536]{2,1,0:T(8,128)(2,1)} %get-tuple-element.484) | copy-start | bytes 1179652 | tf_op jit(solution)/shard_map/while
  166.0 60.6 %reduce-scatter.2.cloned.1.call-start = ((), (), s32[]{:S(2)}) async-start(), calls=%async_computation.1 | async-start | bytes 983040 | tf_op jit(solution)/shard_map/while/body/eval_jaxpr/reduce_scatter | solution.py:78
  227.5 13.2 %collective-permute-start = (bf16[16,3072]{1,0:T(8,128)(2,1)S(1)}, bf16[16,3072]{1,0:T(8,128)(2,1)S(1)}, u32[]{:S(2)}, u32[]{:S(2)}) collective-permute-start(bf16[16,3072]{1,0:T(8,128)(2,1)S(1)} %get-tuple-element.439), channel_id=1, source_target_pairs={{4,0},{8,4},{12,8},{5,1},{9,5},{13,9},{6,2},{10,6},{14,10},{7,3},{... | collective-permute-start | bytes 294920 | tf_op jit(solution)/shard_map/while/body/eval_jaxpr/ppermute | solution.py:12
  240.8 36.7 %copy-start.1 = (bf16[2,64,1536]{2,1,0:T(8,128)(2,1)S(1)}, bf16[2,64,1536]{2,1,0:T(8,128)(2,1)}, u32[]{:S(2)}) copy-start(bf16[2,64,1536]{2,1,0:T(8,128)(2,1)} %get-tuple-element.484) | copy-start | bytes 1179652 | tf_op jit(solution)/shard_map/while
  240.8 60.6 %reduce-scatter.2.cloned.1.call-start = ((), (), s32[]{:S(2)}) async-start(), calls=%async_computation.1 | async-start | bytes 983040 | tf_op jit(solution)/shard_map/while/body/eval_jaxpr/reduce_scatter | solution.py:78
  302.3 13.2 %collective-permute-start = (bf16[16,3072]{1,0:T(8,128)(2,1)S(1)}, bf16[16,3072]{1,0:T(8,128)(2,1)S(1)}, u32[]{:S(2)}, u32[]{:S(2)}) collective-permute-start(bf16[16,3072]{1,0:T(8,128)(2,1)S(1)} %get-tuple-element.439), channel_id=1, source_target_pairs={{4,0},{8,4},{12,8},{5,1},{9,5},{13,9},{6,2},{10,6},{14,10},{7,3},{... | collective-permute-start | bytes 294920 | tf_op jit(solution)/shard_map/while/body/eval_jaxpr/ppermute | solution.py:12
  315.6 36.7 %copy-start.1 = (bf16[2,64,1536]{2,1,0:T(8,128)(2,1)S(1)}, bf16[2,64,1536]{2,1,0:T(8,128)(2,1)}, u32[]{:S(2)}) copy-start(bf16[2,64,1536]{2,1,0:T(8,128)(2,1)} %get-tuple-element.484) | copy-start | bytes 1179652 | tf_op jit(solution)/shard_map/while
  315.6 60.6 %reduce-scatter.2.cloned.1.call-start = ((), (), s32[]{:S(2)}) async-start(), calls=%async_computation.1 | async-start | bytes 983040 | tf_op jit(solution)/shard_map/while/body/eval_jaxpr/reduce_scatter | solution.py:78
  377.1 13.2 %collective-permute-start = (bf16[16,3072]{1,0:T(8,128)(2,1)S(1)}, bf16[16,3072]{1,0:T(8,128)(2,1)S(1)}, u32[]{:S(2)}, u32[]{:S(2)}) collective-permute-start(bf16[16,3072]{1,0:T(8,128)(2,1)S(1)} %get-tuple-element.439), channel_id=1, source_target_pairs={{4,0},{8,4},{12,8},{5,1},{9,5},{13,9},{6,2},{10,6},{14,10},{7,3},{... | collective-permute-start | bytes 294920 | tf_op jit(solution)/shard_map/while/body/eval_jaxpr/ppermute | solution.py:12
  390.3 19.8 %copy-start.2 = (bf16[2,16,3072]{2,1,0:T(8,128)(2,1)}, bf16[2,16,3072]{2,1,0:T(8,128)(2,1)S(1)}, u32[]{:S(2)}) copy-start(bf16[2,16,3072]{2,1,0:T(8,128)(2,1)S(1)} %get-tuple-element.285) | copy-start | bytes 589828
  390.3 15.3 %copy-start = (f32[1536,3072]{1,0:T(8,128)S(1)}, f32[1536,3072]{1,0:T(8,128)}, u32[]{:S(2)}) copy-start(f32[1536,3072]{1,0:T(8,128)} %get-tuple-element.287) | copy-start | bytes 56623108
Sparse Core Ops, SparseCore 0:
  57.9 23.0 reduce-scatter.1
  128.0 23.7 reduce-scatter.1
  202.8 23.7 reduce-scatter.1
  277.6 23.7 reduce-scatter.1
  352.3 23.7 reduce-scatter.1
where the time goes:
time: 418 us; the launch traced here: 417 us
  matrix products  185 us (44%)
  blocking collectives  117 us (28%)
  waiting for transfers between devices  61.8 us (15%)
  other arithmetic  25.6 us (6%)
  between operations  13.7 us (3%)
  starting transfers between devices  6.65 us (2%)
  local copies, waits for them, and re-layouts  6.42 us (2%)
    psum x5, blocking collectives, tick(): ctx_grad = lax.psum(ctx_part, 'dp').astype(jnp.bfloat16)  75.8 us
    reduce_scatter x5, waiting for transfers between devices, tick(): summed = lax.psum_scatter(branch, 'tensor', scatter_dimension=0, tiled=True)  61.7 us
    dot_general x5, matrix products, tick(): lax.dot_general(context_here, grad_cols, (((0,), (0,)), ((), ())), prefer...  57 us
    dot_general x5, matrix products, tick(): lax.dot_general(input_here, value_grad, (((0,), (0,)), ((), ())), preferr...  55.6 us
    dot_general x5, matrix products, tick(): lax.dot_general(value_grad, value_proj, (((1,), (1,)), ((), ())), preferr...  37.5 us
    dot_general x5, matrix products, tick(): lax.dot_general(grad_cols, out_proj, (((1,), (1,)), ((), ())), preferred_...  33.2 us
    all_gather x5, blocking collectives, tick(): grad_cols = lax.all_gather(incoming, 'tensor', axis=0, tiled=True)  31.1 us
    broadcast_in_dim x1, other arithmetic, per_device(): acc_value.astype(jnp.bfloat16)[None]  11.5 us
  transfers between devices with their start and end apart: 10, of which 5 were waited for; matrix products, arithmetic and copies ran while one was open for 27% of the time, Pallas kernels for 0%

commit v1 on v0

v1 whole, which is shorter than its diff:
```python
import functools

import jax
import jax.numpy as jnp
from jax import lax
from jax.experimental import pallas as pl
from jax.experimental.pallas import tpu as pltpu
from jax.sharding import PartitionSpec as P

HEAD_DIM = 128
MIB = 1 << 20
F32 = jnp.float32
BF16 = jnp.bfloat16


def vmem():
    return pl.BlockSpec(memory_space=pltpu.VMEM)


def smem():
    return pl.BlockSpec(memory_space=pltpu.SMEM)


def params(mib):
    return pltpu.CompilerParams(vmem_limit_bytes=mib * MIB)


def cost(flops, moved):
    return pl.CostEstimate(flops=flops, bytes_accessed=moved, transcendentals=0)


def across(array, axis, flip):
    count = lax.axis_size(axis)
    return lax.ppermute(array, axis, [(i, i ^ flip) for i in range(count)])


def below(array, giver, flip):
    sections, tensors = lax.axis_size("section"), lax.axis_size("tensor")
    pairs = []
    for s in range(sections):
        peer = s - 1 if (s - giver) % 2 == 0 else s + 1
        if not 0 <= peer < sections:
            peer = s
        for t in range(tensors):
            pairs.append((s * tensors + t, peer * tensors + (t ^ flip)))
    return lax.ppermute(array, ("section", "tensor"), pairs)


def probs_kernel(order_ref, q_ref, k_ref, mask_ref, *out_refs):
    seq = q_ref.shape[1]
    heads = q_ref.shape[2] // HEAD_DIM
    half = heads // 2
    blocks = order_ref.shape[0]
    rows = seq // blocks
    causal = mask_ref[...] > 0
    for m, out_ref in enumerate(out_refs):
        starts = [pl.multiple_of(order_ref[b] * rows, rows) for b in range(blocks)]
        q = jnp.concatenate([q_ref[m, pl.ds(s, rows), :] for s in starts], axis=0)
        k = jnp.concatenate([k_ref[m, pl.ds(s, rows), :] for s in starts], axis=0)
        for h in range(heads):
            cols = slice(h * HEAD_DIM, (h + 1) * HEAD_DIM)
            scores = lax.dot_general(
                q[:, cols], k[:, cols], (((1,), (1,)), ((), ())), preferred_element_type=F32
            )
            scores = scores / jnp.sqrt(F32(HEAD_DIM))
            scores = jnp.where(causal, scores, F32(-1e30))
            expo = jnp.exp(scores - jnp.max(scores, axis=-1, keepdims=True))
            probs = (expo / jnp.sum(expo, axis=-1, keepdims=True)).astype(BF16)
            none = jnp.zeros((seq, seq), BF16)
            pair = [probs, none] if h < half else [none, probs]
            out_ref[h, :, :] = jnp.concatenate(pair, axis=0)


def attention_probs(order, queries, keys, mask):
    micro, seq, cols = queries.shape
    heads = cols // HEAD_DIM
    return pl.pallas_call(
        probs_kernel,
        out_shape=[jax.ShapeDtypeStruct((heads, 2 * seq, seq), BF16)] * micro,
        in_specs=[smem(), vmem(), vmem(), vmem()],
        out_specs=[vmem()] * micro,
        compiler_params=params(8),
        cost_estimate=cost(4 * micro * seq * seq * cols, 4 * micro * seq * cols),
        name="probs",
    )(order, queries, keys, mask)


def ctx_matmul(weight_ref, upper, part_ref):
    half = weight_ref.shape[0] // 2
    dims = (((1,), (1,)), ((), ()))
    step = half // 2
    for r in range(0, half, step):
        low = lax.dot_general(weight_ref[r : r + step, :], upper, dims, preferred_element_type=F32)
        high = lax.dot_general(
            weight_ref[half + r : half + r + step, :], upper, dims, preferred_element_type=F32
        )
        part_ref[r : r + step, :] = jnp.concatenate([low, high], axis=1).astype(BF16)


def first_kernel(*refs):
    blocks = refs[:-3]
    weight_ref, part_ref, upper_ref = refs[-3:]
    upper_ref[...] = jnp.concatenate([b[...] for b in blocks], axis=0)
    ctx_matmul(weight_ref, upper_ref[...], part_ref)


def next_kernel(rows, take_ref, *refs):
    near, far = refs[: (len(refs) - 4) // 2], refs[(len(refs) - 4) // 2 : -4]
    prev_ref, weight_ref, part_ref, upper_ref = refs[-4:]
    take = take_ref[0] > 0
    count = len(near)
    for side, group in enumerate((near, far)):
        for b in range(count):
            total = None
            for d, ref in enumerate(group):
                at = (b ^ d) * rows
                term = ref[at : at + rows, :].astype(F32)
                total = term if total is None else total + term
            at = (side * count + b) * rows
            old = prev_ref[at : at + rows, :]
            upper_ref[at : at + rows, :] = jnp.where(take, total, old.astype(F32)).astype(BF16)
    ctx_matmul(weight_ref, upper_ref[...], part_ref)


def ctx_call(kernel, specs, operands, tokens, weight, name):
    cols, width = weight.shape
    return pl.pallas_call(
        kernel,
        out_shape=[
            jax.ShapeDtypeStruct((cols // 2, 2 * tokens), BF16),
            jax.ShapeDtypeStruct((tokens, width), BF16),
        ],
        in_specs=specs,
        out_specs=[vmem(), vmem()],
        compiler_params=params(20),
        cost_estimate=cost(4 * tokens * cols * width, 2 * cols * width),
        name=name,
    )(*operands)


def branch_kernel(terms, *refs):
    parts, (probs_ref, weight_ref) = refs[:terms], refs[terms : terms + 2]
    keep_ref, send_ref, grad_ref = refs[terms + 2 :]
    tokens = probs_ref.shape[2]
    heads = probs_ref.shape[0]
    half = heads // 2
    packed = parts[0][...].astype(F32)
    for ref in parts[1:]:
        packed = packed + ref[...].astype(F32)
    packed = packed.astype(BF16)
    for h in range(heads):
        row = (h % half) * HEAD_DIM
        grad = jnp.dot(
            packed[row : row + HEAD_DIM, :], probs_ref[h], preferred_element_type=F32
        )
        grad_ref[h * HEAD_DIM : (h + 1) * HEAD_DIM, :] = grad.astype(BF16)
    grads = grad_ref[...]
    width = weight_ref.shape[0]
    step = min(width, 768)
    for r in range(0, width, step):
        out = jnp.dot(weight_ref[r : r + step, :], grads, preferred_element_type=F32)
        out = out.T.astype(BF16)
        keep_ref[:, r : r + step] = out[: tokens // 2]
        send_ref[:, r : r + step] = out[tokens // 2 :]


def branch(parts, probs, weight):
    width, cols = weight.shape
    tokens = probs.shape[2]
    half = jax.ShapeDtypeStruct((tokens // 2, width), BF16)
    return pl.pallas_call(
        functools.partial(branch_kernel, len(parts)),
        out_shape=[half, half, jax.ShapeDtypeStruct((cols, tokens), BF16)],
        in_specs=[vmem()] * (len(parts) + 2),
        out_specs=[vmem()] * 3,
        compiler_params=params(20),
        cost_estimate=cost(4 * tokens * cols * width, 2 * cols * width),
        name="branch",
    )(*parts, probs, weight)


def pair_kernel(rows, keep_ref, got_ref, upper_ref, out_ref):
    out = keep_ref[...].astype(F32) + got_ref[...].astype(F32)
    out_ref[:rows, :] = (out[:rows] + upper_ref[:rows, :].astype(F32)).astype(BF16)
    if out.shape[0] > rows:
        out_ref[rows:, :] = out[rows:].astype(BF16)


def pair_sum(keep, got, upper, rows):
    return pl.pallas_call(
        functools.partial(pair_kernel, rows),
        out_shape=jax.ShapeDtypeStruct(keep.shape, BF16),
        in_specs=[vmem()] * 3,
        out_specs=vmem(),
        compiler_params=params(4),
        cost_estimate=cost(keep.size, 6 * keep.size),
        name="pair",
    )(keep, got, upper)


def out_grad_kernel(order_ref, ctx_ref, *refs):
    uppers, out_ref, scratch = refs[:-2], refs[-2], refs[-1]
    tokens = uppers[0].shape[0]
    blocks = order_ref.shape[0]
    rows = tokens // blocks

    @pl.when(pl.program_id(0) == 0)
    def _():
        for m, ref in enumerate(uppers):
            for b in range(blocks):
                at = pl.multiple_of(m * tokens + order_ref[b] * rows, rows)
                scratch[pl.ds(at, rows), :] = ref[b * rows : (b + 1) * rows, :]

    out_ref[...] = lax.dot_general(
        ctx_ref[...], scratch[...], (((0,), (0,)), ((), ())), preferred_element_type=F32
    ).astype(BF16)


def out_grad(order, context, uppers, step):
    total, cols = context.shape
    width = uppers[0].shape[1]
    return pl.pallas_call(
        out_grad_kernel,
        grid=(cols // step,),
        out_shape=jax.ShapeDtypeStruct((cols, width), BF16),
        in_specs=[smem(), pl.BlockSpec((total, step), lambda i: (0, i))] + [vmem()] * len(uppers),
        out_specs=pl.BlockSpec((step, width), lambda i: (i, 0)),
        scratch_shapes=[pltpu.VMEM((total, width), BF16)],
        compiler_params=params(12),
        cost_estimate=cost(2 * total * cols * width, 2 * cols * width),
        name="out_grad",
    )(order, context, *uppers)


def value_grad_kernel(micro, *refs):
    blocks, grads, out_ref, rhs = refs[: -micro - 2], refs[-micro - 2 : -2], refs[-2], refs[-1]

    @pl.when(pl.program_id(0) == 0)
    def _():
        rhs[...] = jnp.concatenate([g[...] for g in grads], axis=1)

    lhs = jnp.concatenate([b[m] for m in range(micro) for b in blocks], axis=0)
    out_ref[...] = lax.dot_general(
        lhs, rhs[...], (((0,), (1,)), ((), ())), preferred_element_type=F32
    ).astype(BF16)


def value_weight_grad(blocks, grads, step):
    micro, rows, width = blocks[0].shape
    cols, tokens = grads[0].shape
    return pl.pallas_call(
        functools.partial(value_grad_kernel, micro),
        grid=(width // step,),
        out_shape=jax.ShapeDtypeStruct((width, cols), BF16),
        in_specs=[pl.BlockSpec((micro, rows, step), lambda i: (0, 0, i))] * len(blocks)
        + [vmem()] * micro,
        out_specs=pl.BlockSpec((step, cols), lambda i: (i, 0)),
        scratch_shapes=[pltpu.VMEM((cols, micro * tokens), BF16)],
        compiler_params=params(12),
        cost_estimate=cost(2 * micro * tokens * cols * width, 2 * cols * width),
        name="value_weight_grad",
    )(*blocks, *grads)


def per_device(cotangent, inputs, queries, keys, context, value_weight, out_weight):
    sections = lax.axis_size("section")
    place = lax.axis_index("section")
    tensors = lax.axis_size("tensor")
    here = lax.axis_index("tensor")
    replicas = lax.axis_size("dp")
    micro, rows, width = cotangent.shape
    seq = queries.shape[2]
    cols = queries.shape[3]
    flips = list(range(0, tensors, 2)) + list(range(1, tensors, 2))
    order = here ^ jnp.array(flips, jnp.int32)
    token = jnp.repeat(order, rows, total_repeat_length=seq) * rows + jnp.arange(seq) % rows
    mask = (token[:, None] >= token[None, :]).astype(jnp.int32)
    value_proj, out_proj = value_weight[0], out_weight[0]

    def gathered(block):
        own = {0: block}
        for f in range(2, tensors, 2):
            own[f] = across(block, "tensor", f)
        for f in range(0, tensors, 2):
            own[f + 1] = across(own[f], "tensor", 1)
        return [own[f] for f in flips]

    probs = attention_probs(order, queries[0], keys[0], mask)

    parts, uppers, grads, sums = [None] * micro, [None] * micro, [None] * micro, [None] * micro
    for m in range(micro):
        blocks = gathered(cotangent[m])
        parts[m], uppers[m] = ctx_call(
            first_kernel, [vmem()] * (len(blocks) + 1), (*blocks, out_proj), seq, out_proj, "first"
        )
    in_blocks = gathered(inputs[0])
    for stage in range(sections):
        for m in range(micro):
            heard = [across(parts[m], "dp", d) for d in range(1, replicas)]
            keep, send, grads[m] = branch([parts[m], *heard], probs[m], value_proj)
            got = across(send, "tensor", 1)
            sums[m] = pair_sum(keep, got, uppers[m], rows)
        if stage == sections - 1:
            break
        take = (place == sections - 2 - stage).astype(jnp.int32).reshape(1)
        for m in range(micro):
            near = [below(sums[m], sections - 1 - stage, f) for f in range(0, tensors, 2)]
            far = [across(n, "tensor", 1) for n in near]
            specs = [smem()] + [vmem()] * (len(near) + len(far) + 2)
            parts[m], uppers[m] = ctx_call(
                functools.partial(next_kernel, rows),
                specs,
                (take, *near, *far, uppers[m], out_proj),
                seq,
                out_proj,
                "next",
            )
    fresh = []
    for m in range(micro):
        total = sums[m][:rows].astype(F32)
        for b in range(1, tensors // 2):
            total = total + across(sums[m][b * rows : (b + 1) * rows], "tensor", 2 * b).astype(F32)
        fresh.append(total.astype(BF16))
    out_w = out_grad(order, context[0].reshape(micro * seq, cols), uppers, 256)
    value_w = value_weight_grad(in_blocks, grads, 256)
    return (jnp.stack(fresh)[None], value_w[None], out_w[None])


def solution(mesh):
    placed = (
        P(None, "tensor", "dp"),
        P("section", None, "tensor", "dp"),
        P("section", None, None, "tensor"),
        P("section", None, None, "tensor"),
        P("section", None, None, "tensor"),
        P("section", "dp", "tensor"),
        P("section", "tensor", "dp"),
    )
    return jax.shard_map(
        per_device,
        mesh=mesh,
        in_specs=placed,
        out_specs=(
            P("section", None, "tensor", "dp"),
            P("section", "dp", "tensor"),
            P("section", "tensor", "dp"),
        ),
        check_vma=False,
    )
```

time: 418 us -> 180 us (0.43)
  matrix products: 185 us -> 0 us
  blocking collectives: 117 us -> 0 us
  Pallas kernels: 0 us -> 60.9 us
  starting transfers between devices: 6.65 us -> 40.7 us
  other arithmetic: 25.6 us -> 4.75 us
  between operations: 13.7 us -> 1.05 us
  local copies, waits for them, and re-layouts: 6.42 us -> 16.4 us
  waiting for transfers between devices: 61.8 us -> 55.6 us
    dot_general x25 -> x0, matrix products: 184 us -> none  [the longest x5 57 us: tick(): lax.dot_general(context_here, grad_cols, (((0,), (0,)), ((), ())), prefer...]
    psum x5 -> x0, blocking collectives: 75.8 us -> none  [tick(): ctx_grad = lax.psum(ctx_part, 'dp').astype(jnp.bfloat16)]
    reduce_scatter x5 -> x0, waiting for transfers between devices: 61.7 us -> none  [tick(): summed = lax.psum_scatter(branch, 'tensor', scatter_dimension=0, tiled=True)]
    pallas_call x0 -> x27, Pallas kernels: none -> 60.9 us  [the longest x8 23 us: branch(): pl.pallas_call(functools.partial(branch_kernel, len(parts)), out_shape=[h...]
    ppermute x5 -> x51, waiting for transfers between devices: 0.01 us -> 55.6 us  [the longest x12 38.8 us: below(): return lax.ppermute(array, ('section', 'tensor'), pairs)]
    all_gather x6 -> x0, blocking collectives: 41.4 us -> none  [the longest x5 31.1 us: tick(): grad_cols = lax.all_gather(incoming, 'tensor', axis=0, tiled=True)]
    ppermute x5 -> x51, starting transfers between devices: 6.46 us -> 40.7 us  [the longest x12 21.5 us: below(): return lax.ppermute(array, ('section', 'tensor'), pairs)]
    broadcast_in_dim x2 -> x1, other arithmetic: 16.1 us -> 0.7 us  [per_device(): return (jnp.stack(fresh)[None], value_w[None], out_w[None])]
  transfers between devices with their start and end apart: 10 -> 51, of which waited for: 5 -> 21; matrix products, arithmetic and copies ran while one was open for 27% -> 3% of each run, Pallas kernels for 0% -> 34%
where the time goes in v1:
time: 180 us; the launch traced here: 179 us
  Pallas kernels  60.9 us (34%)
  waiting for transfers between devices  55.6 us (31%)
  starting transfers between devices  40.7 us (23%)
  local copies, waits for them, and re-layouts  16.4 us (9%)
  other arithmetic  4.75 us (3%)
    ppermute x12, waiting for transfers between devices, below(): return lax.ppermute(array, ('section', 'tensor'), pairs)  38.8 us
    pallas_call x8, Pallas kernels, branch(): pl.pallas_call(functools.partial(branch_kernel, len(parts)), out_shape=[h...  23 us
    ppermute x12, starting transfers between devices, below(): return lax.ppermute(array, ('section', 'tensor'), pairs)  21.5 us
    pallas_call x8, Pallas kernels, ctx_call(): pl.pallas_call(kernel, out_shape=[jax.ShapeDtypeStruct((cols // 2, 2 * to...  21.4 us
    ppermute x39, starting transfers between devices, across(): return lax.ppermute(array, axis, [(i, i ^ flip) for i in range(count)])  19.2 us
    ppermute x39, waiting for transfers between devices, across(): return lax.ppermute(array, axis, [(i, i ^ flip) for i in range(count)])  16.9 us
    unnamed x38, local copies, waits for them, and re-layouts  14.8 us
    pallas_call x1, Pallas kernels, value_weight_grad(): pl.pallas_call(functools.partial(value_grad_kernel, micro), grid=(width /...  8.3 us
  transfers between devices with their start and end apart: 51, of which 21 were waited for; matrix products, arithmetic and copies ran while one was open for 3% of the time, Pallas kernels for 34%

profile of v1, /device:TPU:0, one launch (start us, length us, event | category | flops | bytes accessed | tf_op | source)
XLA Modules:
  0.0 179.4 jit_solution(6178712996902249742)
XLA Ops:
  8.4 3.3 %fusion.2 = s32[64]{0:T(128)S(1)} fusion(pred[64]{0:T(512)(128)(4,1)} %constant.131, pred[64]{0:T(512)(128)(4,1)} %constant.132, pred[64]{0:T(512)(128)(4,1)} %constant.133, s32[]{:T(128)} %bitcast.10, s32[]{:T(128)} %bitcast.7, s32[]{:T(128)} %bitcast.8, s32[]{:T(128)} %bitcast.9), kind=kLoop, calls=%fused_computation.9 | loop fusion | flops 704 | bytes 464 | tf_op jit(solution)/shard_map/add | solution.py:276
  12.2 3.7 %copy-done = bf16[1,1536,3072]{2,1,0:T(8,128)(2,1)S(1)} copy-done((bf16[1,1536,3072]{2,1,0:T(8,128)(2,1)S(1)}, bf16[1,1536,3072]{2,1,0:T(8,128)(2,1)}, u32[]{:S(2)}) %copy-start) | copy-done | bytes 9437208
  32.9 2.9 %collective-permute-start.6 = (bf16[32,3072]{1,0:T(8,128)(2,1)S(1)}, bf16[32,3072]{1,0:T(8,128)(2,1)S(1)}, u32[]{:S(2)}, u32[]{:S(2)}) collective-permute-start(bf16[32,3072]{1,0:T(8,128)(2,1)S(1)} %pair.8), channel_id=1, source_target_pairs={{0,6},{1,7},{2,4},{3,5},{4,2},{5,3},{6,0},{7,1},{8,14},{9,15},{10,... | collective-permute-start | bytes 589832 | tf_op jit(solution)/shard_map/ppermute | solution.py:46
  38.1 3.6 %collective-permute-done.6.refs_1_ = bf16[32,3072]{1,0:T(8,128)(2,1)S(1)} collective-permute-done((bf16[32,3072]{1,0:T(8,128)(2,1)S(1)}, bf16[32,3072]{1,0:T(8,128)(2,1)S(1)}, u32[]{:S(2)}, u32[]{:S(2)}) %collective-permute-start.6) | collective-permute-done | bytes 196640 | tf_op jit(solution)/shard_map/ppermute | solution.py:46
  41.7 4.6 %collective-permute-done.5.refs_0_ = bf16[32,3072]{1,0:T(8,128)(2,1)S(1)} collective-permute-done((bf16[32,3072]{1,0:T(8,128)(2,1)S(1)}, bf16[32,3072]{1,0:T(8,128)(2,1)S(1)}, u32[]{:S(2)}, u32[]{:S(2)}) %collective-permute-start.5) | collective-permute-done | bytes 196640 | tf_op jit(solution)/shard_map/ppermute | solution.py:46
  46.2 3.9 %collective-permute-done.30.refs_1_ = bf16[32,3072]{1,0:T(8,128)(2,1)S(1)} collective-permute-done((bf16[32,3072]{1,0:T(8,128)(2,1)S(1)}, bf16[32,3072]{1,0:T(8,128)(2,1)S(1)}, u32[]{:S(2)}, u32[]{:S(2)}) %collective-permute-start.30) | collective-permute-done | bytes 196640 | tf_op jit(solution)/shard_map/ppermute | solution.py:46
  50.1 4.1 %collective-permute-done.29.refs_0_ = bf16[32,3072]{1,0:T(8,128)(2,1)S(1)} collective-permute-done((bf16[32,3072]{1,0:T(8,128)(2,1)S(1)}, bf16[32,3072]{1,0:T(8,128)(2,1)S(1)}, u32[]{:S(2)}, u32[]{:S(2)}) %collective-permute-start.29) | collective-permute-done | bytes 196640 | tf_op jit(solution)/shard_map/ppermute | solution.py:46
  54.2 3.7 %copy-done.2 = bf16[1,1536,3072]{2,1,0:T(8,128)(2,1)S(1)} copy-done((bf16[1,1536,3072]{2,1,0:T(8,128)(2,1)S(1)}, bf16[1,1536,3072]{2,1,0:T(8,128)(2,1)}, u32[]{:S(2)}) %copy-start.2) | copy-done | bytes 9437208
  68.0 2.9 %branch.9 = (bf16[32,3072]{1,0:T(8,128)(2,1)S(1)}, bf16[32,3072]{1,0:T(8,128)(2,1)S(1)}, bf16[1536,64]{1,0:T(8,128)(2,1)}) custom-call(bf16[768,128]{1,0:T(8,128)(2,1)S(1)} %get-tuple-element.56.refs_0_, bf16[768,128]{1,0:T(8,128)(2,1)S(1)} %collective-permute-done.9.refs_1_, bf16[12,128,64]{2,1,0:T(8,128)(2,1)S(1)} %get-tuple-element.52.refs_2_, ...), custom_call_target="tpu_custom_call" | custom-call | flops 1207959552 | bytes 9437184 | tf_op jit(solution)/shard_map/branch/pallas_call | solution.py:171
  78.7 4.3 %collective-permute-done.12.refs_1_ = bf16[32,3072]{1,0:T(8,128)(2,1)S(1)} collective-permute-done((bf16[32,3072]{1,0:T(8,128)(2,1)S(1)}, bf16[32,3072]{1,0:T(8,128)(2,1)S(1)}, u32[]{:S(2)}, u32[]{:S(2)}) %collective-permute-start.12) | collective-permute-done | bytes 196640 | tf_op jit(solution)/shard_map/ppermute | solution.py:46
  83.5 3.2 %collective-permute-done.36.refs_1_ = bf16[32,3072]{1,0:T(8,128)(2,1)S(1)} collective-permute-done((bf16[32,3072]{1,0:T(8,128)(2,1)S(1)}, bf16[32,3072]{1,0:T(8,128)(2,1)S(1)}, u32[]{:S(2)}, u32[]{:S(2)}) %collective-permute-start.36) | collective-permute-done | bytes 196640 | tf_op jit(solution)/shard_map/ppermute | solution.py:46
  87.2 3.7 %copy-done.3 = bf16[1,1536,3072]{2,1,0:T(8,128)(2,1)S(1)} copy-done((bf16[1,1536,3072]{2,1,0:T(8,128)(2,1)S(1)}, bf16[1,1536,3072]{2,1,0:T(8,128)(2,1)}, u32[]{:S(2)}) %copy-start.3) | copy-done | bytes 9437208
  100.7 2.9 %branch.10 = (bf16[32,3072]{1,0:T(8,128)(2,1)S(1)}, bf16[32,3072]{1,0:T(8,128)(2,1)S(1)}, bf16[1536,64]{1,0:T(8,128)(2,1)}) custom-call(bf16[768,128]{1,0:T(8,128)(2,1)S(1)} %get-tuple-element.60.refs_0_, bf16[768,128]{1,0:T(8,128)(2,1)S(1)} %collective-permute-done.15.refs_1_, bf16[12,128,64]{2,1,0:T(8,128)(2,1)S(1)} %get-tuple-element.52.refs_2_, ...), custom_call_target="tpu_custom_call" | custom-call | flops 1207959552 | bytes 9437184 | tf_op jit(solution)/shard_map/branch/pallas_call | solution.py:171
  104.7 2.9 %branch.14 = (bf16[32,3072]{1,0:T(8,128)(2,1)S(1)}, bf16[32,3072]{1,0:T(8,128)(2,1)S(1)}, bf16[1536,64]{1,0:T(8,128)(2,1)}) custom-call(bf16[768,128]{1,0:T(8,128)(2,1)S(1)} %get-tuple-element.77.refs_0_, bf16[768,128]{1,0:T(8,128)(2,1)S(1)} %collective-permute-done.39.refs_1_, bf16[12,128,64]{2,1,0:T(8,128)(2,1)S(1)} %get-tuple-element.69.refs_2_, ...), custom_call_target="tpu_custom_call" | custom-call | flops 1207959552 | bytes 9437184 | tf_op jit(solution)/shard_map/branch/pallas_call | solution.py:171
  107.7 11.0 %collective-permute-start.18 = (bf16[32,3072]{1,0:T(8,128)(2,1)S(1)}, bf16[32,3072]{1,0:T(8,128)(2,1)S(1)}, u32[]{:S(2)}, u32[]{:S(2)}) collective-permute-start(bf16[32,3072]{1,0:T(8,128)(2,1)S(1)} %pair.10), channel_id=1, source_target_pairs={{0,6},{1,7},{2,4},{3,5},{4,2},{5,3},{6,0},{7,1},{8,14},{9,15},{10,... | collective-permute-start | bytes 589832 | tf_op jit(solution)/shard_map/ppermute | solution.py:46
  120.9 3.5 %collective-permute-done.18.refs_1_ = bf16[32,3072]{1,0:T(8,128)(2,1)S(1)} collective-permute-done((bf16[32,3072]{1,0:T(8,128)(2,1)S(1)}, bf16[32,3072]{1,0:T(8,128)(2,1)S(1)}, u32[]{:S(2)}, u32[]{:S(2)}) %collective-permute-start.18) | collective-permute-done | bytes 196640 | tf_op jit(solution)/shard_map/ppermute | solution.py:46
  124.4 3.7 %collective-permute-done.17.refs_0_ = bf16[32,3072]{1,0:T(8,128)(2,1)S(1)} collective-permute-done((bf16[32,3072]{1,0:T(8,128)(2,1)S(1)}, bf16[32,3072]{1,0:T(8,128)(2,1)S(1)}, u32[]{:S(2)}, u32[]{:S(2)}) %collective-permute-start.17) | collective-permute-done | bytes 196640 | tf_op jit(solution)/shard_map/ppermute | solution.py:46
  128.1 4.7 %collective-permute-done.42.refs_1_ = bf16[32,3072]{1,0:T(8,128)(2,1)S(1)} collective-permute-done((bf16[32,3072]{1,0:T(8,128)(2,1)S(1)}, bf16[32,3072]{1,0:T(8,128)(2,1)S(1)}, u32[]{:S(2)}, u32[]{:S(2)}) %collective-permute-start.42) | collective-permute-done | bytes 196640 | tf_op jit(solution)/shard_map/ppermute | solution.py:46
  132.8 3.3 %collective-permute-done.41.refs_0_ = bf16[32,3072]{1,0:T(8,128)(2,1)S(1)} collective-permute-done((bf16[32,3072]{1,0:T(8,128)(2,1)S(1)}, bf16[32,3072]{1,0:T(8,128)(2,1)S(1)}, u32[]{:S(2)}, u32[]{:S(2)}) %collective-permute-start.41) | collective-permute-done | bytes 196640 | tf_op jit(solution)/shard_map/ppermute | solution.py:46
  137.4 3.7 %copy-done.4 = bf16[1,1536,3072]{2,1,0:T(8,128)(2,1)S(1)} copy-done((bf16[1,1536,3072]{2,1,0:T(8,128)(2,1)S(1)}, bf16[1,1536,3072]{2,1,0:T(8,128)(2,1)}, u32[]{:S(2)}) %copy-start.4) | copy-done | bytes 9437208
  151.1 3.1 %branch.11 = (bf16[32,3072]{1,0:T(8,128)(2,1)S(1)}, bf16[32,3072]{1,0:T(8,128)(2,1)S(1)}, bf16[1536,64]{1,0:T(8,128)(2,1)S(1)}) custom-call(bf16[768,128]{1,0:T(8,128)(2,1)S(1)} %get-tuple-element.64.refs_0_, bf16[768,128]{1,0:T(8,128)(2,1)S(1)} %collective-permute-done.21.refs_1_, bf16[12,128,64]{2,1,0:T(8,128)(2,1)S(1)} %get-tuple-element.52.refs_2_, ...), custom_call_target="tpu_custom_call" | custom-call | flops 1207959552 | bytes 9437184 | tf_op jit(solution)/shard_map/branch/pallas_call | solution.py:171
  158.0 6.5 %out_grad.1 = bf16[1536,3072]{1,0:T(8,128)(2,1)} custom-call(s32[4]{0:T(128)S(1)} %broadcast_xor_fusion.order_ref, bf16[128,1536]{1,0:T(8,128)(2,1)S(1)} %bitcast.49, bf16[64,3072]{1,0:T(8,128)(2,1)S(1)} %get-tuple-element.67.upper_ref.refs_0_, bf16[64,3072]{1,0:T(8,128)(2,1)S(1)} %get-tuple-element.84.upper_ref.refs_1_), custom_call_target="tpu_custom_call" | custom-call | flops 1207959552 | bytes 9437184 | tf_op jit(solution)/shard_map/out_grad/pallas_call | solution.py:222
  165.4 8.3 %value_weight_grad.1 = bf16[3072,1536]{1,0:T(8,128)(2,1)} custom-call(bf16[2,16,3072]{2,1,0:T(8,128)(2,1)S(1)} %bitcast.52, bf16[2,16,3072]{2,1,0:T(8,128)(2,1)S(1)} %collective-permute-done.48.refs_1_, bf16[2,16,3072]{2,1,0:T(8,128)(2,1)S(1)} %collective-permute-done.49.refs_2_, bf16[2,16,3072]{2,1,0:T(8,128)(2,1)S(1)} %collective-permute-done.50.refs_3_, ...), custom_call_target="tpu_custom_call" | custom-call | flops 1207959552 | bytes 9437184 | tf_op jit(solution)/shard_map/value_weight_grad/pallas_call | solution.py:251
  175.2 3.5 %collective-permute-done.47 = bf16[16,3072]{1,0:T(8,128)(2,1)S(1)} collective-permute-done((bf16[16,3072]{1,0:T(8,128)(2,1)S(1)}, bf16[16,3072]{1,0:T(8,128)(2,1)S(1)}, u32[]{:S(2)}, u32[]{:S(2)}) %collective-permute-start.47) | collective-permute-done | bytes 98336 | tf_op jit(solution)/shard_map/ppermute | solution.py:34
  (156 shorter events, 77.8 us)
Async XLA Ops:
  1.6 10.6 %collective-permute-start.1 = (bf16[16,3072]{1,0:T(8,128)(2,1)S(1)}, bf16[16,3072]{1,0:T(8,128)(2,1)S(1)}, u32[]{:S(2)}, u32[]{:S(2)}) collective-permute-start(bf16[16,3072]{1,0:T(8,128)(2,1)S(1)} %get-tuple-element.87.refs_0_), channel_id=1, source_target_pairs={{0,1},{1,0},{2,3},{3,2},{4,5},{5,4},{6,7},{7,6},{8,9},{9,8},{10,11... | collective-permute-start | bytes 294920 | tf_op jit(solution)/shard_map/ppermute | solution.py:34
  4.7 15.9 %collective-permute-start.25 = (bf16[16,3072]{1,0:T(8,128)(2,1)S(1)}, bf16[16,3072]{1,0:T(8,128)(2,1)S(1)}, u32[]{:S(2)}, u32[]{:S(2)}) collective-permute-start(bf16[16,3072]{1,0:T(8,128)(2,1)S(1)} %get-tuple-element.88.refs_0_), channel_id=1, source_target_pairs={{0,1},{1,0},{2,3},{3,2},{4,5},{5,4},{6,7},{7,6},{8,9},{9,8},{10,11... | collective-permute-start | bytes 294920 | tf_op jit(solution)/shard_map/ppermute | solution.py:34
  11.7 9.0 %collective-permute-start.26 = (bf16[16,3072]{1,0:T(8,128)(2,1)S(1)}, bf16[16,3072]{1,0:T(8,128)(2,1)S(1)}, u32[]{:S(2)}, u32[]{:S(2)}) collective-permute-start(bf16[16,3072]{1,0:T(8,128)(2,1)S(1)} %collective-permute-done.24.refs_1_), channel_id=1, source_target_pairs={{0,1},{1,0},{2,3},{3,2},{4,5},{5,4},{6,7},{7,6},{8,9},{9,8},{10,11... | collective-permute-start | bytes 294920 | tf_op jit(solution)/shard_map/ppermute | solution.py:34
  35.8 10.4 %collective-permute-start.5 = (bf16[32,3072]{1,0:T(8,128)(2,1)S(1)}, bf16[32,3072]{1,0:T(8,128)(2,1)S(1)}, u32[]{:S(2)}, u32[]{:S(2)}) collective-permute-start(bf16[32,3072]{1,0:T(8,128)(2,1)S(1)} %pair.8), channel_id=1, source_target_pairs={{0,4},{1,5},{2,6},{3,7},{4,0},{5,1},{6,2},{7,3},{8,12},{9,13},{10,... | collective-permute-start | bytes 589832 | tf_op jit(solution)/shard_map/ppermute | solution.py:46
  36.3 13.8 %collective-permute-start.30 = (bf16[32,3072]{1,0:T(8,128)(2,1)S(1)}, bf16[32,3072]{1,0:T(8,128)(2,1)S(1)}, u32[]{:S(2)}, u32[]{:S(2)}) collective-permute-start(bf16[32,3072]{1,0:T(8,128)(2,1)S(1)} %pair.12), channel_id=1, source_target_pairs={{0,6},{1,7},{2,4},{3,5},{4,2},{5,3},{6,0},{7,1},{8,14},{9,15},{10,... | collective-permute-start | bytes 589832 | tf_op jit(solution)/shard_map/ppermute | solution.py:46
  37.9 16.3 %collective-permute-start.29 = (bf16[32,3072]{1,0:T(8,128)(2,1)S(1)}, bf16[32,3072]{1,0:T(8,128)(2,1)S(1)}, u32[]{:S(2)}, u32[]{:S(2)}) collective-permute-start(bf16[32,3072]{1,0:T(8,128)(2,1)S(1)} %pair.12), channel_id=1, source_target_pairs={{0,4},{1,5},{2,6},{3,7},{4,0},{5,1},{6,2},{7,3},{8,12},{9,13},{10,... | collective-permute-start | bytes 589832 | tf_op jit(solution)/shard_map/ppermute | solution.py:46
  41.7 12.5 %collective-permute-start.8 = (bf16[32,3072]{1,0:T(8,128)(2,1)S(1)}, bf16[32,3072]{1,0:T(8,128)(2,1)S(1)}, u32[]{:S(2)}, u32[]{:S(2)}) collective-permute-start(bf16[32,3072]{1,0:T(8,128)(2,1)S(1)} %collective-permute-done.6.refs_1_), channel_id=1, source_target_pairs={{0,1},{1,0},{2,3},{3,2},{4,5},{5,4},{6,7},{7,6},{8,9},{9,8},{10,11... | collective-permute-start | bytes 589832 | tf_op jit(solution)/shard_map/ppermute | solution.py:34
  50.1 12.0 %collective-permute-start.32 = (bf16[32,3072]{1,0:T(8,128)(2,1)S(1)}, bf16[32,3072]{1,0:T(8,128)(2,1)S(1)}, u32[]{:S(2)}, u32[]{:S(2)}) collective-permute-start(bf16[32,3072]{1,0:T(8,128)(2,1)S(1)} %collective-permute-done.30.refs_1_), channel_id=1, source_target_pairs={{0,1},{1,0},{2,3},{3,2},{4,5},{5,4},{6,7},{7,6},{8,9},{9,8},{10,11... | collective-permute-start | bytes 589832 | tf_op jit(solution)/shard_map/ppermute | solution.py:34
  76.5 10.2 %collective-permute-start.36 = (bf16[32,3072]{1,0:T(8,128)(2,1)S(1)}, bf16[32,3072]{1,0:T(8,128)(2,1)S(1)}, u32[]{:S(2)}, u32[]{:S(2)}) collective-permute-start(bf16[32,3072]{1,0:T(8,128)(2,1)S(1)} %pair.13), channel_id=1, source_target_pairs={{0,2},{1,3},{2,0},{3,1},{4,10},{5,11},{6,8},{7,9},{8,6},{9,7},{10,... | collective-permute-start | bytes 589832 | tf_op jit(solution)/shard_map/ppermute | solution.py:46
  107.5 11.1 %collective-permute-start.40 = (bf16[32,3072]{1,0:T(8,128)(2,1)S(1)}, bf16[32,3072]{1,0:T(8,128)(2,1)S(1)}, u32[]{:S(2)}, u32[]{:S(2)}) collective-permute-start(bf16[32,3072]{1,0:T(8,128)(2,1)S(1)} %get-tuple-element.79), channel_id=1, source_target_pairs={{0,1},{1,0},{2,3},{3,2},{4,5},{5,4},{6,7},{7,6},{8,9},{9,8},{10,11... | collective-permute-start | bytes 589832 | tf_op jit(solution)/shard_map/ppermute | solution.py:34
  107.7 16.7 %collective-permute-start.18 = (bf16[32,3072]{1,0:T(8,128)(2,1)S(1)}, bf16[32,3072]{1,0:T(8,128)(2,1)S(1)}, u32[]{:S(2)}, u32[]{:S(2)}) collective-permute-start(bf16[32,3072]{1,0:T(8,128)(2,1)S(1)} %pair.10), channel_id=1, source_target_pairs={{0,6},{1,7},{2,4},{3,5},{4,2},{5,3},{6,0},{7,1},{8,14},{9,15},{10,... | collective-permute-start | bytes 589832 | tf_op jit(solution)/shard_map/ppermute | solution.py:46
  118.6 9.5 %collective-permute-start.17 = (bf16[32,3072]{1,0:T(8,128)(2,1)S(1)}, bf16[32,3072]{1,0:T(8,128)(2,1)S(1)}, u32[]{:S(2)}, u32[]{:S(2)}) collective-permute-start(bf16[32,3072]{1,0:T(8,128)(2,1)S(1)} %pair.10), channel_id=1, source_target_pairs={{0,4},{1,5},{2,6},{3,7},{4,0},{5,1},{6,2},{7,3},{8,12},{9,13},{10,... | collective-permute-start | bytes 589832 | tf_op jit(solution)/shard_map/ppermute | solution.py:46
  118.7 14.1 %collective-permute-start.42 = (bf16[32,3072]{1,0:T(8,128)(2,1)S(1)}, bf16[32,3072]{1,0:T(8,128)(2,1)S(1)}, u32[]{:S(2)}, u32[]{:S(2)}) collective-permute-start(bf16[32,3072]{1,0:T(8,128)(2,1)S(1)} %pair.14), channel_id=1, source_target_pairs={{0,6},{1,7},{2,4},{3,5},{4,2},{5,3},{6,0},{7,1},{8,14},{9,15},{10,... | collective-permute-start | bytes 589832 | tf_op jit(solution)/shard_map/ppermute | solution.py:46
  120.7 15.4 %collective-permute-start.41 = (bf16[32,3072]{1,0:T(8,128)(2,1)S(1)}, bf16[32,3072]{1,0:T(8,128)(2,1)S(1)}, u32[]{:S(2)}, u32[]{:S(2)}) collective-permute-start(bf16[32,3072]{1,0:T(8,128)(2,1)S(1)} %pair.14), channel_id=1, source_target_pairs={{0,4},{1,5},{2,6},{3,7},{4,0},{5,1},{6,2},{7,3},{8,12},{9,13},{10,... | collective-permute-start | bytes 589832 | tf_op jit(solution)/shard_map/ppermute | solution.py:46
  124.4 13.0 %collective-permute-start.20 = (bf16[32,3072]{1,0:T(8,128)(2,1)S(1)}, bf16[32,3072]{1,0:T(8,128)(2,1)S(1)}, u32[]{:S(2)}, u32[]{:S(2)}) collective-permute-start(bf16[32,3072]{1,0:T(8,128)(2,1)S(1)} %collective-permute-done.18.refs_1_), channel_id=1, source_target_pairs={{0,1},{1,0},{2,3},{3,2},{4,5},{5,4},{6,7},{7,6},{8,9},{9,8},{10,11... | collective-permute-start | bytes 589832 | tf_op jit(solution)/shard_map/ppermute | solution.py:34
  128.1 9.3 %collective-permute-start.19 = (bf16[32,3072]{1,0:T(8,128)(2,1)S(1)}, bf16[32,3072]{1,0:T(8,128)(2,1)S(1)}, u32[]{:S(2)}, u32[]{:S(2)}) collective-permute-start(bf16[32,3072]{1,0:T(8,128)(2,1)S(1)} %collective-permute-done.17.refs_0_), channel_id=1, source_target_pairs={{0,1},{1,0},{2,3},{3,2},{4,5},{5,4},{6,7},{7,6},{8,9},{9,8},{10,11... | collective-permute-start | bytes 589832 | tf_op jit(solution)/shard_map/ppermute | solution.py:34
  132.8 12.5 %collective-permute-start.44 = (bf16[32,3072]{1,0:T(8,128)(2,1)S(1)}, bf16[32,3072]{1,0:T(8,128)(2,1)S(1)}, u32[]{:S(2)}, u32[]{:S(2)}) collective-permute-start(bf16[32,3072]{1,0:T(8,128)(2,1)S(1)} %collective-permute-done.42.refs_1_), channel_id=1, source_target_pairs={{0,1},{1,0},{2,3},{3,2},{4,5},{5,4},{6,7},{7,6},{8,9},{9,8},{10,11... | collective-permute-start | bytes 589832 | tf_op jit(solution)/shard_map/ppermute | solution.py:34
  136.1 9.2 %collective-permute-start.43 = (bf16[32,3072]{1,0:T(8,128)(2,1)S(1)}, bf16[32,3072]{1,0:T(8,128)(2,1)S(1)}, u32[]{:S(2)}, u32[]{:S(2)}) collective-permute-start(bf16[32,3072]{1,0:T(8,128)(2,1)S(1)} %collective-permute-done.41.refs_0_), channel_id=1, source_target_pairs={{0,1},{1,0},{2,3},{3,2},{4,5},{5,4},{6,7},{7,6},{8,9},{9,8},{10,11... | collective-permute-start | bytes 589832 | tf_op jit(solution)/shard_map/ppermute | solution.py:34
  136.1 12.5 %collective-permute-start.48 = (bf16[2,16,3072]{2,1,0:T(8,128)(2,1)S(1)}, bf16[2,16,3072]{2,1,0:T(8,128)(2,1)S(1)}, u32[]{:S(2)}, u32[]{:S(2)}) collective-permute-start(bf16[2,16,3072]{2,1,0:T(8,128)(2,1)S(1)} %bitcast.50), channel_id=1, source_target_pairs={{0,2},{1,3},{2,0},{3,1},{4,6},{5,7},{6,4},{7,5},{8,10},{9,11},{10,... | collective-permute-start | bytes 589832 | tf_op jit(solution)/shard_map/ppermute | solution.py:34
  148.6 16.8 %collective-permute-start.49 = (bf16[2,16,3072]{2,1,0:T(8,128)(2,1)S(1)}, bf16[2,16,3072]{2,1,0:T(8,128)(2,1)S(1)}, u32[]{:S(2)}, u32[]{:S(2)}) collective-permute-start(bf16[2,16,3072]{2,1,0:T(8,128)(2,1)S(1)} %bitcast.51), channel_id=1, source_target_pairs={{0,1},{1,0},{2,3},{3,2},{4,5},{5,4},{6,7},{7,6},{8,9},{9,8},{10,11... | collective-permute-start | bytes 589832 | tf_op jit(solution)/shard_map/ppermute | solution.py:34
  148.6 16.8 %collective-permute-start.50 = (bf16[2,16,3072]{2,1,0:T(8,128)(2,1)S(1)}, bf16[2,16,3072]{2,1,0:T(8,128)(2,1)S(1)}, u32[]{:S(2)}, u32[]{:S(2)}) collective-permute-start(bf16[2,16,3072]{2,1,0:T(8,128)(2,1)S(1)} %collective-permute-done.48.refs_1_), channel_id=1, source_target_pairs={{0,1},{1,0},{2,3},{3,2},{4,5},{5,4},{6,7},{7,6},{8,9},{9,8},{10,11... | collective-permute-start | bytes 589832 | tf_op jit(solution)/shard_map/ppermute | solution.py:34
  154.2 10.3 %collective-permute-start.22 = (bf16[32,3072]{1,0:T(8,128)(2,1)S(1)}, bf16[32,3072]{1,0:T(8,128)(2,1)S(1)}, u32[]{:S(2)}, u32[]{:S(2)}) collective-permute-start(bf16[32,3072]{1,0:T(8,128)(2,1)S(1)} %get-tuple-element.66), channel_id=1, source_target_pairs={{0,1},{1,0},{2,3},{3,2},{4,5},{5,4},{6,7},{7,6},{8,9},{9,8},{10,11... | collective-permute-start | bytes 589832 | tf_op jit(solution)/shard_map/ppermute | solution.py:34
  157.9 15.8 %collective-permute-start.46 = (bf16[32,3072]{1,0:T(8,128)(2,1)S(1)}, bf16[32,3072]{1,0:T(8,128)(2,1)S(1)}, u32[]{:S(2)}, u32[]{:S(2)}) collective-permute-start(bf16[32,3072]{1,0:T(8,128)(2,1)S(1)} %get-tuple-element.83), channel_id=1, source_target_pairs={{0,1},{1,0},{2,3},{3,2},{4,5},{5,4},{6,7},{7,6},{8,9},{9,8},{10,11... | collective-permute-start | bytes 589832 | tf_op jit(solution)/shard_map/ppermute | solution.py:34
  164.6 10.6 %collective-permute-start.23 = (bf16[16,3072]{1,0:T(8,128)(2,1)S(1)}, bf16[16,3072]{1,0:T(8,128)(2,1)S(1)}, u32[]{:S(2)}, u32[]{:S(2)}) collective-permute-start(bf16[16,3072]{1,0:T(8,128)(2,1)S(1)} %slice.43), channel_id=1, source_target_pairs={{0,2},{1,3},{2,0},{3,1},{4,6},{5,7},{6,4},{7,5},{8,10},{9,11},{10,... | collective-permute-start | bytes 294920 | tf_op jit(solution)/shard_map/ppermute | solution.py:34
  (46 other events, 346.5 us)

commit v2 on v0

v2 whole, which is shorter than its diff:
```python
import functools

import jax
import jax.numpy as jnp
from jax import lax
from jax.experimental import pallas as pl
from jax.experimental.pallas import tpu as pltpu
from jax.sharding import PartitionSpec as P


HEAD_DIM = 128
MIB = 1 << 20
F32 = jnp.float32
BF16 = jnp.bfloat16


def vmem():
    return pl.BlockSpec(memory_space=pltpu.VMEM)


def params(mib):
    return pltpu.CompilerParams(vmem_limit_bytes=mib * MIB)


def cost(flops, moved):
    return pl.CostEstimate(flops=flops, bytes_accessed=moved, transcendentals=0)


def run(kernel, outs, operands, after, flops, moved):
    count = len(operands)

    def body(*refs):
        kernel(*refs[:count], *refs[count + len(after) :])

    return pl.pallas_call(
        body,
        out_shape=[jax.ShapeDtypeStruct(*out) for out in outs],
        in_specs=[vmem()] * (count + len(after)),
        out_specs=[vmem()] * len(outs),
        compiler_params=params(4),
        cost_estimate=cost(flops, moved),
    )(*operands, *after)


def across(array, axis, flip):
    count = lax.axis_size(axis)
    return lax.ppermute(array, axis, [(i, i ^ flip) for i in range(count)])


def below(array, giver, flip):
    sections, tensors = lax.axis_size("section"), lax.axis_size("tensor")
    pairs = []
    for s in range(sections):
        peer = s - 1 if (s - giver) % 2 == 0 else s + 1
        if not 0 <= peer < sections:
            peer = s
        for t in range(tensors):
            pairs.append((s * tensors + t, peer * tensors + (t ^ flip)))
    return lax.ppermute(array, ("section", "tensor"), pairs)


def token_order(tensors):
    here = lax.axis_index("tensor")
    return [here ^ f for f in [*range(0, tensors, 2), *range(1, tensors, 2)]]


def probs_kernel(tensors, q_ref, k_ref, *out_refs):
    seq = q_ref.shape[1]
    heads = q_ref.shape[2] // HEAD_DIM
    half = heads // 2
    rows = seq // tensors
    order = token_order(tensors)
    starts = [pl.multiple_of(block * rows, rows) for block in order]
    down = lax.broadcasted_iota(jnp.int32, (seq, seq), 0)
    along = lax.broadcasted_iota(jnp.int32, (seq, seq), 1)
    query_at, key_at = down % rows, along % rows
    for b, start in enumerate(starts):
        query_at = query_at + jnp.where(down // rows == b, start, 0)
        key_at = key_at + jnp.where(along // rows == b, start, 0)
    causal = query_at >= key_at
    for m, out_ref in enumerate(out_refs):
        q = jnp.concatenate([q_ref[m, pl.ds(s, rows), :] for s in starts], axis=0)
        k = jnp.concatenate([k_ref[m, pl.ds(s, rows), :] for s in starts], axis=0)
        for h in range(heads):
            cols = slice(h * HEAD_DIM, (h + 1) * HEAD_DIM)
            scores = lax.dot_general(
                q[:, cols], k[:, cols], (((1,), (1,)), ((), ())), preferred_element_type=F32
            )
            scores = scores / jnp.sqrt(F32(HEAD_DIM))
            scores = jnp.where(causal, scores, F32(-1e30))
            expo = jnp.exp(scores - jnp.max(scores, axis=-1, keepdims=True))
            probs = (expo / jnp.sum(expo, axis=-1, keepdims=True)).astype(BF16)
            none = jnp.zeros((seq, seq), BF16)
            pair = [probs, none] if h < half else [none, probs]
            out_ref[h, :, :] = jnp.concatenate(pair, axis=0)


def attention_probs(queries, keys, tensors):
    micro, seq, cols = queries.shape
    outs = [((cols // HEAD_DIM, 2 * seq, seq), BF16)] * micro
    flops = 4 * micro * seq * seq * cols
    kernel = functools.partial(probs_kernel, tensors)
    return run(kernel, outs, [queries, keys], [], flops, 4 * queries.size)


def ctx_matmul(weight_ref, upper, part_ref):
    half = weight_ref.shape[0] // 2
    step = min(half, 384)
    dims = (((1,), (1,)), ((), ()))
    for at in range(0, half, step):
        low, high = (
            lax.dot_general(
                weight_ref[at + off : at + off + step, :], upper, dims, preferred_element_type=F32
            )
            for off in (0, half)
        )
        part_ref[at : at + step, :] = jnp.concatenate([low, high], axis=1).astype(BF16)


def first_kernel(*refs):
    blocks = refs[:-3]
    weight_ref, part_ref, upper_ref = refs[-3:]
    upper_ref[...] = jnp.concatenate([b[...] for b in blocks], axis=0)
    ctx_matmul(weight_ref, upper_ref[...], part_ref)


def next_kernel(rows, taker, *refs):
    blocks = refs[:-4]
    prev_ref, weight_ref, part_ref, upper_ref = refs[-4:]
    take = lax.axis_index("section") == taker
    for b, ref in enumerate(blocks):
        at = slice(b * rows, (b + 1) * rows)
        upper_ref[at, :] = jnp.where(take, ref[...], prev_ref[at, :])
    ctx_matmul(weight_ref, upper_ref[...], part_ref)


def ctx_call(kernel, operands, tokens, weight, after):
    cols, width = weight.shape
    outs = [((cols // 2, 2 * tokens), BF16), ((tokens, width), BF16)]
    flops = 2 * tokens * cols * width
    return run(kernel, outs, [*operands, weight], after, flops, 2 * weight.size)


def branch_kernel(terms, *refs):
    parts, (probs_ref, weight_ref) = refs[:terms], refs[terms : terms + 2]
    keep_ref, send_ref, grad_ref = refs[-3:]
    tokens = probs_ref.shape[2]
    heads = probs_ref.shape[0]
    half = heads // 2
    packed = parts[0][...].astype(F32)
    for ref in parts[1:]:
        packed = packed + ref[...].astype(F32)
    packed = packed.astype(BF16)
    for h in range(heads):
        row = (h % half) * HEAD_DIM
        grad = jnp.dot(
            packed[row : row + HEAD_DIM, :], probs_ref[h], preferred_element_type=F32
        )
        grad_ref[h * HEAD_DIM : (h + 1) * HEAD_DIM, :] = grad.astype(BF16)
    grads = grad_ref[...]
    width = weight_ref.shape[0]
    step = min(width, 768)
    for at in range(0, width, step):
        out = jnp.dot(weight_ref[at : at + step, :], grads, preferred_element_type=F32)
        out = out.T.astype(BF16)
        keep_ref[:, at : at + step] = out[: tokens // 2]
        send_ref[:, at : at + step] = out[tokens // 2 :]


def branch(parts, probs, weight, after):
    width, cols = weight.shape
    tokens = probs.shape[2]
    half = ((tokens // 2, width), BF16)
    outs = [half, half, ((cols, tokens), BF16)]
    kernel = functools.partial(branch_kernel, len(parts))
    flops = 2 * tokens * cols * width
    return run(kernel, outs, [*parts, probs, weight], after, flops, 2 * weight.size)


def pair_kernel(rows, keep_ref, got_ref, mine_ref, *away_refs):
    out = keep_ref[...].astype(F32) + got_ref[...].astype(F32)
    mine_ref[...] = out[:rows]
    for b, ref in enumerate(away_refs):
        ref[...] = out[(b + 1) * rows : (b + 2) * rows].astype(BF16)


def pair_sum(keep, got, rows, after):
    total, width = keep.shape
    outs = [((rows, width), F32)] + [((rows, width), BF16)] * (total // rows - 1)
    kernel = functools.partial(pair_kernel, rows)
    return run(kernel, outs, [keep, got], after, keep.size, 6 * keep.size)


def fresh_kernel(*refs):
    mine_ref, upper_ref, out_ref = refs[0], refs[-2], refs[-1]
    total = mine_ref[...]
    for ref in refs[1:-2]:
        total = total + ref[...].astype(F32)
    rows = mine_ref.shape[0]
    out_ref[...] = (total + upper_ref[:rows, :].astype(F32)).astype(BF16)


def fresh_rows(mine, heard, upper, after):
    operands = [mine, *heard, upper]
    outs = [(mine.shape, BF16)]
    return run(fresh_kernel, outs, operands, after, mine.size, 6 * mine.size)[0]


def hold_kernel(src_ref, out_ref, sems):
    parts = sems.shape[0]
    rows = src_ref.shape[0] // parts
    copies = [
        pltpu.make_async_copy(
            src_ref.at[pl.ds(i * rows, rows), :], out_ref.at[pl.ds(i * rows, rows), :], sems.at[i]
        )
        for i in range(parts)
    ]
    for copy in copies:
        copy.start()
    for copy in copies:
        copy.wait()


def held(array):
    return pl.pallas_call(
        hold_kernel,
        out_shape=jax.ShapeDtypeStruct(array.shape, array.dtype),
        in_specs=[pl.BlockSpec(memory_space=pltpu.HBM)],
        out_specs=vmem(),
        scratch_shapes=[pltpu.SemaphoreType.DMA((4,))],
        compiler_params=params(4),
        cost_estimate=cost(array.size, 2 * array.size),
        name="held",
    )(pltpu.with_memory_space_constraint(array, pltpu.HBM))


def stream_product(lhs_of, rhs, out_ref, buf, sems):
    count = sems.shape[0]
    step = buf.shape[0] // count

    def copy(i):
        rows = pl.ds(pl.multiple_of(i * step, step), step)
        return pltpu.make_async_copy(buf.at[rows, :], out_ref.at[rows, :], sems.at[i])

    @pl.loop(0, count, unroll=2)
    def _(i):
        rows = pl.ds(pl.multiple_of(i * step, step), step)
        product = jnp.dot(lhs_of(rows).T, rhs, preferred_element_type=F32)
        buf[rows, :] = product.astype(BF16)
        copy(i).start()

    @pl.loop(0, count)
    def _(i):
        copy(i).wait()


def out_grad_kernel(tensors, ctx_ref, *refs):
    uppers, (out_ref, buf, sems, rhs) = refs[:-4], refs[-4:]
    tokens = uppers[0].shape[0]
    rows = tokens // tensors
    for m, ref in enumerate(uppers):
        for b, block in enumerate(token_order(tensors)):
            at = pl.multiple_of(m * tokens + block * rows, rows)
            rhs[pl.ds(at, rows), :] = ref[b * rows : (b + 1) * rows, :]
    stream_product(lambda at: ctx_ref[:, at], rhs[...], out_ref, buf, sems)


def value_grad_kernel(micro, *refs):
    blocks, grads = refs[: -micro - 4], refs[-micro - 4 : -4]
    out_ref, buf, sems, rhs = refs[-4:]
    tokens = grads[0].shape[1]
    for m, ref in enumerate(grads):
        rhs[m * tokens : (m + 1) * tokens, :] = ref[...].T

    def lhs_of(at):
        return jnp.concatenate([b[m, :, at] for m in range(micro) for b in blocks], axis=0)

    stream_product(lhs_of, rhs[...], out_ref, buf, sems)


def weight_grad(kernel, operands, shape, tokens):
    rows, cols = shape
    step = min(rows, 256)
    return pl.pallas_call(
        kernel,
        out_shape=jax.ShapeDtypeStruct(shape, BF16),
        in_specs=[vmem()] * len(operands),
        out_specs=pl.BlockSpec(memory_space=pltpu.HBM),
        scratch_shapes=[
            pltpu.VMEM(shape, BF16),
            pltpu.SemaphoreType.DMA((rows // step,)),
            pltpu.VMEM((tokens, cols), BF16),
        ],
        compiler_params=params(20),
        cost_estimate=cost(2 * tokens * rows * cols, 2 * rows * cols),
    )(*operands)


def per_device(cotangent, inputs, queries, keys, context, value_weight, out_weight):
    sections = lax.axis_size("section")
    tensors = lax.axis_size("tensor")
    replicas = lax.axis_size("dp")
    micro, rows, width = cotangent.shape
    seq, cols = queries.shape[2:]
    value_proj = value_weight[0]
    turns = range(0, tensors, 2)

    def both_cores(near):
        return [*near, *(across(n, "tensor", 1) for n in near)]

    def gathered(block):
        near = [block] + [across(block, "tensor", f) for f in turns[1:]]
        return both_cores(near)

    first = []
    for m in range(micro):
        first.append(gathered(cotangent[m]))
    probs = attention_probs(queries[0], keys[0], tensors)
    out_proj = held(out_weight[0])
    parts, uppers, grads, fresh = [None] * micro, [None] * micro, [None] * micro, [None] * micro
    last = list(probs[:1])
    for m in range(micro):
        parts[m], uppers[m] = ctx_call(first_kernel, first[m], seq, out_proj, last)
        last = [parts[m]]
    in_blocks = gathered(inputs[0])
    for stage in range(sections):
        giver = sections - 1 - stage
        mine, away = [None] * micro, [None] * micro
        for m in range(micro + 1):
            if m < micro:
                heard = [across(parts[m], "dp", d) for d in range(1, replicas)]
                keep, send, grads[m] = branch(
                    [parts[m], *heard], probs[m], value_proj, last
                )
                last = [send]
            if m > 0:
                heard = [across(a, "tensor", f) for a, f in zip(away[m - 1], turns[1:])]
                fresh[m - 1] = fresh_rows(mine[m - 1], heard, uppers[m - 1], last)
                last = [fresh[m - 1]]
            if m < micro:
                mine[m], *away[m] = pair_sum(keep, across(send, "tensor", 1), rows, last)
                last = [mine[m]]
        if stage == sections - 1:
            break
        for m in range(micro):
            blocks = both_cores([below(fresh[m], giver, f) for f in turns])
            kernel = functools.partial(next_kernel, rows, giver - 1)
            parts[m], uppers[m] = ctx_call(kernel, [*blocks, uppers[m]], seq, out_proj, last)
            last = [parts[m]]
    out_w = weight_grad(
        functools.partial(out_grad_kernel, tensors),
        [context[0].reshape(micro * seq, cols), *uppers],
        (cols, width),
        micro * seq,
    )
    value_w = weight_grad(
        functools.partial(value_grad_kernel, micro),
        [*in_blocks, *grads],
        (width, cols),
        micro * seq,
    )
    return (jnp.stack(fresh)[None], value_w[None], out_w[None])


def solution(mesh):
    placed = (
        P(None, "tensor", "dp"),
        P("section", None, "tensor", "dp"),
        P("section", None, None, "tensor"),
        P("section", None, None, "tensor"),
        P("section", None, None, "tensor"),
        P("section", "dp", "tensor"),
        P("section", "tensor", "dp"),
    )
    return jax.shard_map(
        per_device,
        mesh=mesh,
        in_specs=placed,
        out_specs=(
            P("section", None, "tensor", "dp"),
            P("section", "dp", "tensor"),
            P("section", "tensor", "dp"),
        ),
        check_vma=False,
    )
```

time: 418 us -> 166 us (0.40)
  matrix products: 185 us -> 0 us
  blocking collectives: 117 us -> 0 us
  Pallas kernels: 0 us -> 58.9 us
  starting transfers between devices: 6.65 us -> 48.1 us
  other arithmetic: 25.6 us -> 0.7 us
  between operations: 13.7 us -> 1.02 us
  waiting for transfers between devices: 61.8 us -> 56 us
  local copies, waits for them, and re-layouts: 6.42 us -> 0.99 us
    dot_general x25 -> x0, matrix products: 184 us -> none  [the longest x5 57 us: tick(): lax.dot_general(context_here, grad_cols, (((0,), (0,)), ((), ())), prefer...]
    psum x5 -> x0, blocking collectives: 75.8 us -> none  [tick(): ctx_grad = lax.psum(ctx_part, 'dp').astype(jnp.bfloat16)]
    reduce_scatter x5 -> x0, waiting for transfers between devices: 61.7 us -> none  [tick(): summed = lax.psum_scatter(branch, 'tensor', scatter_dimension=0, tiled=True)]
    pallas_call x0 -> x36, Pallas kernels: none -> 58.9 us  [the longest x33 45.8 us: run(): pl.pallas_call(body, out_shape=[jax.ShapeDtypeStruct(*out) for out in out...]
    ppermute x5 -> x57, waiting for transfers between devices: 0.01 us -> 56 us  [the longest x45 45.7 us: across(): return lax.ppermute(array, axis, [(i, i ^ flip) for i in range(count)])]
    ppermute x5 -> x57, starting transfers between devices: 6.46 us -> 48.1 us  [the longest x45 30.4 us: across(): return lax.ppermute(array, axis, [(i, i ^ flip) for i in range(count)])]
    all_gather x6 -> x0, blocking collectives: 41.4 us -> none  [the longest x5 31.1 us: tick(): grad_cols = lax.all_gather(incoming, 'tensor', axis=0, tiled=True)]
    broadcast_in_dim x2 -> x1, other arithmetic: 16.1 us -> 0.7 us  [per_device(): return (jnp.stack(fresh)[None], value_w[None], out_w[None])]
  transfers between devices with their start and end apart: 10 -> 57, of which waited for: 5 -> 29; matrix products, arithmetic and copies ran while one was open for 27% -> 0% of each run, Pallas kernels for 0% -> 23%
where the time goes in v2:
time: 166 us
  Pallas kernels  58.9 us (35%)
  waiting for transfers between devices  56 us (34%)
  starting transfers between devices  48.1 us (29%)
    pallas_call x33, Pallas kernels, run(): pl.pallas_call(body, out_shape=[jax.ShapeDtypeStruct(*out) for out in out...  45.8 us
    ppermute x45, waiting for transfers between devices, across(): return lax.ppermute(array, axis, [(i, i ^ flip) for i in range(count)])  45.7 us
    ppermute x45, starting transfers between devices, across(): return lax.ppermute(array, axis, [(i, i ^ flip) for i in range(count)])  30.4 us
    ppermute x12, starting transfers between devices, below(): return lax.ppermute(array, ('section', 'tensor'), pairs)  17.7 us
    ppermute x12, waiting for transfers between devices, below(): return lax.ppermute(array, ('section', 'tensor'), pairs)  10.3 us
    pallas_call x2, Pallas kernels, weight_grad(): pl.pallas_call(kernel, out_shape=jax.ShapeDtypeStruct(shape, BF16), in_sp...  9.27 us
    pallas_call x1, Pallas kernels, held(): pl.pallas_call(hold_kernel, out_shape=jax.ShapeDtypeStruct(array.shape, a...  3.86 us
  transfers between devices with their start and end apart: 57, of which 29 were waited for; matrix products, arithmetic and copies ran while one was open for 0% of the time, Pallas kernels for 23%

profile of v2, /device:TPU:0, one launch (start us, length us, event | category | flops | bytes accessed | tf_op | source)
XLA Modules:
  0.0 165.7 jit_solution(5137504259192705710)
XLA Ops:
  1.6 3.1 %collective-permute-start = (bf16[16,3072]{1,0:T(8,128)(2,1)S(1)}, bf16[16,3072]{1,0:T(8,128)(2,1)S(1)}, u32[]{:S(2)}, u32[]{:S(2)}) collective-permute-start(bf16[16,3072]{1,0:T(8,128)(2,1)S(1)} %get-tuple-element.107.refs_0_), channel_id=1, source_target_pairs={{0,2},{1,3},{2,0},{3,1},{4,6},{5,7},{6,4},{7,5},{8,10},{9,11},{10,... | collective-permute-start | bytes 294920 | tf_op jit(solution)/shard_map/ppermute | solution.py:47
  4.7 2.8 %collective-permute-done.refs_1_ = bf16[16,3072]{1,0:T(8,128)(2,1)S(1)} collective-permute-done((bf16[16,3072]{1,0:T(8,128)(2,1)S(1)}, bf16[16,3072]{1,0:T(8,128)(2,1)S(1)}, u32[]{:S(2)}, u32[]{:S(2)}) %collective-permute-start) | collective-permute-done | bytes 98336 | tf_op jit(solution)/shard_map/ppermute | solution.py:47
  9.3 3.9 %held.1.refs_4_.refs_5_ = bf16[1536,3072]{1,0:T(8,128)(2,1)S(1)} custom-call(bf16[1536,3072]{1,0:T(8,128)(2,1)} %bitcast.34), custom_call_target="tpu_custom_call" | custom-call | flops 4718592 | bytes 9437184 | tf_op jit(solution)/shard_map/held/pallas_call | solution.py:225
  23.7 2.9 %shard_map.97 = (bf16[32,3072]{1,0:T(8,128)(2,1)S(1)}, bf16[32,3072]{1,0:T(8,128)(2,1)S(1)}, bf16[1536,64]{1,0:T(8,128)(2,1)}) custom-call(bf16[768,128]{1,0:T(8,128)(2,1)S(1)} %get-tuple-element.56.refs_5_.refs_0_, bf16[768,128]{1,0:T(8,128)(2,1)S(1)} %collective-permute-done.3.refs_1_, bf16[12,128,64]{2,1,0:T(8,128)(2,1)S(1)} %get-tuple-element.55.refs_5_.refs_2_, ...), custom_call_target="tpu_custom_call" | custom-call | flops 603979776 | bytes 9437184 | tf_op jit(solution)/shard_map/pallas_call | solution.py:35
  28.2 5.7 %collective-permute-done.9.refs_1_ = bf16[768,128]{1,0:T(8,128)(2,1)S(1)} collective-permute-done((bf16[768,128]{1,0:T(8,128)(2,1)S(1)}, bf16[768,128]{1,0:T(8,128)(2,1)S(1)}, u32[]{:S(2)}, u32[]{:S(2)}) %collective-permute-start.9) | collective-permute-done | bytes 196640 | tf_op jit(solution)/shard_map/ppermute | solution.py:47
  33.9 2.9 %shard_map.99 = (bf16[32,3072]{1,0:T(8,128)(2,1)S(1)}, bf16[32,3072]{1,0:T(8,128)(2,1)S(1)}, bf16[1536,64]{1,0:T(8,128)(2,1)}) custom-call(bf16[768,128]{1,0:T(8,128)(2,1)S(1)} %get-tuple-element.57.refs_4_.refs_0_, bf16[768,128]{1,0:T(8,128)(2,1)S(1)} %collective-permute-done.9.refs_1_, bf16[12,128,64]{2,1,0:T(8,128)(2,1)S(1)} %get-tuple-element.63.refs_2_, ...), custom_call_target="tpu_custom_call" | custom-call | flops 603979776 | bytes 9437184 | tf_op jit(solution)/shard_map/pallas_call | solution.py:35
  37.2 4.8 %collective-permute-done.8.refs_1_ = bf16[16,3072]{1,0:T(8,128)(2,1)S(1)} collective-permute-done((bf16[16,3072]{1,0:T(8,128)(2,1)S(1)}, bf16[16,3072]{1,0:T(8,128)(2,1)S(1)}, u32[]{:S(2)}, u32[]{:S(2)}) %collective-permute-start.8) | collective-permute-done | bytes 98336 | tf_op jit(solution)/shard_map/ppermute | solution.py:47
  45.8 2.9 %collective-permute-done.11.refs_1_ = bf16[16,3072]{1,0:T(8,128)(2,1)S(1)} collective-permute-done((bf16[16,3072]{1,0:T(8,128)(2,1)S(1)}, bf16[16,3072]{1,0:T(8,128)(2,1)S(1)}, u32[]{:S(2)}, u32[]{:S(2)}) %collective-permute-start.11) | collective-permute-done | bytes 98336 | tf_op jit(solution)/shard_map/ppermute | solution.py:59
  58.4 2.8 %shard_map.104 = (bf16[768,128]{1,0:T(8,128)(2,1)S(1)}, bf16[64,3072]{1,0:T(8,128)(2,1)S(1)}) custom-call(bf16[16,3072]{1,0:T(8,128)(2,1)S(1)} %collective-permute-done.17.refs_0_, bf16[16,3072]{1,0:T(8,128)(2,1)S(1)} %collective-permute-done.18.refs_1_, bf16[16,3072]{1,0:T(8,128)(2,1)S(1)} %collective-permute-done.19.refs_2_, ...), custom_call_target="tpu_custom_call" | custom-call | flops 603979776 | bytes 9437184 | tf_op jit(solution)/shard_map/pallas_call | solution.py:35
  61.3 2.8 %shard_map.105 = (bf16[32,3072]{1,0:T(8,128)(2,1)S(1)}, bf16[32,3072]{1,0:T(8,128)(2,1)S(1)}, bf16[1536,64]{1,0:T(8,128)(2,1)}) custom-call(bf16[768,128]{1,0:T(8,128)(2,1)S(1)} %get-tuple-element.69.refs_6_.refs_0_, bf16[768,128]{1,0:T(8,128)(2,1)S(1)} %collective-permute-done.16.refs_1_, bf16[12,128,64]{2,1,0:T(8,128)(2,1)S(1)} %get-tuple-element.55.refs_5_.refs_2_, ...), custom_call_target="tpu_custom_call" | custom-call | flops 603979776 | bytes 9437184 | tf_op jit(solution)/shard_map/pallas_call | solution.py:35
  65.9 5.7 %collective-permute-done.23.refs_1_ = bf16[768,128]{1,0:T(8,128)(2,1)S(1)} collective-permute-done((bf16[768,128]{1,0:T(8,128)(2,1)S(1)}, bf16[768,128]{1,0:T(8,128)(2,1)S(1)}, u32[]{:S(2)}, u32[]{:S(2)}) %collective-permute-start.23) | collective-permute-done | bytes 196640 | tf_op jit(solution)/shard_map/ppermute | solution.py:47
  71.5 2.9 %shard_map.107 = (bf16[32,3072]{1,0:T(8,128)(2,1)S(1)}, bf16[32,3072]{1,0:T(8,128)(2,1)S(1)}, bf16[1536,64]{1,0:T(8,128)(2,1)}) custom-call(bf16[768,128]{1,0:T(8,128)(2,1)S(1)} %get-tuple-element.70.refs_4_.refs_0_, bf16[768,128]{1,0:T(8,128)(2,1)S(1)} %collective-permute-done.23.refs_1_, bf16[12,128,64]{2,1,0:T(8,128)(2,1)S(1)} %get-tuple-element.63.refs_2_, ...), custom_call_target="tpu_custom_call" | custom-call | flops 603979776 | bytes 9437184 | tf_op jit(solution)/shard_map/pallas_call | solution.py:35
  75.0 4.7 %collective-permute-done.22.refs_1_ = bf16[16,3072]{1,0:T(8,128)(2,1)S(1)} collective-permute-done((bf16[16,3072]{1,0:T(8,128)(2,1)S(1)}, bf16[16,3072]{1,0:T(8,128)(2,1)S(1)}, u32[]{:S(2)}, u32[]{:S(2)}) %collective-permute-start.22) | collective-permute-done | bytes 98336 | tf_op jit(solution)/shard_map/ppermute | solution.py:47
  96.4 2.8 %shard_map.113 = (bf16[32,3072]{1,0:T(8,128)(2,1)S(1)}, bf16[32,3072]{1,0:T(8,128)(2,1)S(1)}, bf16[1536,64]{1,0:T(8,128)(2,1)}) custom-call(bf16[768,128]{1,0:T(8,128)(2,1)S(1)} %get-tuple-element.81.refs_6_.refs_0_, bf16[768,128]{1,0:T(8,128)(2,1)S(1)} %collective-permute-done.30.refs_1_, bf16[12,128,64]{2,1,0:T(8,128)(2,1)S(1)} %get-tuple-element.55.refs_5_.refs_2_, ...), custom_call_target="tpu_custom_call" | custom-call | flops 603979776 | bytes 9437184 | tf_op jit(solution)/shard_map/pallas_call | solution.py:35
  101.0 5.7 %collective-permute-done.37.refs_1_ = bf16[768,128]{1,0:T(8,128)(2,1)S(1)} collective-permute-done((bf16[768,128]{1,0:T(8,128)(2,1)S(1)}, bf16[768,128]{1,0:T(8,128)(2,1)S(1)}, u32[]{:S(2)}, u32[]{:S(2)}) %collective-permute-start.37) | collective-permute-done | bytes 196640 | tf_op jit(solution)/shard_map/ppermute | solution.py:47
  106.7 2.9 %shard_map.115 = (bf16[32,3072]{1,0:T(8,128)(2,1)S(1)}, bf16[32,3072]{1,0:T(8,128)(2,1)S(1)}, bf16[1536,64]{1,0:T(8,128)(2,1)}) custom-call(bf16[768,128]{1,0:T(8,128)(2,1)S(1)} %get-tuple-element.82.refs_4_.refs_0_, bf16[768,128]{1,0:T(8,128)(2,1)S(1)} %collective-permute-done.37.refs_1_, bf16[12,128,64]{2,1,0:T(8,128)(2,1)S(1)} %get-tuple-element.63.refs_2_, ...), custom_call_target="tpu_custom_call" | custom-call | flops 603979776 | bytes 9437184 | tf_op jit(solution)/shard_map/pallas_call | solution.py:35
  110.9 3.9 %collective-permute-done.36.refs_1_ = bf16[16,3072]{1,0:T(8,128)(2,1)S(1)} collective-permute-done((bf16[16,3072]{1,0:T(8,128)(2,1)S(1)}, bf16[16,3072]{1,0:T(8,128)(2,1)S(1)}, u32[]{:S(2)}, u32[]{:S(2)}) %collective-permute-start.36) | collective-permute-done | bytes 98336 | tf_op jit(solution)/shard_map/ppermute | solution.py:47
  114.9 7.4 %collective-permute-start.39 = (bf16[16,3072]{1,0:T(8,128)(2,1)S(1)}, bf16[16,3072]{1,0:T(8,128)(2,1)S(1)}, u32[]{:S(2)}, u32[]{:S(2)}) collective-permute-start(bf16[16,3072]{1,0:T(8,128)(2,1)S(1)} %shard_map.116.refs_2_), channel_id=1, source_target_pairs={{0,6},{1,7},{2,4},{3,5},{4,2},{5,3},{6,0},{7,1},{8,14},{9,15},{10,... | collective-permute-start | bytes 294920 | tf_op jit(solution)/shard_map/ppermute | solution.py:59
  127.2 2.9 %collective-permute-start.46 = (bf16[16,3072]{1,0:T(8,128)(2,1)S(1)}, bf16[16,3072]{1,0:T(8,128)(2,1)S(1)}, u32[]{:S(2)}, u32[]{:S(2)}) collective-permute-start(bf16[16,3072]{1,0:T(8,128)(2,1)S(1)} %shard_map.118.refs_6_), channel_id=1, source_target_pairs={{0,6},{1,7},{2,4},{3,5},{4,2},{5,3},{6,0},{7,1},{8,14},{9,15},{10,... | collective-permute-start | bytes 294920 | tf_op jit(solution)/shard_map/ppermute | solution.py:59
  139.5 3.1 %shard_map.121 = (bf16[32,3072]{1,0:T(8,128)(2,1)S(1)}, bf16[32,3072]{1,0:T(8,128)(2,1)S(1)}, bf16[1536,64]{1,0:T(8,128)(2,1)S(1)}) custom-call(bf16[768,128]{1,0:T(8,128)(2,1)S(1)} %get-tuple-element.93.refs_6_.refs_0_, bf16[768,128]{1,0:T(8,128)(2,1)S(1)} %collective-permute-done.44.refs_1_, bf16[12,128,64]{2,1,0:T(8,128)(2,1)S(1)} %get-tuple-element.55.refs_5_.refs_2_, ...), custom_call_target="tpu_custom_call" | custom-call | flops 603979776 | bytes 9437184 | tf_op jit(solution)/shard_map/pallas_call | solution.py:35
  144.9 5.0 %collective-permute-done.51.refs_1_ = bf16[768,128]{1,0:T(8,128)(2,1)S(1)} collective-permute-done((bf16[768,128]{1,0:T(8,128)(2,1)S(1)}, bf16[768,128]{1,0:T(8,128)(2,1)S(1)}, u32[]{:S(2)}, u32[]{:S(2)}) %collective-permute-start.51) | collective-permute-done | bytes 196640 | tf_op jit(solution)/shard_map/ppermute | solution.py:47
  150.0 2.8 %shard_map.123 = (bf16[32,3072]{1,0:T(8,128)(2,1)S(1)}, bf16[32,3072]{1,0:T(8,128)(2,1)S(1)}, bf16[1536,64]{1,0:T(8,128)(2,1)S(1)}) custom-call(bf16[768,128]{1,0:T(8,128)(2,1)S(1)} %get-tuple-element.94.refs_4_.refs_0_, bf16[768,128]{1,0:T(8,128)(2,1)S(1)} %collective-permute-done.51.refs_1_, bf16[12,128,64]{2,1,0:T(8,128)(2,1)S(1)} %get-tuple-element.63.refs_2_, ...), custom_call_target="tpu_custom_call" | custom-call | flops 603979776 | bytes 9437184 | tf_op jit(solution)/shard_map/pallas_call | solution.py:35
  154.1 4.4 %shard_map.128 = bf16[1536,3072]{1,0:T(8,128)(2,1)} custom-call(bf16[128,1536]{1,0:T(8,128)(2,1)S(1)} %bitcast.30, bf16[64,3072]{1,0:T(8,128)(2,1)S(1)} %get-tuple-element.99.refs_2_.refs_0_, bf16[64,3072]{1,0:T(8,128)(2,1)S(1)} %get-tuple-element.104.refs_2_.refs_1_), custom_call_target="tpu_custom_call" | custom-call | flops 1207959552 | bytes 9437184 | tf_op jit(solution)/shard_map/pallas_call | solution.py:284
  160.1 4.8 %shard_map.127 = bf16[3072,1536]{1,0:T(8,128)(2,1)} custom-call(bf16[2,16,3072]{2,1,0:T(8,128)(2,1)S(1)} %bitcast.33, bf16[2,16,3072]{2,1,0:T(8,128)(2,1)S(1)} %collective-permute-done.54.refs_1_, bf16[2,16,3072]{2,1,0:T(8,128)(2,1)S(1)} %collective-permute-done.55.refs_2_, bf16[2,16,3072]{2,1,0:T(8,128)(2,1)S(1)} %collective-permute-done.56.refs_3_, ...), custom_call_target="tpu_custom_call" | custom-call | flops 1207959552 | bytes 9437184 | tf_op jit(solution)/shard_map/pallas_call | solution.py:284
  (143 shorter events, 71.1 us)
Async XLA Ops:
  1.6 5.9 %collective-permute-start = (bf16[16,3072]{1,0:T(8,128)(2,1)S(1)}, bf16[16,3072]{1,0:T(8,128)(2,1)S(1)}, u32[]{:S(2)}, u32[]{:S(2)}) collective-permute-start(bf16[16,3072]{1,0:T(8,128)(2,1)S(1)} %get-tuple-element.107.refs_0_), channel_id=1, source_target_pairs={{0,2},{1,3},{2,0},{3,1},{4,6},{5,7},{6,4},{7,5},{8,10},{9,11},{10,... | collective-permute-start | bytes 294920 | tf_op jit(solution)/shard_map/ppermute | solution.py:47
  4.6 9.2 %collective-permute-start.1 = (bf16[16,3072]{1,0:T(8,128)(2,1)S(1)}, bf16[16,3072]{1,0:T(8,128)(2,1)S(1)}, u32[]{:S(2)}, u32[]{:S(2)}) collective-permute-start(bf16[16,3072]{1,0:T(8,128)(2,1)S(1)} %get-tuple-element.107.refs_0_), channel_id=1, source_target_pairs={{0,1},{1,0},{2,3},{3,2},{4,5},{5,4},{6,7},{7,6},{8,9},{9,8},{10,11... | collective-permute-start | bytes 294920 | tf_op jit(solution)/shard_map/ppermute | solution.py:47
  7.4 6.4 %collective-permute-start.2 = (bf16[16,3072]{1,0:T(8,128)(2,1)S(1)}, bf16[16,3072]{1,0:T(8,128)(2,1)S(1)}, u32[]{:S(2)}, u32[]{:S(2)}) collective-permute-start(bf16[16,3072]{1,0:T(8,128)(2,1)S(1)} %collective-permute-done.refs_1_), channel_id=1, source_target_pairs={{0,1},{1,0},{2,3},{3,2},{4,5},{5,4},{6,7},{7,6},{8,9},{9,8},{10,11... | collective-permute-start | bytes 294920 | tf_op jit(solution)/shard_map/ppermute | solution.py:47
  7.4 10.7 %collective-permute-start.4 = (bf16[16,3072]{1,0:T(8,128)(2,1)S(1)}, bf16[16,3072]{1,0:T(8,128)(2,1)S(1)}, u32[]{:S(2)}, u32[]{:S(2)}) collective-permute-start(bf16[16,3072]{1,0:T(8,128)(2,1)S(1)} %get-tuple-element.108.refs_0_), channel_id=1, source_target_pairs={{0,2},{1,3},{2,0},{3,1},{4,6},{5,7},{6,4},{7,5},{8,10},{9,11},{10,... | collective-permute-start | bytes 294920 | tf_op jit(solution)/shard_map/ppermute | solution.py:47
  16.6 7.1 %collective-permute-start.3 = (bf16[768,128]{1,0:T(8,128)(2,1)S(1)}, bf16[768,128]{1,0:T(8,128)(2,1)S(1)}, u32[]{:S(2)}, u32[]{:S(2)}) collective-permute-start(bf16[768,128]{1,0:T(8,128)(2,1)S(1)} %get-tuple-element.56.refs_5_.refs_0_), channel_id=1, source_target_pairs={{0,16},{16,0},{1,17},{17,1},{2,18},{18,2},{3,19},{19,3},{4,20},{20... | collective-permute-start | bytes 589832 | tf_op jit(solution)/shard_map/ppermute | solution.py:47
  26.6 7.3 %collective-permute-start.9 = (bf16[768,128]{1,0:T(8,128)(2,1)S(1)}, bf16[768,128]{1,0:T(8,128)(2,1)S(1)}, u32[]{:S(2)}, u32[]{:S(2)}) collective-permute-start(bf16[768,128]{1,0:T(8,128)(2,1)S(1)} %get-tuple-element.57.refs_4_.refs_0_), channel_id=1, source_target_pairs={{0,16},{16,0},{1,17},{17,1},{2,18},{18,2},{3,19},{19,3},{4,20},{20... | collective-permute-start | bytes 589832 | tf_op jit(solution)/shard_map/ppermute | solution.py:47
  36.8 7.1 %collective-permute-start.14 = (bf16[32,3072]{1,0:T(8,128)(2,1)S(1)}, bf16[32,3072]{1,0:T(8,128)(2,1)S(1)}, u32[]{:S(2)}, u32[]{:S(2)}) collective-permute-start(bf16[32,3072]{1,0:T(8,128)(2,1)S(1)} %get-tuple-element.64.refs_3_), channel_id=1, source_target_pairs={{0,1},{1,0},{2,3},{3,2},{4,5},{5,4},{6,7},{7,6},{8,9},{9,8},{10,11... | collective-permute-start | bytes 589832 | tf_op jit(solution)/shard_map/ppermute | solution.py:47
  42.1 6.5 %collective-permute-start.11 = (bf16[16,3072]{1,0:T(8,128)(2,1)S(1)}, bf16[16,3072]{1,0:T(8,128)(2,1)S(1)}, u32[]{:S(2)}, u32[]{:S(2)}) collective-permute-start(bf16[16,3072]{1,0:T(8,128)(2,1)S(1)} %shard_map.100.refs_2_), channel_id=1, source_target_pairs={{0,6},{1,7},{2,4},{3,5},{4,2},{5,3},{6,0},{7,1},{8,14},{9,15},{10,... | collective-permute-start | bytes 294920 | tf_op jit(solution)/shard_map/ppermute | solution.py:59
  49.5 6.7 %collective-permute-start.18 = (bf16[16,3072]{1,0:T(8,128)(2,1)S(1)}, bf16[16,3072]{1,0:T(8,128)(2,1)S(1)}, u32[]{:S(2)}, u32[]{:S(2)}) collective-permute-start(bf16[16,3072]{1,0:T(8,128)(2,1)S(1)} %shard_map.102.refs_6_), channel_id=1, source_target_pairs={{0,6},{1,7},{2,4},{3,5},{4,2},{5,3},{6,0},{7,1},{8,14},{9,15},{10,... | collective-permute-start | bytes 294920 | tf_op jit(solution)/shard_map/ppermute | solution.py:59
  54.6 6.7 %collective-permute-start.16 = (bf16[768,128]{1,0:T(8,128)(2,1)S(1)}, bf16[768,128]{1,0:T(8,128)(2,1)S(1)}, u32[]{:S(2)}, u32[]{:S(2)}) collective-permute-start(bf16[768,128]{1,0:T(8,128)(2,1)S(1)} %get-tuple-element.69.refs_6_.refs_0_), channel_id=1, source_target_pairs={{0,16},{16,0},{1,17},{17,1},{2,18},{18,2},{3,19},{19,3},{4,20},{20... | collective-permute-start | bytes 589832 | tf_op jit(solution)/shard_map/ppermute | solution.py:47
  64.3 7.2 %collective-permute-start.23 = (bf16[768,128]{1,0:T(8,128)(2,1)S(1)}, bf16[768,128]{1,0:T(8,128)(2,1)S(1)}, u32[]{:S(2)}, u32[]{:S(2)}) collective-permute-start(bf16[768,128]{1,0:T(8,128)(2,1)S(1)} %get-tuple-element.70.refs_4_.refs_0_), channel_id=1, source_target_pairs={{0,16},{16,0},{1,17},{17,1},{2,18},{18,2},{3,19},{19,3},{4,20},{20... | collective-permute-start | bytes 589832 | tf_op jit(solution)/shard_map/ppermute | solution.py:47
  74.4 6.5 %collective-permute-start.28 = (bf16[32,3072]{1,0:T(8,128)(2,1)S(1)}, bf16[32,3072]{1,0:T(8,128)(2,1)S(1)}, u32[]{:S(2)}, u32[]{:S(2)}) collective-permute-start(bf16[32,3072]{1,0:T(8,128)(2,1)S(1)} %get-tuple-element.76.refs_3_), channel_id=1, source_target_pairs={{0,1},{1,0},{2,3},{3,2},{4,5},{5,4},{6,7},{7,6},{8,9},{9,8},{10,11... | collective-permute-start | bytes 589832 | tf_op jit(solution)/shard_map/ppermute | solution.py:47
  86.2 6.0 %collective-permute-start.32 = (bf16[16,3072]{1,0:T(8,128)(2,1)S(1)}, bf16[16,3072]{1,0:T(8,128)(2,1)S(1)}, u32[]{:S(2)}, u32[]{:S(2)}) collective-permute-start(bf16[16,3072]{1,0:T(8,128)(2,1)S(1)} %shard_map.110.refs_6_), channel_id=1, source_target_pairs={{0,2},{1,3},{2,0},{3,1},{4,10},{5,11},{6,8},{7,9},{8,6},{9,7},{10,... | collective-permute-start | bytes 294920 | tf_op jit(solution)/shard_map/ppermute | solution.py:59
  99.6 7.1 %collective-permute-start.37 = (bf16[768,128]{1,0:T(8,128)(2,1)S(1)}, bf16[768,128]{1,0:T(8,128)(2,1)S(1)}, u32[]{:S(2)}, u32[]{:S(2)}) collective-permute-start(bf16[768,128]{1,0:T(8,128)(2,1)S(1)} %get-tuple-element.82.refs_4_.refs_0_), channel_id=1, source_target_pairs={{0,16},{16,0},{1,17},{17,1},{2,18},{18,2},{3,19},{19,3},{4,20},{20... | collective-permute-start | bytes 589832 | tf_op jit(solution)/shard_map/ppermute | solution.py:47
  109.5 12.9 %collective-permute-start.42 = (bf16[32,3072]{1,0:T(8,128)(2,1)S(1)}, bf16[32,3072]{1,0:T(8,128)(2,1)S(1)}, u32[]{:S(2)}, u32[]{:S(2)}) collective-permute-start(bf16[32,3072]{1,0:T(8,128)(2,1)S(1)} %get-tuple-element.88.refs_3_), channel_id=1, source_target_pairs={{0,1},{1,0},{2,3},{3,2},{4,5},{5,4},{6,7},{7,6},{8,9},{9,8},{10,11... | collective-permute-start | bytes 589832 | tf_op jit(solution)/shard_map/ppermute | solution.py:47
  114.9 10.3 %collective-permute-start.39 = (bf16[16,3072]{1,0:T(8,128)(2,1)S(1)}, bf16[16,3072]{1,0:T(8,128)(2,1)S(1)}, u32[]{:S(2)}, u32[]{:S(2)}) collective-permute-start(bf16[16,3072]{1,0:T(8,128)(2,1)S(1)} %shard_map.116.refs_2_), channel_id=1, source_target_pairs={{0,6},{1,7},{2,4},{3,5},{4,2},{5,3},{6,0},{7,1},{8,14},{9,15},{10,... | collective-permute-start | bytes 294920 | tf_op jit(solution)/shard_map/ppermute | solution.py:59
  127.2 7.2 %collective-permute-start.46 = (bf16[16,3072]{1,0:T(8,128)(2,1)S(1)}, bf16[16,3072]{1,0:T(8,128)(2,1)S(1)}, u32[]{:S(2)}, u32[]{:S(2)}) collective-permute-start(bf16[16,3072]{1,0:T(8,128)(2,1)S(1)} %shard_map.118.refs_6_), channel_id=1, source_target_pairs={{0,6},{1,7},{2,4},{3,5},{4,2},{5,3},{6,0},{7,1},{8,14},{9,15},{10,... | collective-permute-start | bytes 294920 | tf_op jit(solution)/shard_map/ppermute | solution.py:59
  132.8 6.7 %collective-permute-start.44 = (bf16[768,128]{1,0:T(8,128)(2,1)S(1)}, bf16[768,128]{1,0:T(8,128)(2,1)S(1)}, u32[]{:S(2)}, u32[]{:S(2)}) collective-permute-start(bf16[768,128]{1,0:T(8,128)(2,1)S(1)} %get-tuple-element.93.refs_6_.refs_0_), channel_id=1, source_target_pairs={{0,16},{16,0},{1,17},{17,1},{2,18},{18,2},{3,19},{19,3},{4,20},{20... | collective-permute-start | bytes 589832 | tf_op jit(solution)/shard_map/ppermute | solution.py:47
  142.7 7.3 %collective-permute-start.51 = (bf16[768,128]{1,0:T(8,128)(2,1)S(1)}, bf16[768,128]{1,0:T(8,128)(2,1)S(1)}, u32[]{:S(2)}, u32[]{:S(2)}) collective-permute-start(bf16[768,128]{1,0:T(8,128)(2,1)S(1)} %get-tuple-element.94.refs_4_.refs_0_), channel_id=1, source_target_pairs={{0,16},{16,0},{1,17},{17,1},{2,18},{18,2},{3,19},{19,3},{4,20},{20... | collective-permute-start | bytes 589832 | tf_op jit(solution)/shard_map/ppermute | solution.py:47
  144.2 9.2 %collective-permute-start.54 = (bf16[2,16,3072]{2,1,0:T(8,128)(2,1)S(1)}, bf16[2,16,3072]{2,1,0:T(8,128)(2,1)S(1)}, u32[]{:S(2)}, u32[]{:S(2)}) collective-permute-start(bf16[2,16,3072]{2,1,0:T(8,128)(2,1)S(1)} %bitcast.31), channel_id=1, source_target_pairs={{0,2},{1,3},{2,0},{3,1},{4,6},{5,7},{6,4},{7,5},{8,10},{9,11},{10,... | collective-permute-start | bytes 589832 | tf_op jit(solution)/shard_map/ppermute | solution.py:47
  152.8 5.8 %collective-permute-start.52 = (bf16[32,3072]{1,0:T(8,128)(2,1)S(1)}, bf16[32,3072]{1,0:T(8,128)(2,1)S(1)}, u32[]{:S(2)}, u32[]{:S(2)}) collective-permute-start(bf16[32,3072]{1,0:T(8,128)(2,1)S(1)} %get-tuple-element.100.refs_3_), channel_id=1, source_target_pairs={{0,1},{1,0},{2,3},{3,2},{4,5},{5,4},{6,7},{7,6},{8,9},{9,8},{10,11... | collective-permute-start | bytes 589832 | tf_op jit(solution)/shard_map/ppermute | solution.py:47
  152.9 7.2 %collective-permute-start.55 = (bf16[2,16,3072]{2,1,0:T(8,128)(2,1)S(1)}, bf16[2,16,3072]{2,1,0:T(8,128)(2,1)S(1)}, u32[]{:S(2)}, u32[]{:S(2)}) collective-permute-start(bf16[2,16,3072]{2,1,0:T(8,128)(2,1)S(1)} %bitcast.32), channel_id=1, source_target_pairs={{0,1},{1,0},{2,3},{3,2},{4,5},{5,4},{6,7},{7,6},{8,9},{9,8},{10,11... | collective-permute-start | bytes 589832 | tf_op jit(solution)/shard_map/ppermute | solution.py:47
  153.4 6.7 %collective-permute-start.56 = (bf16[2,16,3072]{2,1,0:T(8,128)(2,1)S(1)}, bf16[2,16,3072]{2,1,0:T(8,128)(2,1)S(1)}, u32[]{:S(2)}, u32[]{:S(2)}) collective-permute-start(bf16[2,16,3072]{2,1,0:T(8,128)(2,1)S(1)} %collective-permute-done.54.refs_1_), channel_id=1, source_target_pairs={{0,1},{1,0},{2,3},{3,2},{4,5},{5,4},{6,7},{7,6},{8,9},{9,8},{10,11... | collective-permute-start | bytes 589832 | tf_op jit(solution)/shard_map/ppermute | solution.py:47
  158.7 6.3 %collective-permute-start.53 = (bf16[16,3072]{1,0:T(8,128)(2,1)S(1)}, bf16[16,3072]{1,0:T(8,128)(2,1)S(1)}, u32[]{:S(2)}, u32[]{:S(2)}) collective-permute-start(bf16[16,3072]{1,0:T(8,128)(2,1)S(1)} %get-tuple-element.103), channel_id=1, source_target_pairs={{0,2},{1,3},{2,0},{3,1},{4,6},{5,7},{6,4},{7,5},{8,10},{9,11},{10,... | collective-permute-start | bytes 294920 | tf_op jit(solution)/shard_map/ppermute | solution.py:47
  (40 other events, 176.5 us)

commit v3 on v2

--- a/solution.py
+++ b/solution.py
@@ -59,9 +59,17 @@
     return lax.ppermute(array, ("section", "tensor"), pairs)
 
 
+def core_side():
+    return lax.rem(lax.axis_index("tensor"), 2)
+
+
 def token_order(tensors):
-    here = lax.axis_index("tensor")
-    return [here ^ f for f in [*range(0, tensors, 2), *range(1, tensors, 2)]]
+    base = lax.axis_index("tensor") - core_side()
+    return [base ^ j for j in range(tensors)]
+
+
+def part(index, size):
+    return pl.ds(pl.multiple_of(index * size, size), size)
 
 
 def probs_kernel(tensors, q_ref, k_ref, *out_refs):
@@ -103,98 +111,171 @@
     return run(kernel, outs, [queries, keys], [], flops, 4 * queries.size)
 
 
-def ctx_matmul(weight_ref, upper, part_ref):
+def ctx_matmul(weight_ref, terms, start_ref, out_ref):
     half = weight_ref.shape[0] // 2
     step = min(half, 384)
     dims = (((1,), (1,)), ((), ()))
     for at in range(0, half, step):
-        low, high = (
-            lax.dot_general(
-                weight_ref[at + off : at + off + step, :], upper, dims, preferred_element_type=F32
-            )
-            for off in (0, half)
-        )
-        part_ref[at : at + step, :] = jnp.concatenate([low, high], axis=1).astype(BF16)
+        sides = []
+        for off in (0, half):
+            rows = slice(at + off, at + off + step)
+            total = None
+            for cols, upper in terms:
+                term = lax.dot_general(
+                    weight_ref[rows, cols], upper, dims, preferred_element_type=F32
+                )
+                total = term if total is None else total + term
+            sides.append(total)
+        out = jnp.concatenate(sides, axis=1)
+        if start_ref is not None:
+            out = out + start_ref[at : at + step, :]
+        out_ref[at : at + step, :] = out.astype(out_ref.dtype)
 
 
 def first_kernel(*refs):
-    blocks = refs[:-3]
-    weight_ref, part_ref, upper_ref = refs[-3:]
-    upper_ref[...] = jnp.concatenate([b[...] for b in blocks], axis=0)
-    ctx_matmul(weight_ref, upper_ref[...], part_ref)
-
-
-def next_kernel(rows, taker, *refs):
-    blocks = refs[:-4]
-    prev_ref, weight_ref, part_ref, upper_ref = refs[-4:]
+    blocks, (weight_ref, part_ref, near_ref, far_ref) = refs[:-4], refs[-4:]
+    side = core_side()
+    rows, width = blocks[0].shape
+    near, far = part(side, width // 2), part(1 - side, width // 2)
+    for flip, ref in enumerate(blocks):
+        at = part(side ^ flip, rows)
+        near_ref[at, :] = ref[:, near]
+        far_ref[at, :] = ref[:, far]
+    ctx_matmul(weight_ref, [(near, near_ref[...]), (far, far_ref[...])], None, part_ref)
+
+
+def take_turn(taker, blocks, prev_ref, upper_ref):
     take = lax.axis_index("section") == taker
+    rows = blocks[0].shape[0]
     for b, ref in enumerate(blocks):
         at = slice(b * rows, (b + 1) * rows)
         upper_ref[at, :] = jnp.where(take, ref[...], prev_ref[at, :])
-    ctx_matmul(weight_ref, upper_ref[...], part_ref)
-
-
-def ctx_call(kernel, operands, tokens, weight, after):
+
+
+def near_kernel(taker, *refs):
+    blocks, (prev_ref, weight_ref, start_ref, upper_ref) = refs[:-4], refs[-4:]
+    take_turn(taker, blocks, prev_ref, upper_ref)
+    cols = part(core_side(), upper_ref.shape[1])
+    ctx_matmul(weight_ref, [(cols, upper_ref[...])], None, start_ref)
+
+
+def far_kernel(taker, *refs):
+    blocks, (prev_ref, start_ref, weight_ref, part_ref, upper_ref) = refs[:-5], refs[-5:]
+    take_turn(taker, blocks, prev_ref, upper_ref)
+    cols = part(1 - core_side(), upper_ref.shape[1])
+    ctx_matmul(weight_ref, [(cols, upper_ref[...])], start_ref, part_ref)
+
+
+def first_ctx(blocks, weight, tokens, after):
     cols, width = weight.shape
-    outs = [((cols // 2, 2 * tokens), BF16), ((tokens, width), BF16)]
+    side = ((tokens, width // 2), BF16)
+    outs = [((cols // 2, 2 * tokens), BF16), side, side]
     flops = 2 * tokens * cols * width
-    return run(kernel, outs, [*operands, weight], after, flops, 2 * weight.size)
-
-
-def branch_kernel(terms, *refs):
-    parts, (probs_ref, weight_ref) = refs[:terms], refs[terms : terms + 2]
-    keep_ref, send_ref, grad_ref = refs[-3:]
-    tokens = probs_ref.shape[2]
-    heads = probs_ref.shape[0]
-    half = heads // 2
-    packed = parts[0][...].astype(F32)
-    for ref in parts[1:]:
+    return run(first_kernel, outs, [*blocks, weight], after, flops, 2 * weight.size)
+
+
+def half_ctx(taker, blocks, prev, start, weight, after):
+    cols, tokens = weight.shape[0], prev.shape[0]
+    kernel = functools.partial(near_kernel if start is None else far_kernel, taker)
+    starts = [] if start is None else [start]
+    outs = [((cols // 2, 2 * tokens), F32 if start is None else BF16), (prev.shape, BF16)]
+    operands = [*blocks, prev, *starts, weight]
+    return run(kernel, outs, operands, after, 2 * cols * prev.size, weight.size)
+
+
+def value_grads(terms, probs_ref, grad_ref):
+    half = probs_ref.shape[0] // 2
+    packed = terms[0][...].astype(F32)
+    for ref in terms[1:]:
         packed = packed + ref[...].astype(F32)
     packed = packed.astype(BF16)
-    for h in range(heads):
+    for h in range(2 * half):
         row = (h % half) * HEAD_DIM
         grad = jnp.dot(
             packed[row : row + HEAD_DIM, :], probs_ref[h], preferred_element_type=F32
         )
         grad_ref[h * HEAD_DIM : (h + 1) * HEAD_DIM, :] = grad.astype(BF16)
-    grads = grad_ref[...]
-    width = weight_ref.shape[0]
-    step = min(width, 768)
-    for at in range(0, width, step):
-        out = jnp.dot(weight_ref[at : at + step, :], grads, preferred_element_type=F32)
-        out = out.T.astype(BF16)
-        keep_ref[:, at : at + step] = out[: tokens // 2]
-        send_ref[:, at : at + step] = out[tokens // 2 :]
-
-
-def branch(parts, probs, weight, after):
+
+
+def branch_rows(weight_ref, first, count, grads):
+    step = min(count, 768)
+    for at in range(0, count, step):
+        rows = pl.ds(pl.multiple_of(first * count + at, 128), step)
+        out = jnp.dot(weight_ref[rows, :], grads, preferred_element_type=F32)
+        yield slice(at, at + step), out.T
+
+
+def send_kernel(*refs):
+    terms, (probs_ref, weight_ref, send_ref, grad_ref) = refs[:-4], refs[-4:]
+    value_grads(terms, probs_ref, grad_ref)
+    half = send_ref.shape[1]
+    for at, out in branch_rows(weight_ref, 1 - core_side(), half, grad_ref[...]):
+        send_ref[:, at] = out.astype(BF16)
+
+
+def keep_kernel(grad_ref, weight_ref, keep_ref):
+    half = keep_ref.shape[1]
+    for at, out in branch_rows(weight_ref, core_side(), half, grad_ref[...]):
+        keep_ref[:, at] = out
+
+
+def send_branch(terms, probs, weight, after):
     width, cols = weight.shape
     tokens = probs.shape[2]
-    half = ((tokens // 2, width), BF16)
-    outs = [half, half, ((cols, tokens), BF16)]
-    kernel = functools.partial(branch_kernel, len(parts))
+    outs = [((tokens, width // 2), BF16), ((cols, tokens), BF16)]
+    flops = tokens * cols * width
+    return run(send_kernel, outs, [*terms, probs, weight], after, flops, weight.size)
+
+
+def keep_branch(grads, weight, after):
+    width, cols = weight.shape
+    tokens = grads.shape[1]
+    outs = [((tokens, width // 2), F32)]
+    flops = tokens * cols * width
+    return run(keep_kernel, outs, [grads, weight], after, flops, weight.size)[0]
+
+
+def last_kernel(rows, *refs):
+    terms, (probs_ref, weight_ref, keep_ref, send_ref, grad_ref) = refs[:-5], refs[-5:]
+    value_grads(terms, probs_ref, grad_ref)
+    low = core_side() == 0
+    for at, out in branch_rows(weight_ref, 0, keep_ref.shape[1], grad_ref[...]):
+        for b in range(keep_ref.shape[0] // rows):
+            one = out[2 * b * rows : (2 * b + 1) * rows]
+            two = out[(2 * b + 1) * rows : (2 * b + 2) * rows]
+            keep_ref[b * rows : (b + 1) * rows, at] = jnp.where(low, one, two)
+            send_ref[b * rows : (b + 1) * rows, at] = jnp.where(low, two, one).astype(BF16)
+
+
+def last_branch(terms, probs, weight, rows, after):
+    width, cols = weight.shape
+    tokens = probs.shape[2]
+    half = (tokens // 2, width)
+    outs = [(half, F32), (half, BF16), ((cols, tokens), BF16)]
+    kernel = functools.partial(last_kernel, rows)
     flops = 2 * tokens * cols * width
-    return run(kernel, outs, [*parts, probs, weight], after, flops, 2 * weight.size)
-
-
-def pair_kernel(rows, keep_ref, got_ref, mine_ref, *away_refs):
-    out = keep_ref[...].astype(F32) + got_ref[...].astype(F32)
-    mine_ref[...] = out[:rows]
-    for b, ref in enumerate(away_refs):
-        ref[...] = out[(b + 1) * rows : (b + 2) * rows].astype(BF16)
-
-
-def pair_sum(keep, got, rows, after):
+    return run(kernel, outs, [*terms, probs, weight], after, flops, 2 * weight.size)
+
+
+def pair_kernel(keep_ref, got_ref, mine_ref, *away_refs):
+    total = keep_ref[...] + got_ref[...].astype(F32)
+    rows = mine_ref.shape[0]
+    mine_ref[...] = total[:rows]
+    for b, ref in enumerate(away_refs, 1):
+        ref[...] = total[b * rows : (b + 1) * rows].astype(BF16)
+
+
+def pair_sum(keep, got, chips, after):
     total, width = keep.shape
-    outs = [((rows, width), F32)] + [((rows, width), BF16)] * (total // rows - 1)
-    kernel = functools.partial(pair_kernel, rows)
-    return run(kernel, outs, [keep, got], after, keep.size, 6 * keep.size)
+    shape = (total // chips, width)
+    outs = [(shape, F32)] + [(shape, BF16)] * (chips - 1)
+    return run(pair_kernel, outs, [keep, got], after, keep.size, 6 * keep.size)
 
 
 def fresh_kernel(*refs):
-    mine_ref, upper_ref, out_ref = refs[0], refs[-2], refs[-1]
+    mine_ref, heard, (upper_ref, out_ref) = refs[0], refs[1:-2], refs[-2:]
     total = mine_ref[...]
-    for ref in refs[1:-2]:
+    for ref in heard:
         total = total + ref[...].astype(F32)
     rows = mine_ref.shape[0]
     out_ref[...] = (total + upper_ref[:rows, :].astype(F32)).astype(BF16)
@@ -204,6 +285,32 @@
     operands = [mine, *heard, upper]
     outs = [(mine.shape, BF16)]
     return run(fresh_kernel, outs, operands, after, mine.size, 6 * mine.size)[0]
+
+
+def result_kernel(micro, *refs):
+    out_ref = refs[-1]
+    rows, half = out_ref.shape[1], out_ref.shape[2] // 2
+    each = (len(refs) - 1) // micro
+    side = core_side()
+    for m in range(micro):
+        mine_ref, *heard, near_ref, far_ref = refs[m * each : (m + 1) * each]
+        for upper_ref, cols in ((near_ref, part(side, half)), (far_ref, part(1 - side, half))):
+            total = mine_ref[:, cols]
+            for ref in heard:
+                total = total + ref[:, cols].astype(F32)
+            upper = upper_ref[part(side, rows), :].astype(F32)
+            out_ref[m, :, cols] = (total + upper).astype(BF16)
+
+
+def result_rows(mine, heard, uppers):
+    micro, (rows, width) = len(mine), mine[0].shape
+    operands = []
+    for m in range(micro):
+        operands += [mine[m], *heard[m], *uppers[m]]
+    kernel = functools.partial(result_kernel, micro)
+    size = micro * rows * width
+    outs = [((micro, rows, width), BF16)]
+    return run(kernel, outs, operands, [], size, 6 * size)[0]
 
 
 def hold_kernel(src_ref, out_ref, sems):
@@ -227,7 +334,7 @@
         out_shape=jax.ShapeDtypeStruct(array.shape, array.dtype),
         in_specs=[pl.BlockSpec(memory_space=pltpu.HBM)],
         out_specs=vmem(),
-        scratch_shapes=[pltpu.SemaphoreType.DMA((4,))],
+        scratch_shapes=[pltpu.SemaphoreType.DMA((8,))],
         compiler_params=params(4),
         cost_estimate=cost(array.size, 2 * array.size),
         name="held",
@@ -255,27 +362,28 @@
 
 
 def out_grad_kernel(tensors, ctx_ref, *refs):
-    uppers, (out_ref, buf, sems, rhs) = refs[:-4], refs[-4:]
-    tokens = uppers[0].shape[0]
+    uppers, (out_ref, buf, sems, _, rhs) = refs[:-5], refs[-5:]
+    tokens, half = uppers[0].shape
     rows = tokens // tensors
-    for m, ref in enumerate(uppers):
+    sides = (core_side(), 1 - core_side())
+    for i, ref in enumerate(uppers):
         for b, block in enumerate(token_order(tensors)):
-            at = pl.multiple_of(m * tokens + block * rows, rows)
-            rhs[pl.ds(at, rows), :] = ref[b * rows : (b + 1) * rows, :]
+            at = pl.multiple_of((i // 2) * tokens + block * rows, rows)
+            rhs[pl.ds(at, rows), part(sides[i % 2], half)] = ref[b * rows : (b + 1) * rows, :]
     stream_product(lambda at: ctx_ref[:, at], rhs[...], out_ref, buf, sems)
 
 
 def value_grad_kernel(micro, *refs):
-    blocks, grads = refs[: -micro - 4], refs[-micro - 4 : -4]
-    out_ref, buf, sems, rhs = refs[-4:]
+    blocks, grads = refs[: -micro - 5], refs[-micro - 5 : -5]
+    out_ref, buf, sems, lhs, rhs = refs[-5:]
     tokens = grads[0].shape[1]
+    rows = tokens // len(blocks)
     for m, ref in enumerate(grads):
         rhs[m * tokens : (m + 1) * tokens, :] = ref[...].T
-
-    def lhs_of(at):
-        return jnp.concatenate([b[m, :, at] for m in range(micro) for b in blocks], axis=0)
-
-    stream_product(lhs_of, rhs[...], out_ref, buf, sems)
+        for flip, block in enumerate(blocks):
+            at = pl.multiple_of(m * tokens + (core_side() ^ flip) * rows, rows)
+            lhs[pl.ds(at, rows), :] = block[m]
+    stream_product(lambda at: lhs[:, at], rhs[...], out_ref, buf, sems)
 
 
 def weight_grad(kernel, operands, shape, tokens):
@@ -289,6 +397,7 @@
         scratch_shapes=[
             pltpu.VMEM(shape, BF16),
             pltpu.SemaphoreType.DMA((rows // step,)),
+            pltpu.VMEM((tokens, rows), BF16),
             pltpu.VMEM((tokens, cols), BF16),
         ],
         compiler_params=params(20),
@@ -305,51 +414,59 @@
     value_proj = value_weight[0]
     turns = range(0, tensors, 2)
 
-    def both_cores(near):
-        return [*near, *(across(n, "tensor", 1) for n in near)]
-
     def gathered(block):
         near = [block] + [across(block, "tensor", f) for f in turns[1:]]
-        return both_cores(near)
-
-    first = []
+        far = [across(n, "tensor", 1) for n in near]
+        return [b for both in zip(near, far) for b in both]
+
+    def each():
+        return [None] * micro
+
+    first = each()
     for m in range(micro):
-        first.append(gathered(cotangent[m]))
+        first[m] = gathered(cotangent[m])
     probs = attention_probs(queries[0], keys[0], tensors)
     out_proj = held(out_weight[0])
-    parts, uppers, grads, fresh = [None] * micro, [None] * micro, [None] * micro, [None] * micro
+    parts, nears, fars, grads = each(), each(), each(), each()
     last = list(probs[:1])
     for m in range(micro):
-        parts[m], uppers[m] = ctx_call(first_kernel, first[m], seq, out_proj, last)
+        parts[m], nears[m], fars[m] = first_ctx(first[m], out_proj, seq, last)
         last = [parts[m]]
     in_blocks = gathered(inputs[0])
     for stage in range(sections):
-        giver = sections - 1 - stage
-        mine, away = [None] * micro, [None] * micro
-        for m in range(micro + 1):
-            if m < micro:
-                heard = [across(parts[m], "dp", d) for d in range(1, replicas)]
-                keep, send, grads[m] = branch(
-                    [parts[m], *heard], probs[m], value_proj, last
-                )
-                last = [send]
-            if m > 0:
-                heard = [across(a, "tensor", f) for a, f in zip(away[m - 1], turns[1:])]
-                fresh[m - 1] = fresh_rows(mine[m - 1], heard, uppers[m - 1], last)
-                last = [fresh[m - 1]]
-            if m < micro:
-                mine[m], *away[m] = pair_sum(keep, across(send, "tensor", 1), rows, last)
-                last = [mine[m]]
-        if stage == sections - 1:
+        ending = stage == sections - 1
+        mine, heard = each(), each()
+        for m in range(micro):
+            terms = [parts[m]] + [across(parts[m], "dp", d) for d in range(1, replicas)]
+            if ending:
+                keep, send, grads[m] = last_branch(terms, probs[m], value_proj, rows, last)
+                got = across(send, "tensor", 1)
+            else:
+                send, grads[m] = send_branch(terms, probs[m], value_proj, last)
+                got = across(send, "tensor", 1)
+                keep = keep_branch(grads[m], value_proj, [send])
+            mine[m], *away = pair_sum(keep, got, tensors // 2, [])
+            last = [mine[m]]
+            heard[m] = [across(a, "tensor", f) for a, f in zip(away, turns[1:])]
+        if ending:
             break
+        fresh = each()
+        last = last + (in_blocks[2::2] if stage == 0 else in_blocks[1::2] if stage == 1 else [])
         for m in range(micro):
-            blocks = both_cores([below(fresh[m], giver, f) for f in turns])
-            kernel = functools.partial(next_kernel, rows, giver - 1)
-            parts[m], uppers[m] = ctx_call(kernel, [*blocks, uppers[m]], seq, out_proj, last)
+            fresh[m] = fresh_rows(mine[m], heard[m], nears[m], last)
+            last = [fresh[m]]
+        for m in range(micro):
+            near = [below(fresh[m], sections - 1 - stage, f) for f in turns]
+            far = [across(n, "tensor", 1) for n in near]
+            taker = sections - 2 - stage
+            start, nears[m] = half_ctx(taker, near, nears[m], None, out_proj, last)
+            parts[m], fars[m] = half_ctx(taker, far, fars[m], start, out_proj, [])
             last = [parts[m]]
+    uppers = list(zip(nears, fars))
+    result = result_rows(mine, heard, uppers)
     out_w = weight_grad(
         functools.partial(out_grad_kernel, tensors),
-        [context[0].reshape(micro * seq, cols), *uppers],
+        [context[0].reshape(micro * seq, cols), *(side for both in uppers for side in both)],
         (cols, width),
         micro * seq,
     )
@@ -359,7 +476,7 @@
         (width, cols),
         micro * seq,
     )
-    return (jnp.stack(fresh)[None], value_w[None], out_w[None])
+    return (result[None], value_w[None], out_w[None])
 
 
 def solution(mesh):

time: 166 us -> 163 us (0.982)
  waiting for transfers between devices: 56 us -> 49.6 us
  Pallas kernels: 58.9 us -> 62.2 us
    ppermute x45, waiting for transfers between devices: 45.7 us -> 39.4 us  [across(): return lax.ppermute(array, axis, [(i, i ^ flip) for i in range(count)])]
    pallas_call x33 -> x44, Pallas kernels: 45.8 us -> 49.1 us  [run(): pl.pallas_call(body, out_shape=[jax.ShapeDtypeStruct(*out) for out in out...]
  transfers between devices with their start and end apart: 57 -> 57, of which waited for: 29 -> 24; matrix products, arithmetic and copies ran while one was open for 0% -> 0% of each run, Pallas kernels for 23% -> 28%
where the time goes in v3:
time: 163 us
  Pallas kernels  62.2 us (38%)
  waiting for transfers between devices  49.6 us (30%)
  starting transfers between devices  49.2 us (30%)
    pallas_call x44, Pallas kernels, run(): pl.pallas_call(body, out_shape=[jax.ShapeDtypeStruct(*out) for out in out...  49.1 us
    ppermute x45, waiting for transfers between devices, across(): return lax.ppermute(array, axis, [(i, i ^ flip) for i in range(count)])  39.4 us
    ppermute x45, starting transfers between devices, across(): return lax.ppermute(array, axis, [(i, i ^ flip) for i in range(count)])  31.5 us
    ppermute x12, starting transfers between devices, below(): return lax.ppermute(array, ('section', 'tensor'), pairs)  17.7 us
    ppermute x12, waiting for transfers between devices, below(): return lax.ppermute(array, ('section', 'tensor'), pairs)  10.2 us
    pallas_call x2, Pallas kernels, weight_grad(): pl.pallas_call(kernel, out_shape=jax.ShapeDtypeStruct(shape, BF16), in_sp...  9.28 us
    pallas_call x1, Pallas kernels, held(): pl.pallas_call(hold_kernel, out_shape=jax.ShapeDtypeStruct(array.shape, a...  3.85 us
  transfers between devices with their start and end apart: 57, of which 24 were waited for; matrix products, arithmetic and copies ran while one was open for 0% of the time, Pallas kernels for 28%

profile of v3, /device:TPU:0, one launch (start us, length us, event | category | flops | bytes accessed | tf_op | source)
XLA Modules:
  0.0 163.3 jit_solution(13633375859480651477)
XLA Ops:
  1.6 3.1 %collective-permute-start.1 = (bf16[16,3072]{1,0:T(8,128)(2,1)S(1)}, bf16[16,3072]{1,0:T(8,128)(2,1)S(1)}, u32[]{:S(2)}, u32[]{:S(2)}) collective-permute-start(bf16[16,3072]{1,0:T(8,128)(2,1)S(1)} %get-tuple-element.136.refs_0_), channel_id=1, source_target_pairs={{0,2},{1,3},{2,0},{3,1},{4,6},{5,7},{6,4},{7,5},{8,10},{9,11},{10,... | collective-permute-start | bytes 294920 | tf_op jit(solution)/shard_map/ppermute | solution.py:47
  4.7 2.8 %collective-permute-done.1.refs_2_ = bf16[16,3072]{1,0:T(8,128)(2,1)S(1)} collective-permute-done((bf16[16,3072]{1,0:T(8,128)(2,1)S(1)}, bf16[16,3072]{1,0:T(8,128)(2,1)S(1)}, u32[]{:S(2)}, u32[]{:S(2)}) %collective-permute-start.1) | collective-permute-done | bytes 98336 | tf_op jit(solution)/shard_map/ppermute | solution.py:47
  7.4 1.8 %collective-permute-start.5 = (bf16[16,3072]{1,0:T(8,128)(2,1)S(1)}, bf16[16,3072]{1,0:T(8,128)(2,1)S(1)}, u32[]{:S(2)}, u32[]{:S(2)}) collective-permute-start(bf16[16,3072]{1,0:T(8,128)(2,1)S(1)} %get-tuple-element.135.refs_0_), channel_id=1, source_target_pairs={{0,2},{1,3},{2,0},{3,1},{4,6},{5,7},{6,4},{7,5},{8,10},{9,11},{10,... | collective-permute-start | bytes 294920 | tf_op jit(solution)/shard_map/ppermute | solution.py:47
  9.3 3.8 %held.1.refs_4_.refs_3_ = bf16[1536,3072]{1,0:T(8,128)(2,1)S(1)} custom-call(bf16[1536,3072]{1,0:T(8,128)(2,1)} %bitcast.35), custom_call_target="tpu_custom_call" | custom-call | flops 4718592 | bytes 9437184 | tf_op jit(solution)/shard_map/held/pallas_call | solution.py:332
  13.9 2.7 %shard_map.95 = (bf16[768,128]{1,0:T(8,128)(2,1)S(1)}, bf16[64,1536]{1,0:T(8,128)(2,1)S(1)}, bf16[64,1536]{1,0:T(8,128)(2,1)S(1)}) custom-call(bf16[16,3072]{1,0:T(8,128)(2,1)S(1)} %get-tuple-element.136.refs_0_, bf16[16,3072]{1,0:T(8,128)(2,1)S(1)} %collective-permute-done.refs_1_, bf16[16,3072]{1,0:T(8,128)(2,1)S(1)} %collective-permute-done.1.refs_2_, ...), custom_call_target="tpu_custom_call" | custom-call | flops 603979776 | bytes 9437184 | tf_op jit(solution)/shard_map/pallas_call | solution.py:35
  19.6 2.7 %shard_map.96 = (bf16[768,128]{1,0:T(8,128)(2,1)S(1)}, bf16[64,1536]{1,0:T(8,128)(2,1)S(1)}, bf16[64,1536]{1,0:T(8,128)(2,1)S(1)}) custom-call(bf16[16,3072]{1,0:T(8,128)(2,1)S(1)} %get-tuple-element.135.refs_0_, bf16[16,3072]{1,0:T(8,128)(2,1)S(1)} %collective-permute-done.4.refs_1_, bf16[16,3072]{1,0:T(8,128)(2,1)S(1)} %collective-permute-done.5.refs_2_, ...), custom_call_target="tpu_custom_call" | custom-call | flops 603979776 | bytes 9437184 | tf_op jit(solution)/shard_map/pallas_call | solution.py:35
  28.5 4.2 %collective-permute-done.9.refs_1_ = bf16[768,128]{1,0:T(8,128)(2,1)S(1)} collective-permute-done((bf16[768,128]{1,0:T(8,128)(2,1)S(1)}, bf16[768,128]{1,0:T(8,128)(2,1)S(1)}, u32[]{:S(2)}, u32[]{:S(2)}) %collective-permute-start.9) | collective-permute-done | bytes 196640 | tf_op jit(solution)/shard_map/ppermute | solution.py:47
  34.8 1.7 %collective-permute-start.8 = (bf16[32,1536]{1,0:T(8,128)(2,1)S(1)}, bf16[32,1536]{1,0:T(8,128)(2,1)S(1)}, u32[]{:S(2)}, u32[]{:S(2)}) collective-permute-start(bf16[32,1536]{1,0:T(8,128)(2,1)S(1)} %get-tuple-element.75), channel_id=1, source_target_pairs={{0,2},{1,3},{2,0},{3,1},{4,6},{5,7},{6,4},{7,5},{8,10},{9,11},{10,... | collective-permute-start | bytes 294920 | tf_op jit(solution)/shard_map/ppermute | solution.py:47
  38.0 4.2 %collective-permute-done.11.refs_4_.refs_2_ = bf16[2,16,3072]{2,1,0:T(8,128)(2,1)S(1)} collective-permute-done((bf16[2,16,3072]{2,1,0:T(8,128)(2,1)S(1)}, bf16[2,16,3072]{2,1,0:T(8,128)(2,1)S(1)}, u32[]{:S(2)}, u32[]{:S(2)}) %collective-permute-start.11) | collective-permute-done | bytes 196640 | tf_op jit(solution)/shard_map/ppermute | solution.py:47
  47.4 3.0 %collective-permute-done.14.refs_1_ = bf16[32,1536]{1,0:T(8,128)(2,1)S(1)} collective-permute-done((bf16[32,1536]{1,0:T(8,128)(2,1)S(1)}, bf16[32,1536]{1,0:T(8,128)(2,1)S(1)}, u32[]{:S(2)}, u32[]{:S(2)}) %collective-permute-start.14) | collective-permute-done | bytes 98336 | tf_op jit(solution)/shard_map/ppermute | solution.py:59
  51.3 2.0 %collective-permute-start.20 = (bf16[32,1536]{1,0:T(8,128)(2,1)S(1)}, bf16[32,1536]{1,0:T(8,128)(2,1)S(1)}, u32[]{:S(2)}, u32[]{:S(2)}) collective-permute-start(bf16[32,1536]{1,0:T(8,128)(2,1)S(1)} %shard_map.104.refs_4_), channel_id=1, source_target_pairs={{0,6},{1,7},{2,4},{3,5},{4,2},{5,3},{6,0},{7,1},{8,14},{9,15},{10,... | collective-permute-start | bytes 294920 | tf_op jit(solution)/shard_map/ppermute | solution.py:59
  68.1 4.2 %collective-permute-done.24.refs_1_ = bf16[768,128]{1,0:T(8,128)(2,1)S(1)} collective-permute-done((bf16[768,128]{1,0:T(8,128)(2,1)S(1)}, bf16[768,128]{1,0:T(8,128)(2,1)S(1)}, u32[]{:S(2)}, u32[]{:S(2)}) %collective-permute-start.24) | collective-permute-done | bytes 196640 | tf_op jit(solution)/shard_map/ppermute | solution.py:47
  76.6 3.2 %collective-permute-done.23.refs_1_ = bf16[32,1536]{1,0:T(8,128)(2,1)S(1)} collective-permute-done((bf16[32,1536]{1,0:T(8,128)(2,1)S(1)}, bf16[32,1536]{1,0:T(8,128)(2,1)S(1)}, u32[]{:S(2)}, u32[]{:S(2)}) %collective-permute-start.23) | collective-permute-done | bytes 98336 | tf_op jit(solution)/shard_map/ppermute | solution.py:47
  82.6 2.6 %collective-permute-done.30.refs_1_ = bf16[32,1536]{1,0:T(8,128)(2,1)S(1)} collective-permute-done((bf16[32,1536]{1,0:T(8,128)(2,1)S(1)}, bf16[32,1536]{1,0:T(8,128)(2,1)S(1)}, u32[]{:S(2)}, u32[]{:S(2)}) %collective-permute-start.30) | collective-permute-done | bytes 98336 | tf_op jit(solution)/shard_map/ppermute | solution.py:59
  101.4 4.2 %collective-permute-done.40.refs_1_ = bf16[768,128]{1,0:T(8,128)(2,1)S(1)} collective-permute-done((bf16[768,128]{1,0:T(8,128)(2,1)S(1)}, bf16[768,128]{1,0:T(8,128)(2,1)S(1)}, u32[]{:S(2)}, u32[]{:S(2)}) %collective-permute-start.40) | collective-permute-done | bytes 196640 | tf_op jit(solution)/shard_map/ppermute | solution.py:47
  110.3 2.3 %collective-permute-done.39.refs_1_ = bf16[32,1536]{1,0:T(8,128)(2,1)S(1)} collective-permute-done((bf16[32,1536]{1,0:T(8,128)(2,1)S(1)}, bf16[32,1536]{1,0:T(8,128)(2,1)S(1)}, u32[]{:S(2)}, u32[]{:S(2)}) %collective-permute-start.39) | collective-permute-done | bytes 98336 | tf_op jit(solution)/shard_map/ppermute | solution.py:47
  112.6 7.5 %collective-permute-start.44 = (bf16[32,1536]{1,0:T(8,128)(2,1)S(1)}, bf16[32,1536]{1,0:T(8,128)(2,1)S(1)}, u32[]{:S(2)}, u32[]{:S(2)}) collective-permute-start(bf16[32,1536]{1,0:T(8,128)(2,1)S(1)} %shard_map.127.refs_3_), channel_id=1, source_target_pairs={{0,6},{1,7},{2,4},{3,5},{4,2},{5,3},{6,0},{7,1},{8,14},{9,15},{10,... | collective-permute-start | bytes 294920 | tf_op jit(solution)/shard_map/ppermute | solution.py:59
  123.0 1.9 %collective-permute-done.42.refs_0_ = bf16[32,1536]{1,0:T(8,128)(2,1)S(1)} collective-permute-done((bf16[32,1536]{1,0:T(8,128)(2,1)S(1)}, bf16[32,1536]{1,0:T(8,128)(2,1)S(1)}, u32[]{:S(2)}, u32[]{:S(2)}) %collective-permute-start.42) | collective-permute-done | bytes 98336 | tf_op jit(solution)/shard_map/ppermute | solution.py:59
  125.0 3.0 %collective-permute-start.50 = (bf16[32,1536]{1,0:T(8,128)(2,1)S(1)}, bf16[32,1536]{1,0:T(8,128)(2,1)S(1)}, u32[]{:S(2)}, u32[]{:S(2)}) collective-permute-start(bf16[32,1536]{1,0:T(8,128)(2,1)S(1)} %shard_map.128.refs_4_), channel_id=1, source_target_pairs={{0,6},{1,7},{2,4},{3,5},{4,2},{5,3},{6,0},{7,1},{8,14},{9,15},{10,... | collective-permute-start | bytes 294920 | tf_op jit(solution)/shard_map/ppermute | solution.py:59
  137.6 2.8 %shard_map.133 = (f32[32,3072]{1,0:T(8,128)S(1)}, bf16[32,3072]{1,0:T(8,128)(2,1)S(1)}, bf16[1536,64]{1,0:T(8,128)(2,1)S(1)}) custom-call(bf16[768,128]{1,0:T(8,128)(2,1)S(1)} %get-tuple-element.117.refs_4_.refs_0_, bf16[768,128]{1,0:T(8,128)(2,1)S(1)} %collective-permute-done.47.refs_1_, bf16[12,128,64]{2,1,0:T(8,128)(2,1)S(1)} %get-tuple-element.69.refs_5_.refs_2_, ...), custom_call_target="tpu_custom_call" | custom-call | flops 603979776 | bytes 9437184 | tf_op jit(solution)/shard_map/pallas_call | solution.py:35
  142.1 5.7 %collective-permute-done.54.refs_1_ = bf16[768,128]{1,0:T(8,128)(2,1)S(1)} collective-permute-done((bf16[768,128]{1,0:T(8,128)(2,1)S(1)}, bf16[768,128]{1,0:T(8,128)(2,1)S(1)}, u32[]{:S(2)}, u32[]{:S(2)}) %collective-permute-start.54) | collective-permute-done | bytes 196640 | tf_op jit(solution)/shard_map/ppermute | solution.py:47
  147.8 2.8 %shard_map.135 = (f32[32,3072]{1,0:T(8,128)S(1)}, bf16[32,3072]{1,0:T(8,128)(2,1)S(1)}, bf16[1536,64]{1,0:T(8,128)(2,1)S(1)}) custom-call(bf16[768,128]{1,0:T(8,128)(2,1)S(1)} %get-tuple-element.120.refs_4_.refs_0_, bf16[768,128]{1,0:T(8,128)(2,1)S(1)} %collective-permute-done.54.refs_1_, bf16[12,128,64]{2,1,0:T(8,128)(2,1)S(1)} %get-tuple-element.77.refs_2_, ...), custom_call_target="tpu_custom_call" | custom-call | flops 603979776 | bytes 9437184 | tf_op jit(solution)/shard_map/pallas_call | solution.py:35
  150.8 4.4 %shard_map.139 = bf16[1536,3072]{1,0:T(8,128)(2,1)} custom-call(bf16[128,1536]{1,0:T(8,128)(2,1)S(1)} %bitcast.31, bf16[64,1536]{1,0:T(8,128)(2,1)S(1)} %get-tuple-element.125.refs_2_.refs_0_, bf16[64,1536]{1,0:T(8,128)(2,1)S(1)} %get-tuple-element.126.refs_3_.refs_1_, bf16[64,1536]{1,0:T(8,128)(2,1)S(1)} %get-tuple-element.131.refs_6_.refs_2_, ...), custom_call_target="tpu_custom_call" | custom-call | flops 1207959552 | bytes 9437184 | tf_op jit(solution)/shard_map/pallas_call | solution.py:392
  157.4 4.9 %shard_map.138 = bf16[3072,1536]{1,0:T(8,128)(2,1)} custom-call(bf16[2,16,3072]{2,1,0:T(8,128)(2,1)S(1)} %bitcast.34, bf16[2,16,3072]{2,1,0:T(8,128)(2,1)S(1)} %collective-permute-done.26.refs_4_.refs_1_, bf16[2,16,3072]{2,1,0:T(8,128)(2,1)S(1)} %collective-permute-done.11.refs_4_.refs_2_, bf16[2,16,3072]{2,1,0:T(8,128)(2,1)S(1)} %collective-permute-done.27.refs_5_.refs_3_, ...), custom_call_target="tpu_custom_call" | custom-call | flops 1207959552 | bytes 9437184 | tf_op jit(solution)/shard_map/pallas_call | solution.py:392
  (153 shorter events, 80.5 us)
Async XLA Ops:
  1.6 5.9 %collective-permute-start.1 = (bf16[16,3072]{1,0:T(8,128)(2,1)S(1)}, bf16[16,3072]{1,0:T(8,128)(2,1)S(1)}, u32[]{:S(2)}, u32[]{:S(2)}) collective-permute-start(bf16[16,3072]{1,0:T(8,128)(2,1)S(1)} %get-tuple-element.136.refs_0_), channel_id=1, source_target_pairs={{0,2},{1,3},{2,0},{3,1},{4,6},{5,7},{6,4},{7,5},{8,10},{9,11},{10,... | collective-permute-start | bytes 294920 | tf_op jit(solution)/shard_map/ppermute | solution.py:47
  4.6 9.2 %collective-permute-start = (bf16[16,3072]{1,0:T(8,128)(2,1)S(1)}, bf16[16,3072]{1,0:T(8,128)(2,1)S(1)}, u32[]{:S(2)}, u32[]{:S(2)}) collective-permute-start(bf16[16,3072]{1,0:T(8,128)(2,1)S(1)} %get-tuple-element.136.refs_0_), channel_id=1, source_target_pairs={{0,1},{1,0},{2,3},{3,2},{4,5},{5,4},{6,7},{7,6},{8,9},{9,8},{10,11... | collective-permute-start | bytes 294920 | tf_op jit(solution)/shard_map/ppermute | solution.py:47
  7.4 6.4 %collective-permute-start.2 = (bf16[16,3072]{1,0:T(8,128)(2,1)S(1)}, bf16[16,3072]{1,0:T(8,128)(2,1)S(1)}, u32[]{:S(2)}, u32[]{:S(2)}) collective-permute-start(bf16[16,3072]{1,0:T(8,128)(2,1)S(1)} %collective-permute-done.1.refs_2_), channel_id=1, source_target_pairs={{0,1},{1,0},{2,3},{3,2},{4,5},{5,4},{6,7},{7,6},{8,9},{9,8},{10,11... | collective-permute-start | bytes 294920 | tf_op jit(solution)/shard_map/ppermute | solution.py:47
  7.4 10.7 %collective-permute-start.5 = (bf16[16,3072]{1,0:T(8,128)(2,1)S(1)}, bf16[16,3072]{1,0:T(8,128)(2,1)S(1)}, u32[]{:S(2)}, u32[]{:S(2)}) collective-permute-start(bf16[16,3072]{1,0:T(8,128)(2,1)S(1)} %get-tuple-element.135.refs_0_), channel_id=1, source_target_pairs={{0,2},{1,3},{2,0},{3,1},{4,6},{5,7},{6,4},{7,5},{8,10},{9,11},{10,... | collective-permute-start | bytes 294920 | tf_op jit(solution)/shard_map/ppermute | solution.py:47
  16.6 7.1 %collective-permute-start.3 = (bf16[768,128]{1,0:T(8,128)(2,1)S(1)}, bf16[768,128]{1,0:T(8,128)(2,1)S(1)}, u32[]{:S(2)}, u32[]{:S(2)}) collective-permute-start(bf16[768,128]{1,0:T(8,128)(2,1)S(1)} %get-tuple-element.70.refs_5_.refs_0_), channel_id=1, source_target_pairs={{0,16},{16,0},{1,17},{17,1},{2,18},{18,2},{3,19},{19,3},{4,20},{20... | collective-permute-start | bytes 589832 | tf_op jit(solution)/shard_map/ppermute | solution.py:47
  25.4 7.3 %collective-permute-start.9 = (bf16[768,128]{1,0:T(8,128)(2,1)S(1)}, bf16[768,128]{1,0:T(8,128)(2,1)S(1)}, u32[]{:S(2)}, u32[]{:S(2)}) collective-permute-start(bf16[768,128]{1,0:T(8,128)(2,1)S(1)} %get-tuple-element.71.refs_4_.refs_0_), channel_id=1, source_target_pairs={{0,16},{16,0},{1,17},{17,1},{2,18},{18,2},{3,19},{19,3},{4,20},{20... | collective-permute-start | bytes 589832 | tf_op jit(solution)/shard_map/ppermute | solution.py:47
  34.4 7.8 %collective-permute-start.11 = (bf16[2,16,3072]{2,1,0:T(8,128)(2,1)S(1)}, bf16[2,16,3072]{2,1,0:T(8,128)(2,1)S(1)}, u32[]{:S(2)}, u32[]{:S(2)}) collective-permute-start(bf16[2,16,3072]{2,1,0:T(8,128)(2,1)S(1)} %bitcast.32), channel_id=1, source_target_pairs={{0,2},{1,3},{2,0},{3,1},{4,6},{5,7},{6,4},{7,5},{8,10},{9,11},{10,... | collective-permute-start | bytes 589832 | tf_op jit(solution)/shard_map/ppermute | solution.py:47
  34.8 9.1 %collective-permute-start.8 = (bf16[32,1536]{1,0:T(8,128)(2,1)S(1)}, bf16[32,1536]{1,0:T(8,128)(2,1)S(1)}, u32[]{:S(2)}, u32[]{:S(2)}) collective-permute-start(bf16[32,1536]{1,0:T(8,128)(2,1)S(1)} %get-tuple-element.75), channel_id=1, source_target_pairs={{0,2},{1,3},{2,0},{3,1},{4,6},{5,7},{6,4},{7,5},{8,10},{9,11},{10,... | collective-permute-start | bytes 294920 | tf_op jit(solution)/shard_map/ppermute | solution.py:47
  43.9 6.5 %collective-permute-start.14 = (bf16[32,1536]{1,0:T(8,128)(2,1)S(1)}, bf16[32,1536]{1,0:T(8,128)(2,1)S(1)}, u32[]{:S(2)}, u32[]{:S(2)}) collective-permute-start(bf16[32,1536]{1,0:T(8,128)(2,1)S(1)} %shard_map.103.refs_3_), channel_id=1, source_target_pairs={{0,6},{1,7},{2,4},{3,5},{4,2},{5,3},{6,0},{7,1},{8,14},{9,15},{10,... | collective-permute-start | bytes 294920 | tf_op jit(solution)/shard_map/ppermute | solution.py:59
  45.7 5.5 %collective-permute-start.16 = (bf16[32,1536]{1,0:T(8,128)(2,1)S(1)}, bf16[32,1536]{1,0:T(8,128)(2,1)S(1)}, u32[]{:S(2)}, u32[]{:S(2)}) collective-permute-start(bf16[32,1536]{1,0:T(8,128)(2,1)S(1)} %get-tuple-element.82), channel_id=1, source_target_pairs={{0,2},{1,3},{2,0},{3,1},{4,6},{5,7},{6,4},{7,5},{8,10},{9,11},{10,... | collective-permute-start | bytes 294920 | tf_op jit(solution)/shard_map/ppermute | solution.py:47
  51.3 6.9 %collective-permute-start.20 = (bf16[32,1536]{1,0:T(8,128)(2,1)S(1)}, bf16[32,1536]{1,0:T(8,128)(2,1)S(1)}, u32[]{:S(2)}, u32[]{:S(2)}) collective-permute-start(bf16[32,1536]{1,0:T(8,128)(2,1)S(1)} %shard_map.104.refs_4_), channel_id=1, source_target_pairs={{0,6},{1,7},{2,4},{3,5},{4,2},{5,3},{6,0},{7,1},{8,14},{9,15},{10,... | collective-permute-start | bytes 294920 | tf_op jit(solution)/shard_map/ppermute | solution.py:59
  53.3 5.6 %collective-permute-start.18 = (bf16[32,1536]{1,0:T(8,128)(2,1)S(1)}, bf16[32,1536]{1,0:T(8,128)(2,1)S(1)}, u32[]{:S(2)}, u32[]{:S(2)}) collective-permute-start(bf16[32,1536]{1,0:T(8,128)(2,1)S(1)} %shard_map.104.refs_4_), channel_id=1, source_target_pairs={{0,4},{1,5},{2,6},{3,7},{4,0},{5,1},{6,2},{7,3},{8,12},{9,13},{10,... | collective-permute-start | bytes 294920 | tf_op jit(solution)/shard_map/ppermute | solution.py:59
  56.5 6.8 %collective-permute-start.17 = (bf16[768,128]{1,0:T(8,128)(2,1)S(1)}, bf16[768,128]{1,0:T(8,128)(2,1)S(1)}, u32[]{:S(2)}, u32[]{:S(2)}) collective-permute-start(bf16[768,128]{1,0:T(8,128)(2,1)S(1)} %get-tuple-element.85.refs_4_.refs_0_), channel_id=1, source_target_pairs={{0,16},{16,0},{1,17},{17,1},{2,18},{18,2},{3,19},{19,3},{4,20},{20... | collective-permute-start | bytes 589832 | tf_op jit(solution)/shard_map/ppermute | solution.py:47
  65.0 7.3 %collective-permute-start.24 = (bf16[768,128]{1,0:T(8,128)(2,1)S(1)}, bf16[768,128]{1,0:T(8,128)(2,1)S(1)}, u32[]{:S(2)}, u32[]{:S(2)}) collective-permute-start(bf16[768,128]{1,0:T(8,128)(2,1)S(1)} %get-tuple-element.88.refs_4_.refs_0_), channel_id=1, source_target_pairs={{0,16},{16,0},{1,17},{17,1},{2,18},{18,2},{3,19},{19,3},{4,20},{20... | collective-permute-start | bytes 589832 | tf_op jit(solution)/shard_map/ppermute | solution.py:47
  86.3 6.2 %collective-permute-start.36 = (bf16[32,1536]{1,0:T(8,128)(2,1)S(1)}, bf16[32,1536]{1,0:T(8,128)(2,1)S(1)}, u32[]{:S(2)}, u32[]{:S(2)}) collective-permute-start(bf16[32,1536]{1,0:T(8,128)(2,1)S(1)} %shard_map.116.refs_4_), channel_id=1, source_target_pairs={{0,2},{1,3},{2,0},{3,1},{4,10},{5,11},{6,8},{7,9},{8,6},{9,7},{10,... | collective-permute-start | bytes 294920 | tf_op jit(solution)/shard_map/ppermute | solution.py:59
  90.9 5.7 %collective-permute-start.33 = (bf16[768,128]{1,0:T(8,128)(2,1)S(1)}, bf16[768,128]{1,0:T(8,128)(2,1)S(1)}, u32[]{:S(2)}, u32[]{:S(2)}) collective-permute-start(bf16[768,128]{1,0:T(8,128)(2,1)S(1)} %get-tuple-element.101.refs_4_.refs_0_), channel_id=1, source_target_pairs={{0,16},{16,0},{1,17},{17,1},{2,18},{18,2},{3,19},{19,3},{4,20},{20... | collective-permute-start | bytes 589832 | tf_op jit(solution)/shard_map/ppermute | solution.py:47
  98.4 7.3 %collective-permute-start.40 = (bf16[768,128]{1,0:T(8,128)(2,1)S(1)}, bf16[768,128]{1,0:T(8,128)(2,1)S(1)}, u32[]{:S(2)}, u32[]{:S(2)}) collective-permute-start(bf16[768,128]{1,0:T(8,128)(2,1)S(1)} %get-tuple-element.104.refs_4_.refs_0_), channel_id=1, source_target_pairs={{0,16},{16,0},{1,17},{17,1},{2,18},{18,2},{3,19},{19,3},{4,20},{20... | collective-permute-start | bytes 589832 | tf_op jit(solution)/shard_map/ppermute | solution.py:47
  112.6 10.4 %collective-permute-start.44 = (bf16[32,1536]{1,0:T(8,128)(2,1)S(1)}, bf16[32,1536]{1,0:T(8,128)(2,1)S(1)}, u32[]{:S(2)}, u32[]{:S(2)}) collective-permute-start(bf16[32,1536]{1,0:T(8,128)(2,1)S(1)} %shard_map.127.refs_3_), channel_id=1, source_target_pairs={{0,6},{1,7},{2,4},{3,5},{4,2},{5,3},{6,0},{7,1},{8,14},{9,15},{10,... | collective-permute-start | bytes 294920 | tf_op jit(solution)/shard_map/ppermute | solution.py:59
  123.0 6.4 %collective-permute-start.45 = (bf16[32,1536]{1,0:T(8,128)(2,1)S(1)}, bf16[32,1536]{1,0:T(8,128)(2,1)S(1)}, u32[]{:S(2)}, u32[]{:S(2)}) collective-permute-start(bf16[32,1536]{1,0:T(8,128)(2,1)S(1)} %collective-permute-done.44.refs_1_), channel_id=1, source_target_pairs={{0,1},{1,0},{2,3},{3,2},{4,5},{5,4},{6,7},{7,6},{8,9},{9,8},{10,11... | collective-permute-start | bytes 294920 | tf_op jit(solution)/shard_map/ppermute | solution.py:47
  125.0 7.5 %collective-permute-start.50 = (bf16[32,1536]{1,0:T(8,128)(2,1)S(1)}, bf16[32,1536]{1,0:T(8,128)(2,1)S(1)}, u32[]{:S(2)}, u32[]{:S(2)}) collective-permute-start(bf16[32,1536]{1,0:T(8,128)(2,1)S(1)} %shard_map.128.refs_4_), channel_id=1, source_target_pairs={{0,6},{1,7},{2,4},{3,5},{4,2},{5,3},{6,0},{7,1},{8,14},{9,15},{10,... | collective-permute-start | bytes 294920 | tf_op jit(solution)/shard_map/ppermute | solution.py:59
  130.9 6.7 %collective-permute-start.47 = (bf16[768,128]{1,0:T(8,128)(2,1)S(1)}, bf16[768,128]{1,0:T(8,128)(2,1)S(1)}, u32[]{:S(2)}, u32[]{:S(2)}) collective-permute-start(bf16[768,128]{1,0:T(8,128)(2,1)S(1)} %get-tuple-element.117.refs_4_.refs_0_), channel_id=1, source_target_pairs={{0,16},{16,0},{1,17},{17,1},{2,18},{18,2},{3,19},{19,3},{4,20},{20... | collective-permute-start | bytes 589832 | tf_op jit(solution)/shard_map/ppermute | solution.py:47
  140.5 7.3 %collective-permute-start.54 = (bf16[768,128]{1,0:T(8,128)(2,1)S(1)}, bf16[768,128]{1,0:T(8,128)(2,1)S(1)}, u32[]{:S(2)}, u32[]{:S(2)}) collective-permute-start(bf16[768,128]{1,0:T(8,128)(2,1)S(1)} %get-tuple-element.120.refs_4_.refs_0_), channel_id=1, source_target_pairs={{0,16},{16,0},{1,17},{17,1},{2,18},{18,2},{3,19},{19,3},{4,20},{20... | collective-permute-start | bytes 589832 | tf_op jit(solution)/shard_map/ppermute | solution.py:47
  155.2 7.1 %collective-permute-start.53 = (bf16[16,3072]{1,0:T(8,128)(2,1)S(1)}, bf16[16,3072]{1,0:T(8,128)(2,1)S(1)}, u32[]{:S(2)}, u32[]{:S(2)}) collective-permute-start(bf16[16,3072]{1,0:T(8,128)(2,1)S(1)} %get-tuple-element.124), channel_id=1, source_target_pairs={{0,2},{1,3},{2,0},{3,1},{4,6},{5,7},{6,4},{7,5},{8,10},{9,11},{10,... | collective-permute-start | bytes 294920 | tf_op jit(solution)/shard_map/ppermute | solution.py:47
  156.0 6.6 %collective-permute-start.56 = (bf16[16,3072]{1,0:T(8,128)(2,1)S(1)}, bf16[16,3072]{1,0:T(8,128)(2,1)S(1)}, u32[]{:S(2)}, u32[]{:S(2)}) collective-permute-start(bf16[16,3072]{1,0:T(8,128)(2,1)S(1)} %get-tuple-element.130), channel_id=1, source_target_pairs={{0,2},{1,3},{2,0},{3,1},{4,6},{5,7},{6,4},{7,5},{8,10},{9,11},{10,... | collective-permute-start | bytes 294920 | tf_op jit(solution)/shard_map/ppermute | solution.py:47
  (40 other events, 172.1 us)

commit v4 on v3

--- a/solution.py
+++ b/solution.py
@@ -47,16 +47,13 @@
     return lax.ppermute(array, axis, [(i, i ^ flip) for i in range(count)])
 
 
-def below(array, giver, flip):
-    sections, tensors = lax.axis_size("section"), lax.axis_size("tensor")
+def below(array, giver):
+    count = lax.axis_size("section")
     pairs = []
-    for s in range(sections):
+    for s in range(count):
         peer = s - 1 if (s - giver) % 2 == 0 else s + 1
-        if not 0 <= peer < sections:
-            peer = s
-        for t in range(tensors):
-            pairs.append((s * tensors + t, peer * tensors + (t ^ flip)))
-    return lax.ppermute(array, ("section", "tensor"), pairs)
+        pairs.append((s, peer if 0 <= peer < count else s))
+    return lax.ppermute(array, "section", pairs)
 
 
 def core_side():
@@ -132,15 +129,15 @@
         out_ref[at : at + step, :] = out.astype(out_ref.dtype)
 
 
-def first_kernel(*refs):
+def first_kernel(m, *refs):
     blocks, (weight_ref, part_ref, near_ref, far_ref) = refs[:-4], refs[-4:]
     side = core_side()
-    rows, width = blocks[0].shape
+    rows, width = blocks[0].shape[1:]
     near, far = part(side, width // 2), part(1 - side, width // 2)
     for flip, ref in enumerate(blocks):
         at = part(side ^ flip, rows)
-        near_ref[at, :] = ref[:, near]
-        far_ref[at, :] = ref[:, far]
+        near_ref[at, :] = ref[m, :, near]
+        far_ref[at, :] = ref[m, :, far]
     ctx_matmul(weight_ref, [(near, near_ref[...]), (far, far_ref[...])], None, part_ref)
 
 
@@ -166,12 +163,13 @@
     ctx_matmul(weight_ref, [(cols, upper_ref[...])], start_ref, part_ref)
 
 
-def first_ctx(blocks, weight, tokens, after):
+def first_ctx(m, blocks, weight, tokens, after):
     cols, width = weight.shape
     side = ((tokens, width // 2), BF16)
     outs = [((cols // 2, 2 * tokens), BF16), side, side]
     flops = 2 * tokens * cols * width
-    return run(first_kernel, outs, [*blocks, weight], after, flops, 2 * weight.size)
+    kernel = functools.partial(first_kernel, m)
+    return run(kernel, outs, [*blocks, weight], after, flops, 2 * weight.size)
 
 
 def half_ctx(taker, blocks, prev, start, weight, after):
@@ -272,13 +270,27 @@
     return run(pair_kernel, outs, [keep, got], after, keep.size, 6 * keep.size)
 
 
+def whole_pair_kernel(keep_ref, got_ref, mine_ref, away_ref):
+    mine = keep_ref[...] + got_ref[...].astype(F32)
+    mine_ref[...] = mine
+    away_ref[...] = mine.astype(BF16)
+
+
+def whole_pair_sum(keep, got):
+    outs = [(keep.shape, F32), (keep.shape, BF16)]
+    return run(whole_pair_kernel, outs, [keep, got], [], keep.size, 6 * keep.size)
+
+
 def fresh_kernel(*refs):
     mine_ref, heard, (upper_ref, out_ref) = refs[0], refs[1:-2], refs[-2:]
-    total = mine_ref[...]
-    for ref in heard:
-        total = total + ref[...].astype(F32)
-    rows = mine_ref.shape[0]
-    out_ref[...] = (total + upper_ref[:rows, :].astype(F32)).astype(BF16)
+    chips = len(heard) + 1
+    rows = mine_ref.shape[0] // chips
+    for b in range(chips):
+        at = slice(b * rows, (b + 1) * rows)
+        total = mine_ref[at, :]
+        for d, ref in enumerate(heard, 1):
+            total = total + ref[(b ^ d) * rows : ((b ^ d) + 1) * rows, :].astype(F32)
+        out_ref[at, :] = (total + upper_ref[at, :].astype(F32)).astype(BF16)
 
 
 def fresh_rows(mine, heard, upper, after):
@@ -362,7 +374,7 @@
 
 
 def out_grad_kernel(tensors, ctx_ref, *refs):
-    uppers, (out_ref, buf, sems, _, rhs) = refs[:-5], refs[-5:]
+    uppers, (out_ref, done_ref, buf, sems, _, rhs) = refs[:-6], refs[-6:]
     tokens, half = uppers[0].shape
     rows = tokens // tensors
     sides = (core_side(), 1 - core_side())
@@ -371,11 +383,12 @@
             at = pl.multiple_of((i // 2) * tokens + block * rows, rows)
             rhs[pl.ds(at, rows), part(sides[i % 2], half)] = ref[b * rows : (b + 1) * rows, :]
     stream_product(lambda at: ctx_ref[:, at], rhs[...], out_ref, buf, sems)
+    done_ref[...] = jnp.zeros_like(done_ref)
 
 
 def value_grad_kernel(micro, *refs):
-    blocks, grads = refs[: -micro - 5], refs[-micro - 5 : -5]
-    out_ref, buf, sems, lhs, rhs = refs[-5:]
+    blocks, grads = refs[: -micro - 6], refs[-micro - 6 : -6]
+    out_ref, done_ref, buf, sems, lhs, rhs = refs[-6:]
     tokens = grads[0].shape[1]
     rows = tokens // len(blocks)
     for m, ref in enumerate(grads):
@@ -384,16 +397,22 @@
             at = pl.multiple_of(m * tokens + (core_side() ^ flip) * rows, rows)
             lhs[pl.ds(at, rows), :] = block[m]
     stream_product(lambda at: lhs[:, at], rhs[...], out_ref, buf, sems)
-
-
-def weight_grad(kernel, operands, shape, tokens):
+    done_ref[...] = jnp.zeros_like(done_ref)
+
+
+def weight_grad(kernel, operands, shape, tokens, after):
     rows, cols = shape
     step = min(rows, 256)
+    used = len(operands)
+
+    def body(*refs):
+        kernel(*refs[:used], *refs[used + len(after) :])
+
     return pl.pallas_call(
-        kernel,
-        out_shape=jax.ShapeDtypeStruct(shape, BF16),
-        in_specs=[vmem()] * len(operands),
-        out_specs=pl.BlockSpec(memory_space=pltpu.HBM),
+        body,
+        out_shape=[jax.ShapeDtypeStruct(shape, BF16), jax.ShapeDtypeStruct((8, 128), F32)],
+        in_specs=[vmem()] * (used + len(after)),
+        out_specs=[pl.BlockSpec(memory_space=pltpu.HBM), vmem()],
         scratch_shapes=[
             pltpu.VMEM(shape, BF16),
             pltpu.SemaphoreType.DMA((rows // step,)),
@@ -402,7 +421,7 @@
         ],
         compiler_params=params(20),
         cost_estimate=cost(2 * tokens * rows * cols, 2 * rows * cols),
-    )(*operands)
+    )(*operands, *after)
 
 
 def per_device(cotangent, inputs, queries, keys, context, value_weight, out_weight):
@@ -422,20 +441,31 @@
     def each():
         return [None] * micro
 
-    first = each()
-    for m in range(micro):
-        first[m] = gathered(cotangent[m])
+    first = gathered(cotangent)
     probs = attention_probs(queries[0], keys[0], tensors)
     out_proj = held(out_weight[0])
     parts, nears, fars, grads = each(), each(), each(), each()
     last = list(probs[:1])
     for m in range(micro):
-        parts[m], nears[m], fars[m] = first_ctx(first[m], out_proj, seq, last)
+        parts[m], nears[m], fars[m] = first_ctx(m, first, out_proj, seq, last)
         last = [parts[m]]
     in_blocks = gathered(inputs[0])
     for stage in range(sections):
         ending = stage == sections - 1
         mine, heard = each(), each()
+        if ending:
+            uppers = list(zip(nears, fars))
+            out_w, done = weight_grad(
+                functools.partial(out_grad_kernel, tensors),
+                [
+                    context[0].reshape(micro * seq, cols),
+                    *(side for both in uppers for side in both),
+                ],
+                (cols, width),
+                micro * seq,
+                last,
+            )
+            last = [done]
         for m in range(micro):
             terms = [parts[m]] + [across(parts[m], "dp", d) for d in range(1, replicas)]
             if ending:
@@ -445,8 +475,13 @@
                 send, grads[m] = send_branch(terms, probs[m], value_proj, last)
                 got = across(send, "tensor", 1)
                 keep = keep_branch(grads[m], value_proj, [send])
-            mine[m], *away = pair_sum(keep, got, tensors // 2, [])
-            last = [mine[m]]
+            if ending:
+                mine[m], *away = pair_sum(keep, got, tensors // 2, [])
+                last = [send]
+            else:
+                mine[m], away = whole_pair_sum(keep, got)
+                away = [away] * (tensors // 2 - 1)
+                last = [mine[m]]
             heard[m] = [across(a, "tensor", f) for a, f in zip(away, turns[1:])]
         if ending:
             break
@@ -456,25 +491,19 @@
             fresh[m] = fresh_rows(mine[m], heard[m], nears[m], last)
             last = [fresh[m]]
         for m in range(micro):
-            near = [below(fresh[m], sections - 1 - stage, f) for f in turns]
+            near = [below(fresh[m], sections - 1 - stage)]
             far = [across(n, "tensor", 1) for n in near]
             taker = sections - 2 - stage
             start, nears[m] = half_ctx(taker, near, nears[m], None, out_proj, last)
             parts[m], fars[m] = half_ctx(taker, far, fars[m], start, out_proj, [])
             last = [parts[m]]
-    uppers = list(zip(nears, fars))
     result = result_rows(mine, heard, uppers)
-    out_w = weight_grad(
-        functools.partial(out_grad_kernel, tensors),
-        [context[0].reshape(micro * seq, cols), *(side for both in uppers for side in both)],
-        (cols, width),
-        micro * seq,
-    )
-    value_w = weight_grad(
+    value_w, _ = weight_grad(
         functools.partial(value_grad_kernel, micro),
         [*in_blocks, *grads],
         (width, cols),
         micro * seq,
+        mine,
     )
     return (result[None], value_w[None], out_w[None])
 

time: 163 us -> 162 us (level)
  starting transfers between devices: 49.2 us -> 45.1 us
  waiting for transfers between devices: 49.6 us -> 52.5 us
    ppermute x45 -> x36, waiting for transfers between devices: 39.4 us -> 44.7 us  [across(): return lax.ppermute(array, axis, [(i, i ^ flip) for i in range(count)])]
    ppermute x45 -> x36, starting transfers between devices: 31.5 us -> 28.6 us  [across(): return lax.ppermute(array, axis, [(i, i ^ flip) for i in range(count)])]
    ppermute x12 -> x6, waiting for transfers between devices: 10.2 us -> 7.84 us  [below(): return lax.ppermute(array, 'section', pairs)]
    ppermute x12 -> x6, starting transfers between devices: 17.7 us -> 16.5 us  [below(): return lax.ppermute(array, 'section', pairs)]
  transfers between devices with their start and end apart: 57 -> 42, of which waited for: 24 -> 17; matrix products, arithmetic and copies ran while one was open for 0% -> 0% of each run, Pallas kernels for 28% -> 31%
where the time goes in v4:
time: 162 us
  Pallas kernels  63.1 us (39%)
  waiting for transfers between devices  52.5 us (32%)
  starting transfers between devices  45.1 us (28%)
    pallas_call x44, Pallas kernels, run(): pl.pallas_call(body, out_shape=[jax.ShapeDtypeStruct(*out) for out in out...  49.4 us
    ppermute x36, waiting for transfers between devices, across(): return lax.ppermute(array, axis, [(i, i ^ flip) for i in range(count)])  44.7 us
    ppermute x36, starting transfers between devices, across(): return lax.ppermute(array, axis, [(i, i ^ flip) for i in range(count)])  28.6 us
    ppermute x6, starting transfers between devices, below(): return lax.ppermute(array, 'section', pairs)  16.5 us
    pallas_call x2, Pallas kernels, weight_grad(): pl.pallas_call(body, out_shape=[jax.ShapeDtypeStruct(shape, BF16), jax.Sh...  9.87 us
    ppermute x6, waiting for transfers between devices, below(): return lax.ppermute(array, 'section', pairs)  7.84 us
    pallas_call x1, Pallas kernels, held(): pl.pallas_call(hold_kernel, out_shape=jax.ShapeDtypeStruct(array.shape, a...  3.86 us
  transfers between devices with their start and end apart: 42, of which 17 were waited for; matrix products, arithmetic and copies ran while one was open for 0% of the time, Pallas kernels for 31%

profile of v4, /device:TPU:0, one launch (start us, length us, event | category | flops | bytes accessed | tf_op | source)
XLA Modules:
  0.0 162.0 jit_solution(16622375849749370902)
XLA Ops:
  0.6 3.1 %collective-permute-start.1 = (bf16[2,16,3072]{2,1,0:T(8,128)(2,1)}, bf16[2,16,3072]{2,1,0:T(8,128)(2,1)S(1)}, u32[]{:S(2)}, u32[]{:S(2)}) collective-permute-start(bf16[2,16,3072]{2,1,0:T(8,128)(2,1)} %refs_0_.3), channel_id=1, source_target_pairs={{0,2},{1,3},{2,0},{3,1},{4,6},{5,7},{6,4},{7,5},{8,10},{9,11},{10,... | collective-permute-start | bytes 589832 | tf_op jit(solution)/shard_map/ppermute | solution.py:47
  3.7 5.1 %collective-permute-done.1.refs_2_ = bf16[2,16,3072]{2,1,0:T(8,128)(2,1)S(1)} collective-permute-done((bf16[2,16,3072]{2,1,0:T(8,128)(2,1)}, bf16[2,16,3072]{2,1,0:T(8,128)(2,1)S(1)}, u32[]{:S(2)}, u32[]{:S(2)}) %collective-permute-start.1) | collective-permute-done | bytes 196640 | tf_op jit(solution)/shard_map/ppermute | solution.py:47
  8.8 3.9 %held.1.refs_4_.refs_2_.refs_3_ = bf16[1536,3072]{1,0:T(8,128)(2,1)S(1)} custom-call(bf16[1536,3072]{1,0:T(8,128)(2,1)} %bitcast.31), custom_call_target="tpu_custom_call" | custom-call | flops 4718592 | bytes 9437184 | tf_op jit(solution)/shard_map/held/pallas_call | solution.py:344
  13.5 2.7 %shard_map.95 = (bf16[768,128]{1,0:T(8,128)(2,1)S(1)}, bf16[64,1536]{1,0:T(8,128)(2,1)S(1)}, bf16[64,1536]{1,0:T(8,128)(2,1)S(1)}) custom-call(bf16[2,16,3072]{2,1,0:T(8,128)(2,1)S(1)} %copy-done, bf16[2,16,3072]{2,1,0:T(8,128)(2,1)S(1)} %collective-permute-done.refs_1_, bf16[2,16,3072]{2,1,0:T(8,128)(2,1)S(1)} %collective-permute-done.1.refs_2_, ...), custom_call_target="tpu_custom_call" | custom-call | flops 603979776 | bytes 9437184 | tf_op jit(solution)/shard_map/pallas_call | solution.py:35
  17.9 2.7 %shard_map.96 = (bf16[768,128]{1,0:T(8,128)(2,1)S(1)}, bf16[64,1536]{1,0:T(8,128)(2,1)S(1)}, bf16[64,1536]{1,0:T(8,128)(2,1)S(1)}) custom-call(bf16[2,16,3072]{2,1,0:T(8,128)(2,1)S(1)} %copy-done, bf16[2,16,3072]{2,1,0:T(8,128)(2,1)S(1)} %collective-permute-done.refs_1_, bf16[2,16,3072]{2,1,0:T(8,128)(2,1)S(1)} %collective-permute-done.1.refs_2_, ...), custom_call_target="tpu_custom_call" | custom-call | flops 603979776 | bytes 9437184 | tf_op jit(solution)/shard_map/pallas_call | solution.py:35
  20.6 2.9 %collective-permute-done.3.refs_1_ = bf16[768,128]{1,0:T(8,128)(2,1)S(1)} collective-permute-done((bf16[768,128]{1,0:T(8,128)(2,1)S(1)}, bf16[768,128]{1,0:T(8,128)(2,1)S(1)}, u32[]{:S(2)}, u32[]{:S(2)}) %collective-permute-start.3) | collective-permute-done | bytes 196640 | tf_op jit(solution)/shard_map/ppermute | solution.py:47
  28.6 4.0 %collective-permute-done.6.refs_1_ = bf16[768,128]{1,0:T(8,128)(2,1)S(1)} collective-permute-done((bf16[768,128]{1,0:T(8,128)(2,1)S(1)}, bf16[768,128]{1,0:T(8,128)(2,1)S(1)}, u32[]{:S(2)}, u32[]{:S(2)}) %collective-permute-start.6) | collective-permute-done | bytes 196640 | tf_op jit(solution)/shard_map/ppermute | solution.py:47
  39.7 2.4 %collective-permute-done.8.refs_4_.refs_2_ = bf16[2,16,3072]{2,1,0:T(8,128)(2,1)S(1)} collective-permute-done((bf16[2,16,3072]{2,1,0:T(8,128)(2,1)S(1)}, bf16[2,16,3072]{2,1,0:T(8,128)(2,1)S(1)}, u32[]{:S(2)}, u32[]{:S(2)}) %collective-permute-start.8) | collective-permute-done | bytes 196640 | tf_op jit(solution)/shard_map/ppermute | solution.py:47
  42.1 4.2 %collective-permute-done.5.refs_1_ = bf16[64,1536]{1,0:T(8,128)(2,1)S(1)} collective-permute-done((bf16[64,1536]{1,0:T(8,128)(2,1)S(1)}, bf16[64,1536]{1,0:T(8,128)(2,1)S(1)}, u32[]{:S(2)}, u32[]{:S(2)}) %collective-permute-start.5) | collective-permute-done | bytes 196640 | tf_op jit(solution)/shard_map/ppermute | solution.py:47
  53.8 2.8 %collective-permute-done.13.refs_0_ = bf16[64,1536]{1,0:T(8,128)(2,1)S(1)} collective-permute-done((bf16[64,1536]{1,0:T(8,128)(2,1)S(1)}, bf16[64,1536]{1,0:T(8,128)(2,1)S(1)}, u32[]{:S(2)}, u32[]{:S(2)}) %collective-permute-start.13) | collective-permute-done | bytes 196640 | tf_op jit(solution)/shard_map/ppermute | solution.py:56
  62.8 2.6 %collective-permute-done.12.refs_1_ = bf16[768,128]{1,0:T(8,128)(2,1)S(1)} collective-permute-done((bf16[768,128]{1,0:T(8,128)(2,1)S(1)}, bf16[768,128]{1,0:T(8,128)(2,1)S(1)}, u32[]{:S(2)}, u32[]{:S(2)}) %collective-permute-start.12) | collective-permute-done | bytes 196640 | tf_op jit(solution)/shard_map/ppermute | solution.py:47
  70.4 4.1 %collective-permute-done.17.refs_1_ = bf16[768,128]{1,0:T(8,128)(2,1)S(1)} collective-permute-done((bf16[768,128]{1,0:T(8,128)(2,1)S(1)}, bf16[768,128]{1,0:T(8,128)(2,1)S(1)}, u32[]{:S(2)}, u32[]{:S(2)}) %collective-permute-start.17) | collective-permute-done | bytes 196640 | tf_op jit(solution)/shard_map/ppermute | solution.py:47
  80.3 4.2 %collective-permute-done.16.refs_1_ = bf16[64,1536]{1,0:T(8,128)(2,1)S(1)} collective-permute-done((bf16[64,1536]{1,0:T(8,128)(2,1)S(1)}, bf16[64,1536]{1,0:T(8,128)(2,1)S(1)}, u32[]{:S(2)}, u32[]{:S(2)}) %collective-permute-start.16) | collective-permute-done | bytes 196640 | tf_op jit(solution)/shard_map/ppermute | solution.py:47
  85.2 2.9 %collective-permute-done.23.refs_1_ = bf16[64,1536]{1,0:T(8,128)(2,1)S(1)} collective-permute-done((bf16[64,1536]{1,0:T(8,128)(2,1)S(1)}, bf16[64,1536]{1,0:T(8,128)(2,1)S(1)}, u32[]{:S(2)}, u32[]{:S(2)}) %collective-permute-start.23) | collective-permute-done | bytes 196640 | tf_op jit(solution)/shard_map/ppermute | solution.py:47
  97.1 2.3 %collective-permute-done.24.refs_1_ = bf16[768,128]{1,0:T(8,128)(2,1)S(1)} collective-permute-done((bf16[768,128]{1,0:T(8,128)(2,1)S(1)}, bf16[768,128]{1,0:T(8,128)(2,1)S(1)}, u32[]{:S(2)}, u32[]{:S(2)}) %collective-permute-start.24) | collective-permute-done | bytes 196640 | tf_op jit(solution)/shard_map/ppermute | solution.py:47
  104.3 4.1 %collective-permute-done.29.refs_1_ = bf16[768,128]{1,0:T(8,128)(2,1)S(1)} collective-permute-done((bf16[768,128]{1,0:T(8,128)(2,1)S(1)}, bf16[768,128]{1,0:T(8,128)(2,1)S(1)}, u32[]{:S(2)}, u32[]{:S(2)}) %collective-permute-start.29) | collective-permute-done | bytes 196640 | tf_op jit(solution)/shard_map/ppermute | solution.py:47
  113.8 4.2 %collective-permute-done.28.refs_1_ = bf16[64,1536]{1,0:T(8,128)(2,1)S(1)} collective-permute-done((bf16[64,1536]{1,0:T(8,128)(2,1)S(1)}, bf16[64,1536]{1,0:T(8,128)(2,1)S(1)}, u32[]{:S(2)}, u32[]{:S(2)}) %collective-permute-start.28) | collective-permute-done | bytes 196640 | tf_op jit(solution)/shard_map/ppermute | solution.py:47
  118.0 7.8 %collective-permute-start.31 = (bf16[64,1536]{1,0:T(8,128)(2,1)S(1)}, bf16[64,1536]{1,0:T(8,128)(2,1)S(1)}, u32[]{:S(2)}, u32[]{:S(2)}) collective-permute-start(bf16[64,1536]{1,0:T(8,128)(2,1)S(1)} %shard_map.127.refs_3_), channel_id=1, source_target_pairs={{0,4},{4,0},{8,12},{12,8},{1,5},{5,1},{9,13},{13,9},{2,6},{6,2},{1... | collective-permute-start | bytes 589832 | tf_op jit(solution)/shard_map/ppermute | solution.py:56
  125.8 3.6 %collective-permute-start.35 = (bf16[64,1536]{1,0:T(8,128)(2,1)S(1)}, bf16[64,1536]{1,0:T(8,128)(2,1)S(1)}, u32[]{:S(2)}, u32[]{:S(2)}) collective-permute-start(bf16[64,1536]{1,0:T(8,128)(2,1)S(1)} %shard_map.128.refs_3_), channel_id=1, source_target_pairs={{0,4},{4,0},{8,12},{12,8},{1,5},{5,1},{9,13},{13,9},{2,6},{6,2},{1... | collective-permute-start | bytes 589832 | tf_op jit(solution)/shard_map/ppermute | solution.py:56
  129.9 4.2 %collective-permute-done.35.refs_0_ = bf16[64,1536]{1,0:T(8,128)(2,1)S(1)} collective-permute-done((bf16[64,1536]{1,0:T(8,128)(2,1)S(1)}, bf16[64,1536]{1,0:T(8,128)(2,1)S(1)}, u32[]{:S(2)}, u32[]{:S(2)}) %collective-permute-start.35) | collective-permute-done | bytes 196640 | tf_op jit(solution)/shard_map/ppermute | solution.py:56
  142.3 4.4 %shard_map.133 = (bf16[1536,3072]{1,0:T(8,128)(2,1)}, f32[8,128]{1,0:T(8,128)S(1)}) custom-call(bf16[128,1536]{1,0:T(8,128)(2,1)S(1)} %bitcast.27, bf16[64,1536]{1,0:T(8,128)(2,1)S(1)} %get-tuple-element.121.refs_1_.refs_2_, bf16[64,1536]{1,0:T(8,128)(2,1)S(1)} %get-tuple-element.122.refs_2_.refs_3_, ...), custom_call_target="tpu_custom_call" | custom-call | flops 1207959552 | bytes 9437184 | tf_op jit(solution)/shard_map/pallas_call | solution.py:411
  146.7 2.8 %shard_map.134 = (f32[32,3072]{1,0:T(8,128)S(1)}, bf16[32,3072]{1,0:T(8,128)(2,1)S(1)}, bf16[1536,64]{1,0:T(8,128)(2,1)S(1)}) custom-call(bf16[768,128]{1,0:T(8,128)(2,1)S(1)} %get-tuple-element.120.refs_3_.refs_0_, bf16[768,128]{1,0:T(8,128)(2,1)S(1)} %collective-permute-done.34.refs_1_, bf16[12,128,64]{2,1,0:T(8,128)(2,1)S(1)} %get-tuple-element.72.refs_5_.refs_2_, ...), custom_call_target="tpu_custom_call" | custom-call | flops 603979776 | bytes 9437184 | tf_op jit(solution)/shard_map/pallas_call | solution.py:35
  149.7 2.8 %shard_map.136 = (f32[32,3072]{1,0:T(8,128)S(1)}, bf16[32,3072]{1,0:T(8,128)(2,1)S(1)}, bf16[1536,64]{1,0:T(8,128)(2,1)S(1)}) custom-call(bf16[768,128]{1,0:T(8,128)(2,1)S(1)} %get-tuple-element.127.refs_5_.refs_0_, bf16[768,128]{1,0:T(8,128)(2,1)S(1)} %collective-permute-done.39.refs_1_, bf16[12,128,64]{2,1,0:T(8,128)(2,1)S(1)} %get-tuple-element.80.refs_2_, ...), custom_call_target="tpu_custom_call" | custom-call | flops 603979776 | bytes 9437184 | tf_op jit(solution)/shard_map/pallas_call | solution.py:35
  155.7 5.5 %shard_map.139 = (bf16[3072,1536]{1,0:T(8,128)(2,1)}, f32[8,128]{1,0:T(8,128)}) custom-call(bf16[2,16,3072]{2,1,0:T(8,128)(2,1)S(1)} %bitcast.30, bf16[2,16,3072]{2,1,0:T(8,128)(2,1)S(1)} %collective-permute-done.19.refs_4_.refs_1_, bf16[2,16,3072]{2,1,0:T(8,128)(2,1)S(1)} %collective-permute-done.8.refs_4_.refs_2_, ...), custom_call_target="tpu_custom_call" | custom-call | flops 1207959552 | bytes 9437184 | tf_op jit(solution)/shard_map/pallas_call | solution.py:411
  (124 shorter events, 71.7 us)
Async XLA Ops:
  0.6 8.2 %collective-permute-start.1 = (bf16[2,16,3072]{2,1,0:T(8,128)(2,1)}, bf16[2,16,3072]{2,1,0:T(8,128)(2,1)S(1)}, u32[]{:S(2)}, u32[]{:S(2)}) collective-permute-start(bf16[2,16,3072]{2,1,0:T(8,128)(2,1)} %refs_0_.3), channel_id=1, source_target_pairs={{0,2},{1,3},{2,0},{3,1},{4,6},{5,7},{6,4},{7,5},{8,10},{9,11},{10,... | collective-permute-start | bytes 589832 | tf_op jit(solution)/shard_map/ppermute | solution.py:47
  3.7 9.7 %collective-permute-start = (bf16[2,16,3072]{2,1,0:T(8,128)(2,1)}, bf16[2,16,3072]{2,1,0:T(8,128)(2,1)S(1)}, u32[]{:S(2)}, u32[]{:S(2)}) collective-permute-start(bf16[2,16,3072]{2,1,0:T(8,128)(2,1)} %refs_0_.3), channel_id=1, source_target_pairs={{0,1},{1,0},{2,3},{3,2},{4,5},{5,4},{6,7},{7,6},{8,9},{9,8},{10,11... | collective-permute-start | bytes 589832 | tf_op jit(solution)/shard_map/ppermute | solution.py:47
  16.1 7.4 %collective-permute-start.3 = (bf16[768,128]{1,0:T(8,128)(2,1)S(1)}, bf16[768,128]{1,0:T(8,128)(2,1)S(1)}, u32[]{:S(2)}, u32[]{:S(2)}) collective-permute-start(bf16[768,128]{1,0:T(8,128)(2,1)S(1)} %get-tuple-element.73.refs_5_.refs_0_), channel_id=1, source_target_pairs={{0,16},{16,0},{1,17},{17,1},{2,18},{18,2},{3,19},{19,3},{4,20},{20... | collective-permute-start | bytes 589832 | tf_op jit(solution)/shard_map/ppermute | solution.py:47
  25.3 7.3 %collective-permute-start.6 = (bf16[768,128]{1,0:T(8,128)(2,1)S(1)}, bf16[768,128]{1,0:T(8,128)(2,1)S(1)}, u32[]{:S(2)}, u32[]{:S(2)}) collective-permute-start(bf16[768,128]{1,0:T(8,128)(2,1)S(1)} %get-tuple-element.74.refs_4_.refs_0_), channel_id=1, source_target_pairs={{0,16},{16,0},{1,17},{17,1},{2,18},{18,2},{3,19},{19,3},{4,20},{20... | collective-permute-start | bytes 589832 | tf_op jit(solution)/shard_map/ppermute | solution.py:47
  34.3 7.8 %collective-permute-start.8 = (bf16[2,16,3072]{2,1,0:T(8,128)(2,1)S(1)}, bf16[2,16,3072]{2,1,0:T(8,128)(2,1)S(1)}, u32[]{:S(2)}, u32[]{:S(2)}) collective-permute-start(bf16[2,16,3072]{2,1,0:T(8,128)(2,1)S(1)} %bitcast.28), channel_id=1, source_target_pairs={{0,2},{1,3},{2,0},{3,1},{4,6},{5,7},{6,4},{7,5},{8,10},{9,11},{10,... | collective-permute-start | bytes 589832 | tf_op jit(solution)/shard_map/ppermute | solution.py:47
  36.1 10.2 %collective-permute-start.5 = (bf16[64,1536]{1,0:T(8,128)(2,1)S(1)}, bf16[64,1536]{1,0:T(8,128)(2,1)S(1)}, u32[]{:S(2)}, u32[]{:S(2)}) collective-permute-start(bf16[64,1536]{1,0:T(8,128)(2,1)S(1)} %get-tuple-element.78), channel_id=1, source_target_pairs={{0,2},{1,3},{2,0},{3,1},{4,6},{5,7},{6,4},{7,5},{8,10},{9,11},{10,... | collective-permute-start | bytes 589832 | tf_op jit(solution)/shard_map/ppermute | solution.py:47
  37.9 12.1 %collective-permute-start.11 = (bf16[64,1536]{1,0:T(8,128)(2,1)S(1)}, bf16[64,1536]{1,0:T(8,128)(2,1)S(1)}, u32[]{:S(2)}, u32[]{:S(2)}) collective-permute-start(bf16[64,1536]{1,0:T(8,128)(2,1)S(1)} %get-tuple-element.85), channel_id=1, source_target_pairs={{0,2},{1,3},{2,0},{3,1},{4,6},{5,7},{6,4},{7,5},{8,10},{9,11},{10,... | collective-permute-start | bytes 589832 | tf_op jit(solution)/shard_map/ppermute | solution.py:47
  46.4 6.0 %collective-permute-start.9 = (bf16[64,1536]{1,0:T(8,128)(2,1)S(1)}, bf16[64,1536]{1,0:T(8,128)(2,1)S(1)}, u32[]{:S(2)}, u32[]{:S(2)}) collective-permute-start(bf16[64,1536]{1,0:T(8,128)(2,1)S(1)} %shard_map.103.refs_3_), channel_id=1, source_target_pairs={{0,4},{4,0},{8,12},{12,8},{1,5},{5,1},{9,13},{13,9},{2,6},{6,2},{1... | collective-permute-start | bytes 589832 | tf_op jit(solution)/shard_map/ppermute | solution.py:56
  50.1 6.5 %collective-permute-start.13 = (bf16[64,1536]{1,0:T(8,128)(2,1)S(1)}, bf16[64,1536]{1,0:T(8,128)(2,1)S(1)}, u32[]{:S(2)}, u32[]{:S(2)}) collective-permute-start(bf16[64,1536]{1,0:T(8,128)(2,1)S(1)} %shard_map.104.refs_3_), channel_id=1, source_target_pairs={{0,4},{4,0},{8,12},{12,8},{1,5},{5,1},{9,13},{13,9},{2,6},{6,2},{1... | collective-permute-start | bytes 589832 | tf_op jit(solution)/shard_map/ppermute | solution.py:56
  58.0 7.4 %collective-permute-start.12 = (bf16[768,128]{1,0:T(8,128)(2,1)S(1)}, bf16[768,128]{1,0:T(8,128)(2,1)S(1)}, u32[]{:S(2)}, u32[]{:S(2)}) collective-permute-start(bf16[768,128]{1,0:T(8,128)(2,1)S(1)} %get-tuple-element.88.refs_3_.refs_0_), channel_id=1, source_target_pairs={{0,16},{16,0},{1,17},{17,1},{2,18},{18,2},{3,19},{19,3},{4,20},{20... | collective-permute-start | bytes 589832 | tf_op jit(solution)/shard_map/ppermute | solution.py:47
  67.1 7.3 %collective-permute-start.17 = (bf16[768,128]{1,0:T(8,128)(2,1)S(1)}, bf16[768,128]{1,0:T(8,128)(2,1)S(1)}, u32[]{:S(2)}, u32[]{:S(2)}) collective-permute-start(bf16[768,128]{1,0:T(8,128)(2,1)S(1)} %get-tuple-element.91.refs_4_.refs_0_), channel_id=1, source_target_pairs={{0,16},{16,0},{1,17},{17,1},{2,18},{18,2},{3,19},{19,3},{4,20},{20... | collective-permute-start | bytes 589832 | tf_op jit(solution)/shard_map/ppermute | solution.py:47
  76.7 7.8 %collective-permute-start.16 = (bf16[64,1536]{1,0:T(8,128)(2,1)S(1)}, bf16[64,1536]{1,0:T(8,128)(2,1)S(1)}, u32[]{:S(2)}, u32[]{:S(2)}) collective-permute-start(bf16[64,1536]{1,0:T(8,128)(2,1)S(1)} %get-tuple-element.95), channel_id=1, source_target_pairs={{0,2},{1,3},{2,0},{3,1},{4,6},{5,7},{6,4},{7,5},{8,10},{9,11},{10,... | collective-permute-start | bytes 589832 | tf_op jit(solution)/shard_map/ppermute | solution.py:47
  79.9 8.2 %collective-permute-start.23 = (bf16[64,1536]{1,0:T(8,128)(2,1)S(1)}, bf16[64,1536]{1,0:T(8,128)(2,1)S(1)}, u32[]{:S(2)}, u32[]{:S(2)}) collective-permute-start(bf16[64,1536]{1,0:T(8,128)(2,1)S(1)} %get-tuple-element.101), channel_id=1, source_target_pairs={{0,2},{1,3},{2,0},{3,1},{4,6},{5,7},{6,4},{7,5},{8,10},{9,11},{10,... | collective-permute-start | bytes 589832 | tf_op jit(solution)/shard_map/ppermute | solution.py:47
  92.5 6.9 %collective-permute-start.24 = (bf16[768,128]{1,0:T(8,128)(2,1)S(1)}, bf16[768,128]{1,0:T(8,128)(2,1)S(1)}, u32[]{:S(2)}, u32[]{:S(2)}) collective-permute-start(bf16[768,128]{1,0:T(8,128)(2,1)S(1)} %get-tuple-element.104.refs_3_.refs_0_), channel_id=1, source_target_pairs={{0,16},{16,0},{1,17},{17,1},{2,18},{18,2},{3,19},{19,3},{4,20},{20... | collective-permute-start | bytes 589832 | tf_op jit(solution)/shard_map/ppermute | solution.py:47
  101.1 7.3 %collective-permute-start.29 = (bf16[768,128]{1,0:T(8,128)(2,1)S(1)}, bf16[768,128]{1,0:T(8,128)(2,1)S(1)}, u32[]{:S(2)}, u32[]{:S(2)}) collective-permute-start(bf16[768,128]{1,0:T(8,128)(2,1)S(1)} %get-tuple-element.107.refs_4_.refs_0_), channel_id=1, source_target_pairs={{0,16},{16,0},{1,17},{17,1},{2,18},{18,2},{3,19},{19,3},{4,20},{20... | collective-permute-start | bytes 589832 | tf_op jit(solution)/shard_map/ppermute | solution.py:47
  110.1 7.8 %collective-permute-start.28 = (bf16[64,1536]{1,0:T(8,128)(2,1)S(1)}, bf16[64,1536]{1,0:T(8,128)(2,1)S(1)}, u32[]{:S(2)}, u32[]{:S(2)}) collective-permute-start(bf16[64,1536]{1,0:T(8,128)(2,1)S(1)} %get-tuple-element.111), channel_id=1, source_target_pairs={{0,2},{1,3},{2,0},{3,1},{4,6},{5,7},{6,4},{7,5},{8,10},{9,11},{10,... | collective-permute-start | bytes 589832 | tf_op jit(solution)/shard_map/ppermute | solution.py:47
  113.4 12.4 %collective-permute-start.33 = (bf16[64,1536]{1,0:T(8,128)(2,1)S(1)}, bf16[64,1536]{1,0:T(8,128)(2,1)S(1)}, u32[]{:S(2)}, u32[]{:S(2)}) collective-permute-start(bf16[64,1536]{1,0:T(8,128)(2,1)S(1)} %get-tuple-element.117), channel_id=1, source_target_pairs={{0,2},{1,3},{2,0},{3,1},{4,6},{5,7},{6,4},{7,5},{8,10},{9,11},{10,... | collective-permute-start | bytes 589832 | tf_op jit(solution)/shard_map/ppermute | solution.py:47
  118.0 11.9 %collective-permute-start.31 = (bf16[64,1536]{1,0:T(8,128)(2,1)S(1)}, bf16[64,1536]{1,0:T(8,128)(2,1)S(1)}, u32[]{:S(2)}, u32[]{:S(2)}) collective-permute-start(bf16[64,1536]{1,0:T(8,128)(2,1)S(1)} %shard_map.127.refs_3_), channel_id=1, source_target_pairs={{0,4},{4,0},{8,12},{12,8},{1,5},{5,1},{9,13},{13,9},{2,6},{6,2},{1... | collective-permute-start | bytes 589832 | tf_op jit(solution)/shard_map/ppermute | solution.py:56
  125.8 8.2 %collective-permute-start.35 = (bf16[64,1536]{1,0:T(8,128)(2,1)S(1)}, bf16[64,1536]{1,0:T(8,128)(2,1)S(1)}, u32[]{:S(2)}, u32[]{:S(2)}) collective-permute-start(bf16[64,1536]{1,0:T(8,128)(2,1)S(1)} %shard_map.128.refs_3_), channel_id=1, source_target_pairs={{0,4},{4,0},{8,12},{12,8},{1,5},{5,1},{9,13},{13,9},{2,6},{6,2},{1... | collective-permute-start | bytes 589832 | tf_op jit(solution)/shard_map/ppermute | solution.py:56
  134.1 5.9 %collective-permute-start.36 = (bf16[64,1536]{1,0:T(8,128)(2,1)S(1)}, bf16[64,1536]{1,0:T(8,128)(2,1)S(1)}, u32[]{:S(2)}, u32[]{:S(2)}) collective-permute-start(bf16[64,1536]{1,0:T(8,128)(2,1)S(1)} %collective-permute-done.35.refs_0_), channel_id=1, source_target_pairs={{0,1},{1,0},{2,3},{3,2},{4,5},{5,4},{6,7},{7,6},{8,9},{9,8},{10,11... | collective-permute-start | bytes 589832 | tf_op jit(solution)/shard_map/ppermute | solution.py:47
  137.0 9.7 %collective-permute-start.34 = (bf16[768,128]{1,0:T(8,128)(2,1)S(1)}, bf16[768,128]{1,0:T(8,128)(2,1)S(1)}, u32[]{:S(2)}, u32[]{:S(2)}) collective-permute-start(bf16[768,128]{1,0:T(8,128)(2,1)S(1)} %get-tuple-element.120.refs_3_.refs_0_), channel_id=1, source_target_pairs={{0,16},{16,0},{1,17},{17,1},{2,18},{18,2},{3,19},{19,3},{4,20},{20... | collective-permute-start | bytes 589832 | tf_op jit(solution)/shard_map/ppermute | solution.py:47
  141.7 8.0 %collective-permute-start.39 = (bf16[768,128]{1,0:T(8,128)(2,1)S(1)}, bf16[768,128]{1,0:T(8,128)(2,1)S(1)}, u32[]{:S(2)}, u32[]{:S(2)}) collective-permute-start(bf16[768,128]{1,0:T(8,128)(2,1)S(1)} %get-tuple-element.127.refs_5_.refs_0_), channel_id=1, source_target_pairs={{0,16},{16,0},{1,17},{17,1},{2,18},{18,2},{3,19},{19,3},{4,20},{20... | collective-permute-start | bytes 589832 | tf_op jit(solution)/shard_map/ppermute | solution.py:47
  153.1 8.1 %collective-permute-start.38 = (bf16[16,3072]{1,0:T(8,128)(2,1)S(1)}, bf16[16,3072]{1,0:T(8,128)(2,1)S(1)}, u32[]{:S(2)}, u32[]{:S(2)}) collective-permute-start(bf16[16,3072]{1,0:T(8,128)(2,1)S(1)} %get-tuple-element.132), channel_id=1, source_target_pairs={{0,2},{1,3},{2,0},{3,1},{4,6},{5,7},{6,4},{7,5},{8,10},{9,11},{10,... | collective-permute-start | bytes 294920 | tf_op jit(solution)/shard_map/ppermute | solution.py:47
  154.7 6.5 %collective-permute-start.41 = (bf16[16,3072]{1,0:T(8,128)(2,1)S(1)}, bf16[16,3072]{1,0:T(8,128)(2,1)S(1)}, u32[]{:S(2)}, u32[]{:S(2)}) collective-permute-start(bf16[16,3072]{1,0:T(8,128)(2,1)S(1)} %get-tuple-element.136), channel_id=1, source_target_pairs={{0,2},{1,3},{2,0},{3,1},{4,6},{5,7},{6,4},{7,5},{8,10},{9,11},{10,... | collective-permute-start | bytes 294920 | tf_op jit(solution)/shard_map/ppermute | solution.py:47
  (26 other events, 119.5 us)
